TPU v7x, 32 devices: a whole 2x2x4 slice. The times are simulated.
32 devices in a mesh: dp: 8 (over z, y), tensor: 4 (over x, core).
Axes of the slice: x: 2, y: 2, z: 4, core: 2. Of those that a mesh axis runs over, the one named last changes fastest.
Arguments:
- tokens: bfloat16 [1024, 16, 768], P(('dp', 'tensor')), may hold values from -6 to 6
- lengths: int32 [16], replicated, may hold values from 1 to 1024, 12288 in all
- dealing: int32 [16], replicated, may hold values from 0 to 15, each once
- project_weight: bfloat16 [768, 2304], P('dp', 'tensor'), may hold values from -0.21875 to 0.21875
- query_projection_bias: float32 [768], replicated, may hold values from -3 to 3
- value_projection_bias: float32 [768], replicated, may hold values from -3 to 3
- attention_output_weight: bfloat16 [768, 768], P('dp', 'tensor'), may hold values from -3.5 to 3.5
- attention_output_bias: float32 [768], replicated, may hold values from -3 to 3
- first_gain: float32 [768], replicated, may hold values from 0.5 to 1.5
- first_shift: float32 [768], replicated, may hold values from -3 to 3
- feed_input_weight: bfloat16 [768, 3072], P('dp', 'tensor'), may hold values from -0.21875 to 0.21875
- feed_input_bias: float32 [3072], replicated, may hold values from -3 to 3
- feed_output_weight: bfloat16 [768, 3072], P('dp', 'tensor'), may hold values from -0.109375 to 0.109375
- feed_output_bias: float32 [768], replicated, may hold values from -3 to 3
- second_gain: float32 [768], replicated, may hold values from 0.5 to 1.5
- second_shift: float32 [768], replicated, may hold values from -3 to 3
- output_grad: bfloat16 [1024, 16, 768], P(('dp', 'tensor')), may hold values from -6 to 6
Outputs:
- layer_output: bfloat16 [1024, 16, 768], P('tensor', 'dp')
- tokens_grad: bfloat16 [1024, 16, 768], P(('dp', 'tensor'))
- project_grad: float32 [768, 2304], P('dp', 'tensor')
- query_bias_grad: float32 [768], P(('dp', 'tensor'))
- value_bias_grad: float32 [768], P(('dp', 'tensor'))
- output_weight_grad: float32 [768, 768], P('dp', 'tensor')
- output_bias_grad: float32 [768], P(('dp', 'tensor'))
- first_gain_grad: float32 [768], P(('dp', 'tensor'))
- first_shift_grad: float32 [768], P(('dp', 'tensor'))
- up_weight_grad: float32 [768, 3072], P('dp', 'tensor')
- up_bias_grad: float32 [3072], P(('dp', 'tensor'))
- down_weight_grad: float32 [768, 3072], P('dp', 'tensor')
- down_bias_grad: float32 [768], P(('dp', 'tensor'))
- second_gain_grad: float32 [768], P(('dp', 'tensor'))
- second_shift_grad: float32 [768], P(('dp', 'tensor'))
Inputs may be any that keep to these rules, and one draw needn't show every extreme that they name: `lengths`: the longest sequence has exactly 1024 tokens. A permutation: sequence s is processed in slot dealing[s], and slot q belongs to data index q // 2.
All inputs are finite; a program needn't handle non-finite values.
Results may differ from a plain program's by a relative error of at most 0.022.
Values may be sent and summed in bfloat16 or wider, within the bound.
A program may use at most 128 MiB of HBM per device.

v0:
```python
from functools import partial

import jax
import jax.numpy as jnp
from jax import lax
from jax.sharding import PartitionSpec as P

HD = 64


EPSILON = 1e-12
MASKED = -1e30


def norm_forward(value, gain, shift):
    centred = value - jnp.mean(value, axis=-1, keepdims=True)
    inverse = lax.rsqrt(jnp.mean(centred * centred, axis=-1, keepdims=True) + EPSILON)
    normed = centred * inverse
    return (normed * gain + shift, normed, inverse)


def norm_backward(upstream, normed, inverse, gain):
    scaled = upstream * gain
    first_mean = jnp.mean(scaled, axis=-1, keepdims=True)
    second_mean = jnp.mean(scaled * normed, axis=-1, keepdims=True)
    return inverse * (scaled - first_mean - normed * second_mean)


def spread_block(values, block_index, length_total):
    blank = jnp.zeros((length_total,), jnp.float32)
    return lax.dynamic_update_slice_in_dim(blank, values, block_index * values.shape[0], 0)


def reduce_weights(grads):
    return (
        lax.psum_scatter(grads[0], "dp", scatter_dimension=0, tiled=True),
        lax.psum_scatter(grads[1], "dp", scatter_dimension=0, tiled=True),
        lax.psum_scatter(grads[2], "dp", scatter_dimension=0, tiled=True),
        lax.psum_scatter(grads[3], "dp", scatter_dimension=0, tiled=True),
    )


def on_device(
    tokens,
    lengths,
    dealing,
    project_weight,
    query_projection_bias,
    value_projection_bias,
    attention_output_weight,
    attention_output_bias,
    first_gain,
    first_shift,
    feed_input_weight,
    feed_input_bias,
    feed_output_weight,
    feed_output_bias,
    second_gain,
    second_shift,
    output_grad,
):
    n_data = lax.axis_size("dp")
    n_tensor = lax.axis_size("tensor")
    data_index = lax.axis_index("dp")
    tensor_index = lax.axis_index("tensor")
    seq_total = dealing.shape[0]
    seq_here = seq_total // n_data
    piece_rows = tokens.shape[0]
    local_rows = piece_rows * n_data
    seq_rows = local_rows * n_tensor
    width = tokens.shape[2]
    head_cols = attention_output_weight.shape[1]
    heads_here = head_cols // HD
    hidden_cols = feed_input_weight.shape[1]
    score_scale = HD ** (-0.5)
    slot_ids = jnp.arange(seq_total, dtype=jnp.int32)
    placing = (dealing[None, :] == slot_ids[:, None]).astype(jnp.bfloat16)
    send_tokens = jnp.einsum(
        "qs,psd->pqd", placing, tokens, preferred_element_type=jnp.float32
    ).astype(jnp.bfloat16)
    send_grad = jnp.einsum(
        "qs,psd->pqd", placing, output_grad, preferred_element_type=jnp.float32
    ).astype(jnp.bfloat16)
    tokens_here, cotangent_here = (
        lax.all_to_all(send_tokens, "dp", split_axis=1, concat_axis=0, tiled=True),
        lax.all_to_all(send_grad, "dp", split_axis=1, concat_axis=0, tiled=True),
    )
    my_slots = data_index * seq_here + jnp.arange(seq_here, dtype=jnp.int32)
    mine = dealing[None, :] == my_slots[:, None]
    seq_length = jnp.sum(jnp.where(mine, lengths[None, :], 0), axis=1)
    row_ids = jnp.arange(seq_rows, dtype=jnp.int32)
    owner_rows = row_ids // local_rows
    inner_rows = row_ids % local_rows
    position = (
        inner_rows // piece_rows * n_tensor + owner_rows
    ) * piece_rows + inner_rows % piece_rows
    key_valid = position[None, :] < seq_length[:, None]
    project_full, output_full, up_weight_gathered, down_weight_gathered = (
        lax.all_gather(project_weight, "dp", axis=0, tiled=True),
        lax.all_gather(attention_output_weight, "dp", axis=0, tiled=True),
        lax.all_gather(feed_input_weight, "dp", axis=0, tiled=True),
        lax.all_gather(feed_output_weight, "dp", axis=0, tiled=True),
    )
    tokens_full = lax.all_gather(tokens_here, "tensor", axis=0, tiled=True)
    query_part = lax.dynamic_slice_in_dim(
        query_projection_bias, tensor_index * head_cols, head_cols
    )
    value_part = lax.dynamic_slice_in_dim(
        value_projection_bias, tensor_index * head_cols, head_cols
    )
    project_bias = jnp.concatenate([query_part, jnp.zeros_like(query_part), value_part])
    projected = (
        jnp.einsum("lsd,de->sle", tokens_full, project_full, preferred_element_type=jnp.float32)
        + project_bias
    ).astype(jnp.bfloat16)

    def split_heads(qkv_block):
        query_matrix_rows = qkv_block[:, :head_cols].reshape(seq_rows, heads_here, HD)
        key_matrix_rows = qkv_block[:, head_cols : 2 * head_cols].reshape(seq_rows, heads_here, HD)
        value_matrix_rows = qkv_block[:, 2 * head_cols :].reshape(seq_rows, heads_here, HD)
        return (query_matrix_rows, key_matrix_rows, value_matrix_rows)

    def masked_scores(query_matrix_rows, key_matrix_rows, valid_keys):
        raw_scores = (
            jnp.einsum(
                "qhe,khe->hqk",
                query_matrix_rows,
                key_matrix_rows,
                preferred_element_type=jnp.float32,
            )
            * score_scale
        )
        return jnp.where(valid_keys[None, None, :], raw_scores, MASKED)

    def attend(item):
        qkv_block, valid_keys = item
        query_matrix_rows, key_matrix_rows, value_matrix_rows = split_heads(qkv_block)
        scores = masked_scores(query_matrix_rows, key_matrix_rows, valid_keys)
        row_max = jnp.max(scores, axis=-1, keepdims=True)
        exponent = jnp.exp(scores - row_max)
        row_total = jnp.sum(exponent, axis=-1, keepdims=True)
        weights = (exponent / row_total).astype(jnp.bfloat16)
        mixed_heads = jnp.einsum(
            "hqk,khe->qhe", weights, value_matrix_rows, preferred_element_type=jnp.float32
        )
        return (
            mixed_heads.reshape(seq_rows, head_cols).astype(jnp.bfloat16),
            (row_max + jnp.log(row_total))[..., 0],
        )

    mixed_output, log_total = lax.map(attend, (projected, key_valid))
    row_portion = mixed_output
    branch_output = lax.psum_scatter(
        jnp.einsum(
            "sle,de->lsd", row_portion, output_full, preferred_element_type=jnp.float32
        ).astype(jnp.bfloat16),
        "tensor",
        scatter_dimension=0,
        tiled=True,
    ).astype(jnp.float32)
    first_normed_rows, normed_first, inverse_first = norm_forward(
        tokens_here.astype(jnp.float32) + branch_output + attention_output_bias,
        first_gain,
        first_shift,
    )
    first_rows_gathered = lax.all_gather(
        first_normed_rows.astype(jnp.bfloat16), "tensor", axis=0, tiled=True
    )
    up_weight_portion = lax.dynamic_slice_in_dim(
        feed_input_bias, tensor_index * hidden_cols, hidden_cols
    )
    before_gelu = (
        jnp.einsum(
            "pna,ay->pny",
            first_rows_gathered,
            up_weight_gathered,
            preferred_element_type=jnp.float32,
        )
        + up_weight_portion
    )
    activated, gelu_back = jax.vjp(partial(jax.nn.gelu, approximate=False), before_gelu)
    hidden_rows = activated.astype(jnp.bfloat16)
    row_portion = lax.slice_in_dim(hidden_rows, 0, local_rows * lax.axis_size("tensor"), axis=0)
    feed_output = lax.psum_scatter(
        jnp.einsum(
            "ran,en->rae", row_portion, down_weight_gathered, preferred_element_type=jnp.float32
        ).astype(jnp.bfloat16),
        "tensor",
        scatter_dimension=0,
        tiled=True,
    ).astype(jnp.float32)
    second, normed_second, inverse_second = norm_forward(
        first_normed_rows + feed_output + feed_output_bias, second_gain, second_shift
    )
    cotangent = cotangent_here.astype(jnp.float32)
    second_gain_part = jnp.sum(cotangent * normed_second, axis=(0, 1))
    second_shift_part = jnp.sum(cotangent, axis=(0, 1))
    grad_second = norm_backward(cotangent, normed_second, inverse_second, second_gain)
    down_bias_part = jnp.sum(grad_second, axis=(0, 1))
    project_full, output_full, up_weight_gathered, down_weight_gathered = (
        lax.all_gather(project_weight, "dp", axis=0, tiled=True),
        lax.all_gather(attention_output_weight, "dp", axis=0, tiled=True),
        lax.all_gather(feed_input_weight, "dp", axis=0, tiled=True),
        lax.all_gather(feed_output_weight, "dp", axis=0, tiled=True),
    )
    feed_gradient_gathered = lax.all_gather(
        grad_second.astype(jnp.bfloat16), "tensor", axis=0, tiled=True
    )
    grad_hidden = jnp.einsum(
        "pna,ay->pny",
        feed_gradient_gathered,
        down_weight_gathered,
        preferred_element_type=jnp.float32,
    )
    down_grad = jnp.einsum(
        "hkw,hkg->wg", feed_gradient_gathered, hidden_rows, preferred_element_type=jnp.float32
    )
    gradient_before_gelu = gelu_back(grad_hidden)[0].astype(jnp.bfloat16)
    up_gradient = jnp.einsum(
        "hkw,hkg->wg", first_rows_gathered, gradient_before_gelu, preferred_element_type=jnp.float32
    )
    up_bias_part = jnp.sum(gradient_before_gelu, axis=(0, 1), dtype=jnp.float32)
    row_portion = gradient_before_gelu
    grad_first = grad_second + lax.psum_scatter(
        jnp.einsum(
            "ran,en->rae", row_portion, up_weight_gathered, preferred_element_type=jnp.float32
        ).astype(jnp.bfloat16),
        "tensor",
        scatter_dimension=0,
        tiled=True,
    ).astype(jnp.float32)
    first_gain_part = jnp.sum(grad_first * normed_first, axis=(0, 1))
    first_shift_part = jnp.sum(grad_first, axis=(0, 1))
    grad_residual = norm_backward(grad_first, normed_first, inverse_first, first_gain)
    output_bias_part = jnp.sum(grad_residual, axis=(0, 1))
    branch_grad_full = lax.all_gather(
        grad_residual.astype(jnp.bfloat16), "tensor", axis=0, tiled=True
    )
    grad_mixed = jnp.einsum(
        "lsd,de->sle", branch_grad_full, output_full, preferred_element_type=jnp.float32
    ).astype(jnp.bfloat16)
    output_grad_weight = jnp.einsum(
        "lsd,sle->de", branch_grad_full, mixed_output, preferred_element_type=jnp.float32
    )

    def attend_back(item):
        qkv_block, valid_keys, row_lse, grad_block = item
        query_matrix_rows, key_matrix_rows, value_matrix_rows = split_heads(qkv_block)
        weights = jnp.exp(
            masked_scores(query_matrix_rows, key_matrix_rows, valid_keys) - row_lse[..., None]
        )
        grad_heads = grad_block.reshape(seq_rows, heads_here, HD)
        grad_weights = jnp.einsum(
            "qhe,khe->hqk", grad_heads, value_matrix_rows, preferred_element_type=jnp.float32
        )
        inner_sum = jnp.sum(weights * grad_weights, axis=-1, keepdims=True)
        grad_scores = (weights * (grad_weights - inner_sum)).astype(jnp.bfloat16)
        grad_query = (
            jnp.einsum(
                "hqk,khe->qhe", grad_scores, key_matrix_rows, preferred_element_type=jnp.float32
            )
            * score_scale
        )
        grad_key = (
            jnp.einsum(
                "hqk,qhe->khe", grad_scores, query_matrix_rows, preferred_element_type=jnp.float32
            )
            * score_scale
        )
        grad_value = jnp.einsum(
            "hqk,qhe->khe",
            weights.astype(jnp.bfloat16),
            grad_heads,
            preferred_element_type=jnp.float32,
        )
        joined = jnp.concatenate(
            [
                grad_query.reshape(seq_rows, head_cols),
                grad_key.reshape(seq_rows, head_cols),
                grad_value.reshape(seq_rows, head_cols),
            ],
            axis=-1,
        )
        return joined.astype(jnp.bfloat16)

    grad_projected = lax.map(attend_back, (projected, key_valid, log_total, grad_mixed))
    project_grad = jnp.einsum(
        "lsd,sle->de", tokens_full, grad_projected, preferred_element_type=jnp.float32
    )
    bias_sums = jnp.sum(grad_projected, axis=(0, 1), dtype=jnp.float32)
    query_bias_part = bias_sums[:head_cols]
    value_bias_part = bias_sums[2 * head_cols :]
    row_portion = grad_projected
    grad_inputs = grad_residual + lax.psum_scatter(
        jnp.einsum(
            "sle,de->lsd", row_portion, project_full, preferred_element_type=jnp.float32
        ).astype(jnp.bfloat16),
        "tensor",
        scatter_dimension=0,
        tiled=True,
    ).astype(jnp.float32)
    project_shard, output_shard, up_shard, down_shard = reduce_weights(
        (project_grad, output_grad_weight, up_gradient, down_grad)
    )
    vectors = (
        lax.psum_scatter(
            spread_block(query_bias_part, tensor_index, width),
            ("dp", "tensor"),
            scatter_dimension=0,
            tiled=True,
        ),
        lax.psum_scatter(
            spread_block(value_bias_part, tensor_index, width),
            ("dp", "tensor"),
            scatter_dimension=0,
            tiled=True,
        ),
        lax.psum_scatter(output_bias_part, ("dp", "tensor"), scatter_dimension=0, tiled=True),
        lax.psum_scatter(first_gain_part, ("dp", "tensor"), scatter_dimension=0, tiled=True),
        lax.psum_scatter(first_shift_part, ("dp", "tensor"), scatter_dimension=0, tiled=True),
        lax.psum_scatter(
            spread_block(up_bias_part, tensor_index, hidden_cols * n_tensor),
            ("dp", "tensor"),
            scatter_dimension=0,
            tiled=True,
        ),
        lax.psum_scatter(down_bias_part, ("dp", "tensor"), scatter_dimension=0, tiled=True),
        lax.psum_scatter(second_gain_part, ("dp", "tensor"), scatter_dimension=0, tiled=True),
        lax.psum_scatter(second_shift_part, ("dp", "tensor"), scatter_dimension=0, tiled=True),
    )
    layer_output = second.astype(jnp.bfloat16)
    returned = lax.all_to_all(
        grad_inputs.astype(jnp.bfloat16), "dp", split_axis=0, concat_axis=1, tiled=True
    )
    tokens_grad = jnp.einsum(
        "qs,pqd->psd", placing, returned, preferred_element_type=jnp.float32
    ).astype(jnp.bfloat16)
    return (
        layer_output,
        tokens_grad,
        project_shard,
        vectors[0],
        vectors[1],
        output_shard,
        vectors[2],
        vectors[3],
        vectors[4],
        up_shard,
        vectors[5],
        down_shard,
        vectors[6],
        vectors[7],
        vectors[8],
    )


def solution(mesh):
    in_specs = (
        P(("dp", "tensor"), None, None),
        P(),
        P(),
        P("dp", "tensor"),
        P(),
        P(),
        P("dp", "tensor"),
        P(),
        P(),
        P(),
        P("dp", "tensor"),
        P(),
        P("dp", "tensor"),
        P(),
        P(),
        P(),
        P(("dp", "tensor"), None, None),
    )
    out_specs = (
        P("tensor", "dp", None),
        P(("dp", "tensor"), None, None),
        P("dp", "tensor"),
        P(("dp", "tensor")),
        P(("dp", "tensor")),
        P("dp", "tensor"),
        P(("dp", "tensor")),
        P(("dp", "tensor")),
        P(("dp", "tensor")),
        P("dp", "tensor"),
        P(("dp", "tensor")),
        P("dp", "tensor"),
        P(("dp", "tensor")),
        P(("dp", "tensor")),
        P(("dp", "tensor")),
    )
    return jax.shard_map(
        on_device, mesh=mesh, in_specs=in_specs, out_specs=out_specs, check_vma=False
    )
```

profile of v0, /device:TPU:12, one launch (start us, length us, event | category | flops | bytes accessed | tf_op | source)
XLA Modules:
  0.0 819.7 jit_solution(2936986631440480217)
XLA Ops:
  10.6 24.0 %all_to_all.45 = bf16[32,16,768]{2,0,1:T(8,128)(2,1)S(1)} all-to-all(bf16[32,16,768]{2,0,1:T(8,128)(2,1)S(1)} %copy.130), channel_id=1, replica_groups=mesh['dp'=8,'tensor'=4] {'dp'}, dimensions={1} | all-to-all | bytes 1572864 | tf_op jit(solution)/shard_map/all_to_all | solution.py:85
  37.4 28.4 %all_gather.30 = bf16[768,192]{1,0:T(8,128)(2,1)S(1)} all-gather(bf16[96,192]{1,0:T(8,128)(2,1)S(1)} %copy-done.29), channel_id=1, replica_groups=mesh['dp'=8,'tensor'=4] {'dp'}, dimensions={0}, use_global_device_ids=true | all-gather | bytes 331776 | tf_op jit(solution)/shard_map/all_gather | solution.py:100
  65.9 35.0 %all_gather.29 = bf16[768,576]{1,0:T(8,128)(2,1)} all-gather(bf16[96,576]{1,0:T(8,128)(2,1)S(1)} %copy-done.26), channel_id=1, replica_groups=mesh['dp'=8,'tensor'=4] {'dp'}, dimensions={0}, use_global_device_ids=true | all-gather | bytes 995328 | tf_op jit(solution)/shard_map/all_gather | solution.py:99
  105.1 19.3 %while.22 = (s32[]{:T(128)}, bf16[2,1024,192]{1,2,0:T(8,128)(2,1)S(1)}, f32[2,3,1024]{2,1,0:T(4,128)}, bf16[2,1024,576]{1,2,0:T(8,128)(2,1)S(1)}, pred[2,1024]{1,0:T(4,128)(4,1)S(1)}, /*index=5*/s32[]{:T(128)}) while((s32[]{:T(128)}, bf16[2,1024,192]{1,2,0:T(8,128)(2,1)S(1)}, f32[2,3,1024]{2,1,0:T(4,128)}, ...), condition=%wide.region_4.5_spmd, body=%wide.region_1.4_spmd.sunk | while | flops 843248640 | bytes 45139092 | solution.py:151
  130.1 40.8 %reduce-scatter.9.cloned.1.call-done = bf16[256,2,768]{2,0,1:T(8,128)(2,1)} async-done(((bf16[1024,2,768]{2,0,1:T(8,128)(2,1)}), bf16[256,2,768]{2,0,1:T(8,128)(2,1)}) %reduce-scatter.9.cloned.1.call-update) | async-done | bytes 786448 | tf_op jit(solution)/shard_map/reduce_scatter | solution.py:153
  178.7 27.1 %all-gather.9.cloned.1.call-done = bf16[1024,2,768]{2,0,1:T(8,128)(2,1)} async-done(((bf16[256,2,768]{2,0,1:T(8,128)(2,1)}), bf16[1024,2,768]{2,0,1:T(8,128)(2,1)}) %all-gather.9.cloned.1.call-update) | async-done | bytes 3145744 | tf_op jit(solution)/shard_map/all_gather | solution.py:166
  205.7 6.7 fusion.27
  215.1 15.8 %multiply_convert_fusion.1 = (bf16[1024,2,768]{2,0,1:T(8,128)(2,1)}, f32[1024,2,768]{2,0,1:T(8,128)}) fusion(f32[1024,2,768]{2,0,1:T(8,128)S(1)} %get-tuple-element.227, f32[768]{0:T(1024)S(1)} %copy-done.32, u8[1024,768]{1,0:T(8,128)(4,1)S(1)} %get-tuple-element.169, u8[1024,768]{1,0:T(8,128)(4,1)S(1)} %get-tuple-element.168), kind=kLoop, calls=%fused_computation.40 | loop fusion | flops 111673344 | bytes 17304576 | tf_op jit(solution)/shard_map/convert_element_type | solution.py:182
  230.9 16.3 %all-gather.13.cloned.1.call-done = bf16[768,768]{1,0:T(8,128)(2,1)} async-done(((bf16[96,768]{1,0:T(8,128)(2,1)}), bf16[768,768]{1,0:T(8,128)(2,1)}) %all-gather.13.cloned.1.call-update) | async-done | bytes 1179664 | tf_op jit(solution)/shard_map/all_gather | solution.py:102
  247.2 6.5 convolution_convert_fusion.1
  255.7 22.0 %all_to_all.46 = bf16[32,16,768]{2,0,1:T(8,128)(2,1)S(1)} all-to-all(bf16[32,16,768]{2,0,1:T(8,128)(2,1)S(1)} %copy.133), channel_id=1, replica_groups=mesh['dp'=8,'tensor'=4] {'dp'}, dimensions={1} | all-to-all | bytes 1572864 | tf_op jit(solution)/shard_map/all_to_all | solution.py:86
  298.1 29.2 %all-gather.15.cloned.1.call-done = bf16[1024,2,768]{2,0,1:T(8,128)(2,1)} async-done(((bf16[256,2,768]{2,0,1:T(8,128)(2,1)}), bf16[1024,2,768]{2,0,1:T(8,128)(2,1)}) %all-gather.15.cloned.1.call-update) | async-done | bytes 3145744 | tf_op jit(solution)/shard_map/all_gather | solution.py:206
  327.2 11.1 %convert_reduce_fusion = (f32[768]{0:T(1024)}, bf16[1024,2,768]{2,0,1:T(8,128)(2,1)S(1)}) fusion(f32[1024,2,768]{2,0,1:T(8,128)} %get-tuple-element.215, bf16[1024,2,768]{2,0,1:T(8,128)(2,1)} %all-gather.15.cloned.1.call-done, bf16[768,768]{1,0:T(8,128)(2,1)} %all-gather.13.cloned.1.call-done, f32[1024,2,768]{2,0,1:T(8,128)} %copy-done.16, ...), kind=kOutput, calls=%fused_computation.38 | convolution fusion | flops 2442657024 | bytes 20060160 | tf_op jit(solution)/shard_map/pna,ay->pny/dot_general | solution.py:209
  344.1 37.8 %reduce-scatter.13.cloned.1.call-done = bf16[256,2,768]{2,0,1:T(8,128)(2,1)} async-done(((bf16[1024,2,768]{2,0,1:T(8,128)(2,1)}), bf16[256,2,768]{2,0,1:T(8,128)(2,1)}) %reduce-scatter.13.cloned.1.call-update) | async-done | bytes 786448 | tf_op jit(solution)/shard_map/reduce_scatter | solution.py:224
  390.0 28.4 %all-gather.17.cloned.1.call-done = bf16[1024,2,768]{2,0,1:T(8,128)(2,1)} async-done(((bf16[256,2,768]{2,0,1:T(8,128)(2,1)}), bf16[1024,2,768]{2,0,1:T(8,128)(2,1)}) %all-gather.17.cloned.1.call-update) | async-done | bytes 3145744 | tf_op jit(solution)/shard_map/all_gather | solution.py:236
  421.5 52.0 %while.23 = (s32[]{:T(128)}, bf16[2,1024,576]{1,2,0:T(8,128)(2,1)}, bf16[2,1024,576]{1,2,0:T(8,128)(2,1)S(1)}, pred[2,1024]{1,0:T(4,128)(4,1)S(1)}, f32[2,3,1024...) while((s32[]{:T(128)}, bf16[2,1024,576]{1,2,0:T(8,128)(2,1)}, ...), condition=%wide.region_18.19_spmd, body=%wide.region_16.18_spmd.sunk | while | flops 2064970752 | bytes 159737168 | solution.py:286
  424.4 4.3 fusion.149
  428.7 4.8 multiply_reduce_fusion.8
  433.5 5.6 multiply_convert_fusion.3
  454.6 4.8 multiply_reduce_fusion.8
  459.3 5.6 multiply_convert_fusion.3
  473.5 6.3 convert_bitcast_fusion
  479.8 7.0 convolution_bitcast_fusion.1
  486.8 7.9 convolution_bitcast_fusion
  498.9 6.7 convolution_bitcast_fusion.2
  505.7 12.1 %reduce-scatter.15.cloned.1.call-done = bf16[256,2,768]{2,0,1:T(8,128)(2,1)} async-done(((bf16[1024,2,768]{2,0,1:T(8,128)(2,1)}), bf16[256,2,768]{2,0,1:T(8,128)(2,1)}) %reduce-scatter.15.cloned.1.call-update) | async-done | bytes 786448 | tf_op jit(solution)/shard_map/reduce_scatter | solution.py:294
  520.8 6.1 all-to-all-start.2
  531.3 50.8 %all-reduce.9 = (f32[768]{0:T(1024)S(1)}, f32[768]{0:T(1024)S(1)}, f32[768]{0:T(1024)S(1)}, f32[768]{0:T(1024)S(1)}, f32[768]{0:T(1024)S(1)}, /*index=5*/f32[307...) all-reduce(f32[768]{0:T(1024)S(1)} %slice_dynamic-update-slice_fusi, ...), channel_id=7, replica_groups=mesh['dp'=8,'tensor'=4] {'dp','tensor'}, use_global_device_ids=true, to_apply=%region_22.23.clone | all-reduce | flops 9216 | bytes 73728
  589.5 12.9 %reduce-scatter.21.cloned.1.call-done = f32[96,768]{1,0:T(8,128)} async-done(((f32[768,768]{1,0:T(8,128)}), f32[96,768]{1,0:T(8,128)}) %reduce-scatter.21.cloned.1.call-update) | async-done | bytes 294928 | tf_op jit(solution)/shard_map/reduce_scatter | solution.py:38
  602.4 72.8 %reduce-scatter.23.cloned.1.call-done = f32[96,768]{1,0:T(8,128)} async-done(((f32[768,768]{1,0:T(8,128)}), f32[96,768]{1,0:T(8,128)}) %reduce-scatter.23.cloned.1.call-update) | async-done | bytes 294928 | tf_op jit(solution)/shard_map/reduce_scatter | solution.py:39
  675.2 66.8 %reduce-scatter.19.cloned.1.call-done = f32[96,192]{1,0:T(8,128)} async-done(((f32[768,192]{1,0:T(8,128)}), f32[96,192]{1,0:T(8,128)}) %reduce-scatter.19.cloned.1.call-update) | async-done | bytes 73744 | tf_op jit(solution)/shard_map/reduce_scatter | solution.py:37
  742.0 70.0 %reduce-scatter.17.cloned.1.call-done = f32[96,576]{1,0:T(8,128)} async-done(((f32[768,576]{1,0:T(8,128)}), f32[96,576]{1,0:T(8,128)}) %reduce-scatter.17.cloned.1.call-update) | async-done | bytes 221200 | tf_op jit(solution)/shard_map/reduce_scatter | solution.py:36
  (245 shorter events, 129.4 us)
Async XLA Ops:
  8.0 92.9 %all-gather.7.cloned.1.call-start = ((), (), s32[]{:S(2)}) async-start(), calls=%async_computation.11 | async-start | bytes 3932160 | tf_op jit(solution)/shard_map/all_gather | solution.py:104
  10.3 26.9 %copy-start.38 = (s32[16]{0:T(128)S(1)}, s32[16]{0:T(128)}, u32[]{:S(2)}) copy-start(s32[16]{0:T(128)} %param.23) | copy-start | bytes 196
  10.3 26.9 %copy-start.43 = (s32[16]{0:T(128)S(1)}, s32[16]{0:T(128)}, u32[]{:S(2)}) copy-start(s32[16]{0:T(128)} %param.22) | copy-start | bytes 196
  10.3 27.1 %copy-start.29 = (bf16[96,192]{1,0:T(8,128)(2,1)S(1)}, bf16[96,192]{1,0:T(8,128)(2,1)}, u32[]{:S(2)}) copy-start(bf16[96,192]{1,0:T(8,128)(2,1)} %param.27) | copy-start | bytes 110596
  10.3 55.6 %copy-start.26 = (bf16[96,576]{1,0:T(8,128)(2,1)S(1)}, bf16[96,576]{1,0:T(8,128)(2,1)}, u32[]{:S(2)}) copy-start(bf16[96,576]{1,0:T(8,128)(2,1)} %param.24) | copy-start | bytes 331780
  35.5 135.4 %reduce-scatter.9.cloned.1.call-start = ((), (), s32[]{:S(2)}) async-start(), calls=%async_computation.12 | async-start | bytes 3932160 | tf_op jit(solution)/shard_map/reduce_scatter | solution.py:153
  125.3 45.6 %copy-start.4 = (bf16[32,8,2,768]{3,0,1,2:T(8,128)(2,1)S(1)}, bf16[32,8,2,768]{3,0,1,2:T(8,128)(2,1)}, u32[]{:S(2)}) copy-start(bf16[32,8,2,768]{3,0,1,2:T(8,128)(2,1)} %copy.131) | copy-start | bytes 2359300
  125.3 45.6 %copy-start.25 = (f32[768]{0:T(1024)S(1)}, f32[768]{0:T(1024)}, u32[]{:S(2)}) copy-start(f32[768]{0:T(1024)} %param.28) | copy-start | bytes 9220
  129.2 45.4 %copy-start.27 = (f32[768]{0:T(1024)S(1)}, f32[768]{0:T(1024)}, u32[]{:S(2)}) copy-start(f32[768]{0:T(1024)} %param.29) | copy-start | bytes 9220
  129.2 49.5 %all-gather.11.cloned.1.call-start = ((), (), s32[]{:S(2)}) async-start(), calls=%async_computation.14 | async-start | bytes 1327104 | tf_op jit(solution)/shard_map/all_gather | solution.py:101
  129.8 75.9 %all-gather.9.cloned.1.call-start = ((), (), s32[]{:S(2)}) async-start(), calls=%async_computation.13 | async-start | bytes 3932160 | tf_op jit(solution)/shard_map/all_gather | solution.py:166
  176.7 70.6 %all-gather.13.cloned.1.call-start = ((), (), s32[]{:S(2)}) async-start(), calls=%async_computation.15 | async-start | bytes 1327104 | tf_op jit(solution)/shard_map/all_gather | solution.py:102
  177.2 114.6 %reduce-scatter.11.cloned.1.call-start = ((), (), s32[]{:S(2)}) async-start(), calls=%async_computation.16 | async-start | bytes 3932160 | tf_op jit(solution)/shard_map/reduce_scatter | solution.py:184
  253.8 73.4 %all-gather.15.cloned.1.call-start = ((), (), s32[]{:S(2)}) async-start(), calls=%async_computation.17 | async-start | bytes 3932160 | tf_op jit(solution)/shard_map/all_gather | solution.py:206
  255.5 24.4 %copy-start.30 = (f32[768]{0:T(1024)S(1)}, f32[768]{0:T(1024)}, u32[]{:S(2)}) copy-start(f32[768]{0:T(1024)} %param.35) | copy-start | bytes 9220
  298.0 83.9 %reduce-scatter.13.cloned.1.call-start = ((), (), s32[]{:S(2)}) async-start(), calls=%async_computation.18 | async-start | bytes 3932160 | tf_op jit(solution)/shard_map/reduce_scatter | solution.py:224
  327.2 12.8 %copy-start.44 = (bf16[768,768]{1,0:T(8,128)(2,1)S(1)}, bf16[768,768]{1,0:T(8,128)(2,1)}, u32[]{:S(2)}) copy-start(bf16[768,768]{1,0:T(8,128)(2,1)} %all-gather.11.cloned.1.call-done) | copy-start | bytes 3538948
  344.0 74.4 %all-gather.17.cloned.1.call-start = ((), (), s32[]{:S(2)}) async-start(), calls=%async_computation.19 | async-start | bytes 3932160 | tf_op jit(solution)/shard_map/all_gather | solution.py:236
  389.7 128.0 %reduce-scatter.15.cloned.1.call-start = ((), (), s32[]{:S(2)}) async-start(), calls=%async_computation.20 | async-start | bytes 3932160 | tf_op jit(solution)/shard_map/reduce_scatter | solution.py:294
  479.7 122.7 %reduce-scatter.21.cloned.1.call-start = ((), (), s32[]{:S(2)}) async-start(), calls=%async_computation.23 | async-start | bytes 2654208 | tf_op jit(solution)/shard_map/reduce_scatter | solution.py:38
  486.8 188.4 %reduce-scatter.23.cloned.1.call-start = ((), (), s32[]{:S(2)}) async-start(), calls=%async_computation.24 | async-start | bytes 2654208 | tf_op jit(solution)/shard_map/reduce_scatter | solution.py:39
  494.7 247.2 %reduce-scatter.19.cloned.1.call-start = ((), (), s32[]{:S(2)}) async-start(), calls=%async_computation.22 | async-start | bytes 884736 | tf_op jit(solution)/shard_map/reduce_scatter | solution.py:37
  498.6 19.2 %copy-start.8 = (f32[256,2,768]{2,0,1:T(8,128)S(1)}, f32[256,2,768]{2,0,1:T(8,128)}, u32[]{:S(2)}) copy-start(f32[256,2,768]{2,0,1:T(8,128)} %copy-done.7) | copy-start | bytes 4718596
  498.6 313.3 %reduce-scatter.17.cloned.1.call-start = ((), (), s32[]{:S(2)}) async-start(), calls=%async_computation.21 | async-start | bytes 2211840 | tf_op jit(solution)/shard_map/reduce_scatter | solution.py:36
  505.6 21.2 %copy-start.15 = (bf16[32,16,768]{2,0,1:T(8,128)(2,1)S(1)}, bf16[32,16,768]{2,0,1:T(8,128)(2,1)}, u32[]{:S(2)}) copy-start(bf16[32,16,768]{2,0,1:T(8,128)(2,1)} %copy-done.14) | copy-start | bytes 2359300
  505.7 21.3 %copy-start.17 = (bf16[256,2,768]{2,0,1:T(8,128)(2,1)S(1)}, bf16[256,2,768]{2,0,1:T(8,128)(2,1)}, u32[]{:S(2)}) copy-start(bf16[256,2,768]{2,0,1:T(8,128)(2,1)} %get-tuple-element.226) | copy-start | bytes 2359300
  520.8 10.5 %copy-start.35 = (f32[768]{0:T(1024)S(1)}, f32[768]{0:T(1024)}, u32[]{:S(2)}) copy-start(f32[768]{0:T(1024)} %get-tuple-element.175) | copy-start | bytes 9220
  520.8 10.5 %copy-start.36 = (f32[768]{0:T(1024)S(1)}, f32[768]{0:T(1024)}, u32[]{:S(2)}) copy-start(f32[768]{0:T(1024)} %get-tuple-element.176) | copy-start | bytes 9220
  520.8 10.5 %copy-start.37 = (f32[768]{0:T(1024)S(1)}, f32[768]{0:T(1024)}, u32[]{:S(2)}) copy-start(f32[768]{0:T(1024)} %get-tuple-element.208) | copy-start | bytes 9220
  520.8 66.6 %all-to-all-start.2 = ((bf16[256,2,768]{2,1,0:T(2,128)(2,1)}), bf16[256,2,768]{2,1,0:T(2,128)(2,1)S(1)}, u32[]{:S(2)}, u32[]{:S(2)}) async-start(bf16[256,2,768]{2,1,0:T(2,128)(2,1)} %copy.139), calls=%async_computation.6 | async-start | bytes 1572864 | tf_op jit(solution)/shard_map/all_to_all | solution.py:332
  528.7 59.5 %copy-start.39 = (s32[16]{0:T(128)S(1)}, s32[16]{0:T(128)}, u32[]{:S(2)}) copy-start(s32[16]{0:T(128)} %param.23) | copy-start | bytes 196
  528.7 283.2 %copy-start.1 = (bf16[32,16,768]{2,1,0:T(8,128)(2,1)S(1)}, bf16[32,16,768]{2,1,0:T(8,128)(2,1)}, u32[]{:S(2)}) copy-start(bf16[32,16,768]{2,1,0:T(8,128)(2,1)} %param.21) | copy-start | bytes 2359300
  (38 other events, 125.2 us)
Sparse Core Ops, SparseCore 0:
  35.6 29.1 all-gather.6
  129.3 41.4 reduce-scatter.8
  298.1 29.0 all-gather.14
  389.9 28.4 all-gather.16
  479.8 37.8 reduce-scatter.14
  521.7 80.6 reduce-scatter.20
  606.5 68.6 reduce-scatter.22
  679.1 62.8 reduce-scatter.18
  746.0 65.8 reduce-scatter.16
Sparse Core Ops, SparseCore 1:
  131.9 43.1 all-gather.10
  177.0 28.7 all-gather.8
  207.8 39.4 all-gather.12
  253.9 38.0 reduce-scatter.10
  344.1 37.7 reduce-scatter.12
where the time goes:
time: 831 us; the launch traced here: 820 us
  waiting for transfers between devices  415 us (50%)
  blocking collectives  160 us (19%)
  matrix products  120 us (14%)
  other arithmetic  61.3 us (7%)
  local copies, waits for them, and re-layouts  38.1 us (5%)
  between operations  16.4 us (2%)
    reduce_scatter x1, waiting for transfers between devices, reduce_weights(): lax.psum_scatter(grads[3], 'dp', scatter_dimension=0, tiled=True)  72.8 us
    reduce_scatter x1, waiting for transfers between devices, reduce_weights(): lax.psum_scatter(grads[0], 'dp', scatter_dimension=0, tiled=True)  70 us
    reduce_scatter x1, waiting for transfers between devices, reduce_weights(): lax.psum_scatter(grads[1], 'dp', scatter_dimension=0, tiled=True)  66.8 us
    unnamed x1, blocking collectives  50.8 us
    reduce_scatter x1, waiting for transfers between devices, on_device(): lax.psum_scatter(jnp.einsum('sle,de->lsd', row_portion, output_full, pref...  40.8 us
    reduce_scatter x1, waiting for transfers between devices, on_device(): lax.psum_scatter(jnp.einsum('ran,en->rae', row_portion, up_weight_gathere...  37.8 us
    all_gather x1, blocking collectives, on_device(): lax.all_gather(project_weight, 'dp', axis=0, tiled=True)  35 us
    all_gather x1, waiting for transfers between devices, on_device(): lax.all_gather(grad_second.astype(jnp.bfloat16), 'tensor', axis=0, tiled=...  29.2 us
  transfers between devices with their start and end apart: 15, of which 11 were waited for; matrix products, arithmetic and copies ran while one was open for 10% of the time, Pallas kernels for 0%

commit v1 on v0

v1 whole, which is shorter than its diff:
```python
from functools import partial

import jax
import jax.numpy as jnp
from jax import lax
from jax.sharding import PartitionSpec as P

HD = 64


EPSILON = 1e-12
MASKED = -1e30


def norm_forward(value, gain, shift):
    centred = value - jnp.mean(value, axis=-1, keepdims=True)
    inverse = lax.rsqrt(jnp.mean(centred * centred, axis=-1, keepdims=True) + EPSILON)
    normed = centred * inverse
    return (normed * gain + shift, normed, inverse)


def norm_backward(upstream, normed, inverse, gain):
    scaled = upstream * gain
    first_mean = jnp.mean(scaled, axis=-1, keepdims=True)
    second_mean = jnp.mean(scaled * normed, axis=-1, keepdims=True)
    return inverse * (scaled - first_mean - normed * second_mean)


def spread_block(values, block_index, length_total):
    blank = jnp.zeros((length_total,), jnp.float32)
    return lax.dynamic_update_slice_in_dim(blank, values, block_index * values.shape[0], 0)


def gather_rows(block):
    return lax.all_gather(block, "tensor", axis=0, tiled=True)


def scatter_rows(partial_sum):
    return lax.psum_scatter(
        partial_sum.astype(jnp.bfloat16), "tensor", scatter_dimension=0, tiled=True
    ).astype(jnp.float32)


def scatter_weight(grad):
    return lax.psum_scatter(
        grad.astype(jnp.bfloat16), "dp", scatter_dimension=0, tiled=True
    ).astype(jnp.float32)


def on_device(
    tokens,
    lengths,
    dealing,
    project_weight,
    query_projection_bias,
    value_projection_bias,
    attention_output_weight,
    attention_output_bias,
    first_gain,
    first_shift,
    feed_input_weight,
    feed_input_bias,
    feed_output_weight,
    feed_output_bias,
    second_gain,
    second_shift,
    output_grad,
):
    n_data = lax.axis_size("dp")
    n_tensor = lax.axis_size("tensor")
    n_all = n_data * n_tensor
    data_index = lax.axis_index("dp")
    tensor_index = lax.axis_index("tensor")
    seq_total = dealing.shape[0]
    seq_here = seq_total // n_data
    piece_rows = tokens.shape[0]
    local_rows = piece_rows * n_data
    seq_rows = local_rows * n_tensor
    width = tokens.shape[2]
    head_cols = attention_output_weight.shape[1]
    heads_here = head_cols // HD
    hidden_cols = feed_input_weight.shape[1]
    score_scale = HD ** (-0.5)

    slot_ids = jnp.arange(seq_total, dtype=jnp.int32)
    placing = (dealing[None, :] == slot_ids[:, None]).astype(jnp.bfloat16)
    send_tokens = jnp.einsum(
        "qs,psd->pqd", placing, tokens, preferred_element_type=jnp.float32
    ).astype(jnp.bfloat16)
    send_grad = jnp.einsum(
        "qs,psd->pqd", placing, output_grad, preferred_element_type=jnp.float32
    ).astype(jnp.bfloat16)
    tokens_here = lax.all_to_all(send_tokens, "dp", split_axis=1, concat_axis=0, tiled=True)
    cotangent_here = lax.all_to_all(send_grad, "dp", split_axis=1, concat_axis=0, tiled=True)

    my_slots = data_index * seq_here + jnp.arange(seq_here, dtype=jnp.int32)
    mine = dealing[None, :] == my_slots[:, None]
    seq_length = jnp.sum(jnp.where(mine, lengths[None, :], 0), axis=1)
    row_ids = jnp.arange(seq_rows, dtype=jnp.int32)
    owner_rows = row_ids // local_rows
    inner_rows = row_ids % local_rows
    position = (
        inner_rows // piece_rows * n_tensor + owner_rows
    ) * piece_rows + inner_rows % piece_rows
    key_valid = position[None, :] < seq_length[:, None]

    project_full = lax.all_gather(project_weight, "dp", axis=0, tiled=True)
    output_full = lax.all_gather(attention_output_weight, "dp", axis=0, tiled=True)
    up_full = lax.all_gather(feed_input_weight, "dp", axis=0, tiled=True)
    down_full = lax.all_gather(feed_output_weight, "dp", axis=0, tiled=True)

    query_part = lax.dynamic_slice_in_dim(
        query_projection_bias, tensor_index * head_cols, head_cols
    )
    value_part = lax.dynamic_slice_in_dim(
        value_projection_bias, tensor_index * head_cols, head_cols
    )
    project_bias = jnp.concatenate([query_part, jnp.zeros_like(query_part), value_part])
    up_bias_here = lax.dynamic_slice_in_dim(
        feed_input_bias, tensor_index * hidden_cols, hidden_cols
    )

    def split_heads(qkv_block):
        query_rows = qkv_block[:, :head_cols].reshape(seq_rows, heads_here, HD)
        key_rows = qkv_block[:, head_cols : 2 * head_cols].reshape(seq_rows, heads_here, HD)
        value_rows = qkv_block[:, 2 * head_cols :].reshape(seq_rows, heads_here, HD)
        return (query_rows, key_rows, value_rows)

    def masked_scores(query_rows, key_rows, valid_keys):
        raw_scores = (
            jnp.einsum("qhe,khe->hqk", query_rows, key_rows, preferred_element_type=jnp.float32)
            * score_scale
        )
        return jnp.where(valid_keys[None, None, :], raw_scores, MASKED)

    def attend(qkv_block, valid_keys):
        query_rows, key_rows, value_rows = split_heads(qkv_block)
        scores = masked_scores(query_rows, key_rows, valid_keys)
        row_max = jnp.max(scores, axis=-1, keepdims=True)
        exponent = jnp.exp(scores - row_max)
        row_total = jnp.sum(exponent, axis=-1, keepdims=True)
        weights = (exponent / row_total).astype(jnp.bfloat16)
        mixed_heads = jnp.einsum(
            "hqk,khe->qhe", weights, value_rows, preferred_element_type=jnp.float32
        )
        return (
            mixed_heads.reshape(seq_rows, head_cols).astype(jnp.bfloat16),
            (row_max + jnp.log(row_total))[..., 0],
        )

    def attend_back(qkv_block, valid_keys, row_lse, grad_block):
        query_rows, key_rows, value_rows = split_heads(qkv_block)
        weights = jnp.exp(masked_scores(query_rows, key_rows, valid_keys) - row_lse[..., None])
        grad_heads = grad_block.reshape(seq_rows, heads_here, HD)
        grad_weights = jnp.einsum(
            "qhe,khe->hqk", grad_heads, value_rows, preferred_element_type=jnp.float32
        )
        inner_sum = jnp.sum(weights * grad_weights, axis=-1, keepdims=True)
        grad_scores = (weights * (grad_weights - inner_sum)).astype(jnp.bfloat16)
        grad_query = (
            jnp.einsum("hqk,khe->qhe", grad_scores, key_rows, preferred_element_type=jnp.float32)
            * score_scale
        )
        grad_key = (
            jnp.einsum("hqk,qhe->khe", grad_scores, query_rows, preferred_element_type=jnp.float32)
            * score_scale
        )
        grad_value = jnp.einsum(
            "hqk,qhe->khe", weights.astype(jnp.bfloat16), grad_heads,
            preferred_element_type=jnp.float32,
        )
        joined = jnp.concatenate(
            [
                grad_query.reshape(seq_rows, head_cols),
                grad_key.reshape(seq_rows, head_cols),
                grad_value.reshape(seq_rows, head_cols),
            ],
            axis=-1,
        )
        return joined.astype(jnp.bfloat16)

    gelu_exact = partial(jax.nn.gelu, approximate=False)
    seqs = range(seq_here)

    inputs_full = [gather_rows(tokens_here[:, s, :]) for s in seqs]
    projected = [
        (
            jnp.dot(inputs_full[s], project_full, preferred_element_type=jnp.float32)
            + project_bias
        ).astype(jnp.bfloat16)
        for s in seqs
    ]
    attended = [attend(projected[s], key_valid[s]) for s in seqs]
    mixed = [a[0] for a in attended]
    log_total = [a[1] for a in attended]
    branch = [
        scatter_rows(
            lax.dot_general(
                mixed[s], output_full, (((1,), (1,)), ((), ())),
                preferred_element_type=jnp.float32,
            )
        )
        for s in seqs
    ]
    first = [
        norm_forward(
            tokens_here[:, s, :].astype(jnp.float32) + branch[s] + attention_output_bias,
            first_gain,
            first_shift,
        )
        for s in seqs
    ]
    first_full = [gather_rows(first[s][0].astype(jnp.bfloat16)) for s in seqs]
    preact = [
        jnp.dot(first_full[s], up_full, preferred_element_type=jnp.float32) + up_bias_here
        for s in seqs
    ]
    gelu_pairs = [jax.vjp(gelu_exact, preact[s]) for s in seqs]
    hidden = [g[0].astype(jnp.bfloat16) for g in gelu_pairs]
    feed = [
        scatter_rows(
            lax.dot_general(
                hidden[s], down_full, (((1,), (1,)), ((), ())),
                preferred_element_type=jnp.float32,
            )
        )
        for s in seqs
    ]
    second = [
        norm_forward(first[s][0] + feed[s] + feed_output_bias, second_gain, second_shift)
        for s in seqs
    ]
    layer_output = jnp.stack([second[s][0] for s in seqs], axis=1).astype(jnp.bfloat16)

    cot = [cotangent_here[:, s, :].astype(jnp.float32) for s in seqs]
    second_gain_part = sum(jnp.sum(cot[s] * second[s][1], axis=0) for s in seqs)
    second_shift_part = sum(jnp.sum(cot[s], axis=0) for s in seqs)
    grad_second = [norm_backward(cot[s], second[s][1], second[s][2], second_gain) for s in seqs]
    down_bias_part = sum(jnp.sum(grad_second[s], axis=0) for s in seqs)
    grad_feed_full = [gather_rows(grad_second[s].astype(jnp.bfloat16)) for s in seqs]
    grad_hidden = [
        jnp.dot(grad_feed_full[s], down_full, preferred_element_type=jnp.float32) for s in seqs
    ]
    down_grad = sum(
        lax.dot_general(
            grad_feed_full[s], hidden[s], (((0,), (0,)), ((), ())),
            preferred_element_type=jnp.float32,
        )
        for s in seqs
    )
    down_shard = scatter_weight(down_grad)
    grad_preact = [gelu_pairs[s][1](grad_hidden[s])[0].astype(jnp.bfloat16) for s in seqs]
    up_grad = sum(
        lax.dot_general(
            first_full[s], grad_preact[s], (((0,), (0,)), ((), ())),
            preferred_element_type=jnp.float32,
        )
        for s in seqs
    )
    up_shard = scatter_weight(up_grad)
    up_bias_part = sum(jnp.sum(grad_preact[s], axis=0, dtype=jnp.float32) for s in seqs)
    grad_first = [
        grad_second[s]
        + scatter_rows(
            lax.dot_general(
                grad_preact[s], up_full, (((1,), (1,)), ((), ())),
                preferred_element_type=jnp.float32,
            )
        )
        for s in seqs
    ]
    first_gain_part = sum(jnp.sum(grad_first[s] * first[s][1], axis=0) for s in seqs)
    first_shift_part = sum(jnp.sum(grad_first[s], axis=0) for s in seqs)
    grad_residual = [
        norm_backward(grad_first[s], first[s][1], first[s][2], first_gain) for s in seqs
    ]
    output_bias_part = sum(jnp.sum(grad_residual[s], axis=0) for s in seqs)
    early_vectors = jnp.concatenate(
        [
            v.reshape(n_all, -1)
            for v in (
                output_bias_part,
                first_gain_part,
                first_shift_part,
                spread_block(up_bias_part, tensor_index, hidden_cols * n_tensor),
                down_bias_part,
                second_gain_part,
                second_shift_part,
            )
        ],
        axis=1,
    )
    early_reduced = lax.psum_scatter(
        early_vectors, ("dp", "tensor"), scatter_dimension=0, tiled=True
    )[0]
    branch_grad_full = [gather_rows(grad_residual[s].astype(jnp.bfloat16)) for s in seqs]
    grad_mixed = [
        jnp.dot(branch_grad_full[s], output_full, preferred_element_type=jnp.float32).astype(
            jnp.bfloat16
        )
        for s in seqs
    ]
    output_grad_weight = sum(
        lax.dot_general(
            branch_grad_full[s], mixed[s], (((0,), (0,)), ((), ())),
            preferred_element_type=jnp.float32,
        )
        for s in seqs
    )
    output_shard = scatter_weight(output_grad_weight)
    grad_projected = [
        attend_back(projected[s], key_valid[s], log_total[s], grad_mixed[s]) for s in seqs
    ]
    project_grad = sum(
        lax.dot_general(
            inputs_full[s], grad_projected[s], (((0,), (0,)), ((), ())),
            preferred_element_type=jnp.float32,
        )
        for s in seqs
    )
    project_shard = scatter_weight(project_grad)
    bias_sums = sum(jnp.sum(grad_projected[s], axis=0, dtype=jnp.float32) for s in seqs)
    late_vectors = jnp.concatenate(
        [
            spread_block(bias_sums[:head_cols], tensor_index, width).reshape(n_all, -1),
            spread_block(bias_sums[2 * head_cols :], tensor_index, width).reshape(n_all, -1),
        ],
        axis=1,
    )
    late_reduced = lax.psum_scatter(
        late_vectors, ("dp", "tensor"), scatter_dimension=0, tiled=True
    )[0]
    grad_inputs = [
        grad_residual[s]
        + scatter_rows(
            lax.dot_general(
                grad_projected[s], project_full, (((1,), (1,)), ((), ())),
                preferred_element_type=jnp.float32,
            )
        )
        for s in seqs
    ]
    grad_here = jnp.stack(grad_inputs, axis=1).astype(jnp.bfloat16)
    returned = lax.all_to_all(grad_here, "dp", split_axis=0, concat_axis=1, tiled=True)
    tokens_grad = jnp.einsum(
        "qs,pqd->psd", placing, returned, preferred_element_type=jnp.float32
    ).astype(jnp.bfloat16)

    vec_block = width // n_all
    early_split = [vec_block] * 3 + [hidden_cols * n_tensor // n_all] + [vec_block] * 3
    offsets = [sum(early_split[:k]) for k in range(len(early_split) + 1)]
    early = [early_reduced[offsets[k] : offsets[k + 1]] for k in range(len(early_split))]
    late = [late_reduced[:vec_block], late_reduced[vec_block:]]
    return (
        layer_output,
        tokens_grad,
        project_shard,
        late[0],
        late[1],
        output_shard,
        early[0],
        early[1],
        early[2],
        up_shard,
        early[3],
        down_shard,
        early[4],
        early[5],
        early[6],
    )


def solution(mesh):
    in_specs = (
        P(("dp", "tensor"), None, None),
        P(),
        P(),
        P("dp", "tensor"),
        P(),
        P(),
        P("dp", "tensor"),
        P(),
        P(),
        P(),
        P("dp", "tensor"),
        P(),
        P("dp", "tensor"),
        P(),
        P(),
        P(),
        P(("dp", "tensor"), None, None),
    )
    out_specs = (
        P("tensor", "dp", None),
        P(("dp", "tensor"), None, None),
        P("dp", "tensor"),
        P(("dp", "tensor")),
        P(("dp", "tensor")),
        P("dp", "tensor"),
        P(("dp", "tensor")),
        P(("dp", "tensor")),
        P(("dp", "tensor")),
        P("dp", "tensor"),
        P(("dp", "tensor")),
        P("dp", "tensor"),
        P(("dp", "tensor")),
        P(("dp", "tensor")),
        P(("dp", "tensor")),
    )
    return jax.shard_map(
        on_device, mesh=mesh, in_specs=in_specs, out_specs=out_specs, check_vma=False
    )
```

time: 831 us -> 859 us (1.034)
  waiting for transfers between devices: 415 us -> 456 us
  matrix products: 120 us -> 136 us
  blocking collectives: 160 us -> 147 us
  local copies, waits for them, and re-layouts: 38.1 us -> 28.7 us
    reduce_scatter x8 -> x12, waiting for transfers between devices: 313 us -> 344 us  [the longest x4 207 us: scatter_weight(): lax.psum_scatter(grad.astype(jnp.bfloat16), 'dp', scatter_dimension=0, ti...]
    dot_general x24 -> x34, matrix products: 108 us -> 128 us  [the longest x2 22.2 us: on_device(): jnp.dot(first_full[s], up_full, preferred_element_type=jnp.float32)]
    unnamed x1, blocking collectives: 50.8 us -> 40.2 us
    convert_element_type x6 -> x9, other arithmetic: 23.6 us -> 15.3 us  [the longest x4 6.34 us: scatter_weight(): return lax.psum_scatter(grad.astype(jnp.bfloat16), 'dp', scatter_dimensio...]
    all_gather x6 -> x10, waiting for transfers between devices: 101 us -> 109 us  [the longest x8 84.6 us: gather_rows(): return lax.all_gather(block, 'tensor', axis=0, tiled=True)]
    unnamed x85 -> x150, local copies, waits for them, and re-layouts: 17.6 us -> 17.4 us
  transfers between devices with their start and end apart: 15 -> 23, of which waited for: 11 -> 17; matrix products, arithmetic and copies ran while one was open for 10% -> 18% of each run, Pallas kernels for 0% -> 0%
where the time goes in v1:
time: 859 us; the launch traced here: 848 us
  waiting for transfers between devices  456 us (53%)
  blocking collectives  147 us (17%)
  matrix products  136 us (16%)
  other arithmetic  55.4 us (6%)
  local copies, waits for them, and re-layouts  28.7 us (3%)
  between operations  16.9 us (2%)
    reduce_scatter x4, waiting for transfers between devices, scatter_weight(): lax.psum_scatter(grad.astype(jnp.bfloat16), 'dp', scatter_dimension=0, ti...  207 us
    reduce_scatter x8, waiting for transfers between devices, scatter_rows(): lax.psum_scatter(partial_sum.astype(jnp.bfloat16), 'tensor', scatter_dime...  137 us
    all_gather x8, waiting for transfers between devices, gather_rows(): return lax.all_gather(block, 'tensor', axis=0, tiled=True)  84.6 us
    unnamed x1, blocking collectives  40.2 us
    all_gather x1, blocking collectives, on_device(): project_full = lax.all_gather(project_weight, 'dp', axis=0, tiled=True)  32.8 us
    all_gather x1, blocking collectives, on_device(): lax.all_gather(attention_output_weight, 'dp', axis=0, tiled=True)  28.5 us
    all_gather x1, waiting for transfers between devices, on_device(): down_full = lax.all_gather(feed_output_weight, 'dp', axis=0, tiled=True)  24.4 us
    all_to_all x1, blocking collectives, on_device(): lax.all_to_all(send_tokens, 'dp', split_axis=1, concat_axis=0, tiled=True)  24.1 us
  transfers between devices with their start and end apart: 23, of which 17 were waited for; matrix products, arithmetic and copies ran while one was open for 18% of the time, Pallas kernels for 0%

profile of v1, /device:TPU:12, one launch (start us, length us, event | category | flops | bytes accessed | tf_op | source)
XLA Modules:
  0.0 848.4 jit_solution(14724456239618128440)
XLA Ops:
  10.6 24.1 %all_to_all.54 = bf16[32,16,768]{2,0,1:T(8,128)(2,1)S(1)} all-to-all(bf16[32,16,768]{2,0,1:T(8,128)(2,1)S(1)} %copy.78), channel_id=1, replica_groups=mesh['dp'=8,'tensor'=4] {'dp'}, dimensions={1} | all-to-all | bytes 1572864 | tf_op jit(solution)/shard_map/all_to_all | solution.py:93
  38.4 28.5 %all_gather.38 = bf16[768,192]{1,0:T(8,128)(2,1)S(1)} all-gather(bf16[96,192]{1,0:T(8,128)(2,1)S(1)} %copy-done.49), channel_id=1, replica_groups=mesh['dp'=8,'tensor'=4] {'dp'}, dimensions={0}, use_global_device_ids=true | all-gather | bytes 331776 | tf_op jit(solution)/shard_map/all_gather | solution.py:108
  66.9 32.8 %all_gather.37 = bf16[768,576]{1,0:T(8,128)(2,1)S(1)} all-gather(bf16[96,576]{1,0:T(8,128)(2,1)S(1)} %copy-done.45), channel_id=1, replica_groups=mesh['dp'=8,'tensor'=4] {'dp'}, dimensions={0}, use_global_device_ids=true | all-gather | bytes 995328 | tf_op jit(solution)/shard_map/all_gather | solution.py:107
  130.1 19.5 %reduce-scatter.13.cloned.1.call-done = bf16[256,768]{1,0:T(8,128)(2,1)} async-done(((bf16[1024,768]{1,0:T(8,128)(2,1)}), bf16[256,768]{1,0:T(8,128)(2,1)}) %reduce-scatter.13.cloned.1.call-update) | async-done | bytes 393232 | tf_op jit(solution)/shard_map/reduce_scatter | solution.py:39
  150.9 29.2 %reduce-scatter.17.cloned.1.call-done = bf16[256,768]{1,0:T(8,128)(2,1)} async-done(((bf16[1024,768]{1,0:T(8,128)(2,1)}), bf16[256,768]{1,0:T(8,128)(2,1)}) %reduce-scatter.17.cloned.1.call-update) | async-done | bytes 393232 | tf_op jit(solution)/shard_map/reduce_scatter | solution.py:39
  187.7 17.2 %all-gather.19.cloned.1.call-done = bf16[1024,768]{1,0:T(8,128)(2,1)} async-done(((bf16[256,768]{1,0:T(8,128)(2,1)}), bf16[1024,768]{1,0:T(8,128)(2,1)}) %all-gather.19.cloned.1.call-update) | async-done | bytes 1572880 | tf_op jit(solution)/shard_map/all_gather | solution.py:35
  204.9 4.9 fusion.119
  209.8 16.7 %all-gather.13.cloned.1.call-done = bf16[1024,768]{1,0:T(8,128)(2,1)} async-done(((bf16[256,768]{1,0:T(8,128)(2,1)}), bf16[1024,768]{1,0:T(8,128)(2,1)}) %all-gather.13.cloned.1.call-update) | async-done | bytes 1572880 | tf_op jit(solution)/shard_map/all_gather | solution.py:35
  226.5 17.4 %multiply_convert_fusion.3 = (bf16[1024,768]{1,0:T(8,128)(2,1)}, f32[1024,768]{1,0:T(8,128)}, bf16[1024,768]{1,0:T(8,128)(2,1)}, f32[1024,768]{1,0:T(8,128)}, f32[1024,768]{1,0:T(8,128)}) fusion(f32[768]{0:T(1024)S(1)} %dynamic_slice.11, f32[1024,768]{1,0:T(8,128)} %fusion.119, bf16[1024,768]{1,0:T(8,128)(2,1)} %all-gather.13.cloned.1.call-done, ...), kind=kOutput, calls=%fused_computation.43 | convolution fusion | flops 1311768576 | bytes 18484224 | tf_op jit(solution)/shard_map/dot_general | solution.py:215
  243.8 24.4 %all-gather.17.cloned.1.call-done = bf16[768,768]{1,0:T(8,128)(2,1)} async-done(((bf16[96,768]{1,0:T(8,128)(2,1)}), bf16[768,768]{1,0:T(8,128)(2,1)}) %all-gather.17.cloned.1.call-update) | async-done | bytes 1179664 | tf_op jit(solution)/shard_map/all_gather | solution.py:110
  272.6 4.4 convolution_convert_fusion.4
  278.5 21.6 %all_to_all.55 = bf16[32,16,768]{2,0,1:T(8,128)(2,1)S(1)} all-to-all(bf16[32,16,768]{2,0,1:T(8,128)(2,1)S(1)} %copy.83), channel_id=1, replica_groups=mesh['dp'=8,'tensor'=4] {'dp'}, dimensions={1} | all-to-all | bytes 1572864 | tf_op jit(solution)/shard_map/all_to_all | solution.py:94
  300.9 30.5 %reduce-scatter.19.cloned.1.call-done = bf16[256,768]{1,0:T(8,128)(2,1)} async-done(((bf16[1024,768]{1,0:T(8,128)(2,1)}), bf16[256,768]{1,0:T(8,128)(2,1)}) %reduce-scatter.19.cloned.1.call-update) | async-done | bytes 393232 | tf_op jit(solution)/shard_map/reduce_scatter | solution.py:39
  339.5 18.6 %all-gather.21.cloned.1.call-done = bf16[1024,768]{1,0:T(8,128)(2,1)} async-done(((bf16[256,768]{1,0:T(8,128)(2,1)}), bf16[1024,768]{1,0:T(8,128)(2,1)}) %all-gather.21.cloned.1.call-update) | async-done | bytes 1572880 | tf_op jit(solution)/shard_map/all_gather | solution.py:35
  358.1 4.8 fusion.120
  362.9 16.3 %all-gather.25.cloned.1.call-done = bf16[1024,768]{1,0:T(8,128)(2,1)} async-done(((bf16[256,768]{1,0:T(8,128)(2,1)}), bf16[1024,768]{1,0:T(8,128)(2,1)}) %all-gather.25.cloned.1.call-update) | async-done | bytes 1572880 | tf_op jit(solution)/shard_map/all_gather | solution.py:35
  379.2 11.5 %convert_reduce_fusion = (f32[768]{0:T(1024)}, bf16[1024,768]{1,0:T(8,128)(2,1)}, f32[768]{0:T(1024)}, bf16[1024,768]{1,0:T(8,128)(2,1)S(1)}) fusion(f32[1024,768]{1,0:T(8,128)} %get-tuple-element.152, f32[1024,768]{1,0:T(8,128)} %fusion.119, f32[768]{0:T(1024)} %copy-done.58, f32[1024,768]{1,0:T(8,128)} %fusion.120, f32[1024,768]{1,0:T(8,128)} %get-tuple-element.119, ...), kind=kOutput, calls=%fused_computation.26 | convolution fusion | flops 1234696704 | bytes 21636096 | tf_op jit(solution)/shard_map/dot_general | solution.py:242
  399.0 23.6 %reduce-scatter.21.cloned.1.call-done = bf16[256,768]{1,0:T(8,128)(2,1)} async-done(((bf16[1024,768]{1,0:T(8,128)(2,1)}), bf16[256,768]{1,0:T(8,128)(2,1)}) %reduce-scatter.21.cloned.1.call-update) | async-done | bytes 393232 | tf_op jit(solution)/shard_map/reduce_scatter | solution.py:39
  422.6 30.4 %reduce-scatter.25.cloned.1.call-done = bf16[256,768]{1,0:T(8,128)(2,1)} async-done(((bf16[1024,768]{1,0:T(8,128)(2,1)}), bf16[256,768]{1,0:T(8,128)(2,1)}) %reduce-scatter.25.cloned.1.call-update) | async-done | bytes 393232 | tf_op jit(solution)/shard_map/reduce_scatter | solution.py:39
  464.8 15.8 %all-gather.27.cloned.1.call-done = bf16[1024,768]{1,0:T(8,128)(2,1)} async-done(((bf16[256,768]{1,0:T(8,128)(2,1)}), bf16[1024,768]{1,0:T(8,128)(2,1)}) %all-gather.27.cloned.1.call-update) | async-done | bytes 1572880 | tf_op jit(solution)/shard_map/all_gather | solution.py:35
  482.7 6.1 multiply_reduce_fusion
  491.5 5.2 multiply_convert_fusion
  496.7 5.0 fusion.38
  510.1 6.4 multiply_reduce_fusion.1
  519.2 5.2 multiply_convert_fusion.1
  524.4 5.0 fusion.36
  570.2 6.0 all-to-all-start.2
  577.1 62.1 %reduce-scatter.35.cloned.1.call-done = bf16[96,768]{1,0:T(8,128)(2,1)} async-done(((bf16[768,768]{1,0:T(8,128)(2,1)}), bf16[96,768]{1,0:T(8,128)(2,1)}) %reduce-scatter.35.cloned.1.call-update) | async-done | bytes 147472 | tf_op jit(solution)/shard_map/reduce_scatter | solution.py:45
  640.8 65.5 %reduce-scatter.33.cloned.1.call-done = bf16[96,768]{1,0:T(8,128)(2,1)} async-done(((bf16[768,768]{1,0:T(8,128)(2,1)}), bf16[96,768]{1,0:T(8,128)(2,1)}) %reduce-scatter.33.cloned.1.call-update) | async-done | bytes 147472 | tf_op jit(solution)/shard_map/reduce_scatter | solution.py:45
  714.5 40.2 %all-reduce.2 = (f32[32,48]{1,0:T(8,128)S(1)}, f32[32,240]{1,0:T(8,128)S(1)}) all-reduce(f32[32,48]{1,0:T(8,128)S(1)} %pad_maximum_fusion.4, f32[32,240]{1,0:T(8,128)} %concatenate.21), channel_id=13, replica_groups=mesh['dp'=8,'tensor'=4] {'dp','tensor'}, use_global_device_ids=true, to_apply=%region_34.35.clone | all-reduce | flops 9216 | bytes 73728
  756.5 14.5 %reduce-scatter.31.cloned.1.call-done = bf16[96,192]{1,0:T(8,128)(2,1)} async-done(((bf16[768,192]{1,0:T(8,128)(2,1)}), bf16[96,192]{1,0:T(8,128)(2,1)}) %reduce-scatter.31.cloned.1.call-update) | async-done | bytes 36880 | tf_op jit(solution)/shard_map/reduce_scatter | solution.py:45
  772.5 64.8 %reduce-scatter.29.cloned.1.call-done = bf16[96,576]{1,0:T(8,128)(2,1)} async-done(((bf16[768,576]{1,0:T(8,128)(2,1)}), bf16[96,576]{1,0:T(8,128)(2,1)}) %reduce-scatter.29.cloned.1.call-update) | async-done | bytes 110608 | tf_op jit(solution)/shard_map/reduce_scatter | solution.py:45
  (325 shorter events, 153.5 us)
Async XLA Ops:
  8.0 91.6 %all-gather.31.cloned.1.call-start = ((), (), s32[]{:S(2)}) async-start(), calls=%async_computation.36 | async-start | bytes 1966080 | tf_op jit(solution)/shard_map/all_gather | solution.py:35
  10.6 56.3 %copy-start.45 = (bf16[96,576]{1,0:T(8,128)(2,1)S(1)}, bf16[96,576]{1,0:T(8,128)(2,1)}, u32[]{:S(2)}) copy-start(bf16[96,576]{1,0:T(8,128)(2,1)} %param.20) | copy-start | bytes 331780
  35.7 67.6 %all-gather.29.cloned.1.call-start = ((), (), s32[]{:S(2)}) async-start(), calls=%async_computation.35 | async-start | bytes 1966080 | tf_op jit(solution)/shard_map/all_gather | solution.py:35
  36.4 113.2 %reduce-scatter.13.cloned.1.call-start = ((), (), s32[]{:S(2)}) async-start(), calls=%async_computation.15 | async-start | bytes 1966080 | tf_op jit(solution)/shard_map/reduce_scatter | solution.py:39
  118.0 62.2 %reduce-scatter.17.cloned.1.call-start = ((), (), s32[]{:S(2)}) async-start(), calls=%async_computation.20 | async-start | bytes 1966080 | tf_op jit(solution)/shard_map/reduce_scatter | solution.py:39
  127.6 54.0 %copy-start.25 = (bf16[3,64,1024]{2,1,0:T(8,128)(2,1)}, bf16[3,64,1024]{2,1,0:T(8,128)(2,1)S(1)}, u32[]{:S(2)}) copy-start(bf16[3,64,1024]{2,1,0:T(8,128)(2,1)S(1)} %fusion.46) | copy-start | bytes 1179652
  127.7 55.3 %copy-start.48 = (f32[768]{0:T(1024)S(1)}, f32[768]{0:T(1024)}, u32[]{:S(2)}) copy-start(f32[768]{0:T(1024)} %param.25) | copy-start | bytes 9220
  127.7 55.3 %copy-start.54 = (f32[768]{0:T(1024)S(1)}, f32[768]{0:T(1024)}, u32[]{:S(2)}) copy-start(f32[768]{0:T(1024)} %param.26) | copy-start | bytes 9220
  129.5 58.2 %all-gather.15.cloned.1.call-start = ((), (), s32[]{:S(2)}) async-start(), calls=%async_computation.17 | async-start | bytes 1327104 | tf_op jit(solution)/shard_map/all_gather | solution.py:109
  130.1 74.9 %all-gather.19.cloned.1.call-start = ((), (), s32[]{:S(2)}) async-start(), calls=%async_computation.21 | async-start | bytes 1966080 | tf_op jit(solution)/shard_map/all_gather | solution.py:35
  185.3 41.1 %all-gather.13.cloned.1.call-start = ((), (), s32[]{:S(2)}) async-start(), calls=%async_computation.16 | async-start | bytes 1966080 | tf_op jit(solution)/shard_map/all_gather | solution.py:35
  185.9 82.3 %all-gather.17.cloned.1.call-start = ((), (), s32[]{:S(2)}) async-start(), calls=%async_computation.18 | async-start | bytes 1327104 | tf_op jit(solution)/shard_map/all_gather | solution.py:110
  186.6 114.2 %reduce-scatter.15.cloned.1.call-start = ((), (), s32[]{:S(2)}) async-start(), calls=%async_computation.19 | async-start | bytes 1966080 | tf_op jit(solution)/shard_map/reduce_scatter | solution.py:39
  272.5 58.9 %reduce-scatter.19.cloned.1.call-start = ((), (), s32[]{:S(2)}) async-start(), calls=%async_computation.22 | async-start | bytes 1966080 | tf_op jit(solution)/shard_map/reduce_scatter | solution.py:39
  277.0 54.4 %copy-start.7 = (bf16[256,768]{1,0:T(8,128)(2,1)S(1)}, bf16[256,768]{1,0:T(8,128)(2,1)}, u32[]{:S(2)}) copy-start(bf16[256,768]{1,0:T(8,128)(2,1)} %reduce-scatter.17.cloned.1.call-done) | copy-start | bytes 1179652
  277.0 81.1 %all-gather.21.cloned.1.call-start = ((), (), s32[]{:S(2)}) async-start(), calls=%async_computation.23 | async-start | bytes 1966080 | tf_op jit(solution)/shard_map/all_gather | solution.py:35
  338.3 40.9 %all-gather.25.cloned.1.call-start = ((), (), s32[]{:S(2)}) async-start(), calls=%async_computation.27 | async-start | bytes 1966080 | tf_op jit(solution)/shard_map/all_gather | solution.py:35
  339.2 83.4 %reduce-scatter.21.cloned.1.call-start = ((), (), s32[]{:S(2)}) async-start(), calls=%async_computation.24 | async-start | bytes 1966080 | tf_op jit(solution)/shard_map/reduce_scatter | solution.py:39
  394.5 58.5 %reduce-scatter.25.cloned.1.call-start = ((), (), s32[]{:S(2)}) async-start(), calls=%async_computation.28 | async-start | bytes 1966080 | tf_op jit(solution)/shard_map/reduce_scatter | solution.py:39
  399.0 81.6 %all-gather.27.cloned.1.call-start = ((), (), s32[]{:S(2)}) async-start(), calls=%async_computation.29 | async-start | bytes 1966080 | tf_op jit(solution)/shard_map/all_gather | solution.py:35
  460.8 47.2 %all-gather.23.cloned.1.call-start = ((), (), s32[]{:S(2)}) async-start(), calls=%async_computation.25 | async-start | bytes 1966080 | tf_op jit(solution)/shard_map/all_gather | solution.py:35
  464.3 96.8 %reduce-scatter.27.cloned.1.call-start = ((), (), s32[]{:S(2)}) async-start(), calls=%async_computation.30 | async-start | bytes 1966080 | tf_op jit(solution)/shard_map/reduce_scatter | solution.py:39
  507.7 58.6 %reduce-scatter.23.cloned.1.call-start = ((), (), s32[]{:S(2)}) async-start(), calls=%async_computation.26 | async-start | bytes 1966080 | tf_op jit(solution)/shard_map/reduce_scatter | solution.py:39
  535.4 103.8 %reduce-scatter.35.cloned.1.call-start = ((), (), s32[]{:S(2)}) async-start(), calls=%async_computation.34 | async-start | bytes 1327104 | tf_op jit(solution)/shard_map/reduce_scatter | solution.py:45
  541.6 164.7 %reduce-scatter.33.cloned.1.call-start = ((), (), s32[]{:S(2)}) async-start(), calls=%async_computation.33 | async-start | bytes 1327104 | tf_op jit(solution)/shard_map/reduce_scatter | solution.py:45
  548.0 223.1 %reduce-scatter.31.cloned.1.call-start = ((), (), s32[]{:S(2)}) async-start(), calls=%async_computation.32 | async-start | bytes 442368 | tf_op jit(solution)/shard_map/reduce_scatter | solution.py:45
  555.4 281.9 %reduce-scatter.29.cloned.1.call-start = ((), (), s32[]{:S(2)}) async-start(), calls=%async_computation.31 | async-start | bytes 1105920 | tf_op jit(solution)/shard_map/reduce_scatter | solution.py:45
  567.4 145.1 %copy-start.28 = (bf16[3,64,1024]{2,1,0:T(8,128)(2,1)S(1)}, bf16[3,64,1024]{2,1,0:T(8,128)(2,1)}, u32[]{:S(2)}) copy-start(bf16[3,64,1024]{2,1,0:T(8,128)(2,1)} %copy-done.27) | copy-start | bytes 1179652
  567.4 145.1 %copy-start.30 = (bf16[3,64,1024]{2,1,0:T(8,128)(2,1)S(1)}, bf16[3,64,1024]{2,1,0:T(8,128)(2,1)}, u32[]{:S(2)}) copy-start(bf16[3,64,1024]{2,1,0:T(8,128)(2,1)} %copy-done.29) | copy-start | bytes 1179652
  570.2 268.7 %all-to-all-start.2 = ((bf16[256,2,768]{2,1,0:T(2,128)(2,1)}), bf16[256,2,768]{2,1,0:T(2,128)(2,1)S(1)}, u32[]{:S(2)}, u32[]{:S(2)}) async-start(bf16[256,2,768]{2,1,0:T(2,128)(2,1)} %copy.91), calls=%async_computation.10 | async-start | bytes 1572864 | tf_op jit(solution)/shard_map/all_to_all | solution.py:344
  712.5 127.3 %copy-start.57 = (s32[16]{0:T(128)S(1)}, s32[16]{0:T(128)}, u32[]{:S(2)}) copy-start(s32[16]{0:T(128)} %param.19) | copy-start | bytes 196
  712.5 128.6 %copy-start.1 = (bf16[32,16,768]{2,1,0:T(8,128)(2,1)S(1)}, bf16[32,16,768]{2,1,0:T(8,128)(2,1)}, u32[]{:S(2)}) copy-start(bf16[32,16,768]{2,1,0:T(8,128)(2,1)} %param.17) | copy-start | bytes 2359300
  (65 other events, 595.3 us)
Sparse Core Ops, SparseCore 0:
  35.8 20.3 all-gather.30
  58.3 19.6 all-gather.28
  118.1 31.5 reduce-scatter.12
  152.0 28.0 reduce-scatter.16
  338.5 19.6 all-gather.20
  359.5 19.6 all-gather.24
  460.9 19.6 all-gather.26
  482.1 19.6 all-gather.22
  507.8 27.9 reduce-scatter.26
  538.3 27.9 reduce-scatter.22
  569.7 69.4 reduce-scatter.34
  642.4 63.8 reduce-scatter.32
  709.6 61.4 reduce-scatter.30
  774.3 62.9 reduce-scatter.28
Sparse Core Ops, SparseCore 1:
  132.2 42.8 all-gather.14
  185.4 19.5 all-gather.18
  206.9 19.5 all-gather.12
  228.7 39.5 all-gather.16
  272.6 28.2 reduce-scatter.14
  303.4 27.9 reduce-scatter.18
  394.6 27.9 reduce-scatter.20
  425.0 27.9 reduce-scatter.24

commit v2 on v1

v2 whole, which is shorter than its diff:
```python
from functools import partial

import jax
import jax.numpy as jnp
from jax import lax
from jax.sharding import PartitionSpec as P

HD = 64


EPSILON = 1e-12
MASKED = -1e30


def norm_forward(value, gain, shift):
    centred = value - jnp.mean(value, axis=-1, keepdims=True)
    inverse = lax.rsqrt(jnp.mean(centred * centred, axis=-1, keepdims=True) + EPSILON)
    normed = centred * inverse
    return (normed * gain + shift, normed, inverse)


def norm_backward(upstream, normed, inverse, gain):
    scaled = upstream * gain
    first_mean = jnp.mean(scaled, axis=-1, keepdims=True)
    second_mean = jnp.mean(scaled * normed, axis=-1, keepdims=True)
    return inverse * (scaled - first_mean - normed * second_mean)


def dot_nt(a, b):
    return lax.dot_general(a, b, (((1,), (1,)), ((), ())), preferred_element_type=jnp.float32)


def dot_tn(a, b):
    return lax.dot_general(a, b, (((0,), (0,)), ((), ())), preferred_element_type=jnp.float32)


def dot_nn(a, b):
    return jnp.dot(a, b, preferred_element_type=jnp.float32)


def on_device(
    tokens,
    lengths,
    dealing,
    project_weight,
    query_projection_bias,
    value_projection_bias,
    attention_output_weight,
    attention_output_bias,
    first_gain,
    first_shift,
    feed_input_weight,
    feed_input_bias,
    feed_output_weight,
    feed_output_bias,
    second_gain,
    second_shift,
    output_grad,
):
    n_data = lax.axis_size("dp")
    n_tensor = lax.axis_size("tensor")
    n_all = n_data * n_tensor
    data_index = lax.axis_index("dp")
    tensor_index = lax.axis_index("tensor")
    seq_total = dealing.shape[0]
    seq_here = seq_total // n_data
    assert n_tensor == 4 and seq_here == 2
    piece_rows = tokens.shape[0]
    block_rows = piece_rows * n_data
    seq_rows = block_rows * n_tensor
    half_rows = seq_rows // 2
    width = tokens.shape[2]
    head_cols = attention_output_weight.shape[1]
    heads_here = head_cols // HD
    hidden_cols = feed_input_weight.shape[1]
    project_cols = project_weight.shape[1]
    score_scale = HD ** (-0.5)

    chip_side = tensor_index // 2
    core = tensor_index % 2
    partner_slice = tensor_index ^ 2
    across_chips = [(k, k ^ 2) for k in range(n_tensor)]
    across_cores = [(k, k ^ 1) for k in range(n_tensor)]

    def to_chip_partner(value):
        return lax.ppermute(value, "tensor", across_chips)

    def to_core_partner(value):
        return lax.ppermute(value, "tensor", across_cores)

    def gather_cores(mine):
        low = mine.astype(jnp.bfloat16)
        return jnp.concatenate([low, to_core_partner(low)], axis=0)

    def scatter_cores(partial_sum):
        sent = to_core_partner(partial_sum[half_rows:].astype(jnp.bfloat16))
        return partial_sum[:half_rows] + sent.astype(jnp.float32)

    slot_ids = jnp.arange(seq_total, dtype=jnp.int32)
    placing = (dealing[None, :] == slot_ids[:, None]).astype(jnp.bfloat16)
    both = jnp.concatenate([tokens, output_grad], axis=-1)
    send_both = jnp.einsum(
        "qs,psd->pqd", placing, both, preferred_element_type=jnp.float32
    ).astype(jnp.bfloat16)
    here = lax.all_to_all(send_both, "dp", split_axis=1, concat_axis=0, tiled=True)
    slot_mine = lax.dynamic_index_in_dim(here, chip_side, axis=1, keepdims=False)
    slot_other = lax.dynamic_index_in_dim(here, 1 - chip_side, axis=1, keepdims=False)
    mine_both = jnp.concatenate([slot_mine, to_chip_partner(slot_other)], axis=0)
    inputs_mine = mine_both[:, :width]
    cot_mine = mine_both[:, width:]
    inputs_full = jnp.concatenate([inputs_mine, to_core_partner(inputs_mine)], axis=0)

    my_slot = data_index * seq_here + chip_side
    seq_length = jnp.sum(jnp.where(dealing == my_slot, lengths, 0))
    blocks = jnp.stack(
        [
            tensor_index,
            partner_slice,
            tensor_index ^ 1,
            partner_slice ^ 1,
        ]
    )
    row_ids = jnp.arange(seq_rows, dtype=jnp.int32)
    owner = blocks[row_ids // block_rows]
    inner = row_ids % block_rows
    position = (inner // piece_rows * n_tensor + owner) * piece_rows + inner % piece_rows
    key_valid = position < seq_length

    attn_w = jnp.concatenate([project_weight, attention_output_weight], axis=1)
    feed_w = jnp.concatenate([feed_input_weight, feed_output_weight], axis=1)
    attn_own = lax.all_gather(attn_w, "dp", axis=0, tiled=True)
    feed_own = lax.all_gather(feed_w, "dp", axis=0, tiled=True)
    attn_part = to_chip_partner(attn_own)
    feed_part = to_chip_partner(feed_own)
    slices = (tensor_index, partner_slice)
    attn_sets = (attn_own, attn_part)
    feed_sets = (feed_own, feed_part)
    project_ws = [a[:, :project_cols] for a in attn_sets]
    output_ws = [a[:, project_cols:] for a in attn_sets]
    up_ws = [f[:, :hidden_cols] for f in feed_sets]
    down_ws = [f[:, hidden_cols:] for f in feed_sets]

    def project_bias(k):
        query_part = lax.dynamic_slice_in_dim(query_projection_bias, k * head_cols, head_cols)
        value_part = lax.dynamic_slice_in_dim(value_projection_bias, k * head_cols, head_cols)
        return jnp.concatenate([query_part, jnp.zeros_like(query_part), value_part])

    project_biases = [project_bias(k) for k in slices]
    up_biases = [
        lax.dynamic_slice_in_dim(feed_input_bias, k * hidden_cols, hidden_cols) for k in slices
    ]

    def split_heads(qkv_block):
        query_rows = qkv_block[:, :head_cols].reshape(seq_rows, heads_here, HD)
        key_rows = qkv_block[:, head_cols : 2 * head_cols].reshape(seq_rows, heads_here, HD)
        value_rows = qkv_block[:, 2 * head_cols :].reshape(seq_rows, heads_here, HD)
        return (query_rows, key_rows, value_rows)

    def masked_scores(query_rows, key_rows):
        raw_scores = (
            jnp.einsum("qhe,khe->hqk", query_rows, key_rows, preferred_element_type=jnp.float32)
            * score_scale
        )
        return jnp.where(key_valid[None, None, :], raw_scores, MASKED)

    def attend(qkv_block):
        query_rows, key_rows, value_rows = split_heads(qkv_block)
        scores = masked_scores(query_rows, key_rows)
        row_max = jnp.max(scores, axis=-1, keepdims=True)
        exponent = jnp.exp(scores - row_max)
        row_total = jnp.sum(exponent, axis=-1, keepdims=True)
        weights = (exponent / row_total).astype(jnp.bfloat16)
        mixed_heads = jnp.einsum(
            "hqk,khe->qhe", weights, value_rows, preferred_element_type=jnp.float32
        )
        return (
            mixed_heads.reshape(seq_rows, head_cols).astype(jnp.bfloat16),
            (row_max + jnp.log(row_total))[..., 0],
        )

    def attend_back(qkv_block, row_lse, grad_block):
        query_rows, key_rows, value_rows = split_heads(qkv_block)
        weights = jnp.exp(masked_scores(query_rows, key_rows) - row_lse[..., None])
        grad_heads = grad_block.reshape(seq_rows, heads_here, HD)
        grad_weights = jnp.einsum(
            "qhe,khe->hqk", grad_heads, value_rows, preferred_element_type=jnp.float32
        )
        inner_sum = jnp.sum(weights * grad_weights, axis=-1, keepdims=True)
        grad_scores = (weights * (grad_weights - inner_sum)).astype(jnp.bfloat16)
        grad_query = (
            jnp.einsum("hqk,khe->qhe", grad_scores, key_rows, preferred_element_type=jnp.float32)
            * score_scale
        )
        grad_key = (
            jnp.einsum("hqk,qhe->khe", grad_scores, query_rows, preferred_element_type=jnp.float32)
            * score_scale
        )
        grad_value = jnp.einsum(
            "hqk,qhe->khe", weights.astype(jnp.bfloat16), grad_heads,
            preferred_element_type=jnp.float32,
        )
        joined = jnp.concatenate(
            [
                grad_query.reshape(seq_rows, head_cols),
                grad_key.reshape(seq_rows, head_cols),
                grad_value.reshape(seq_rows, head_cols),
            ],
            axis=-1,
        )
        return joined.astype(jnp.bfloat16)

    gelu_exact = partial(jax.nn.gelu, approximate=False)
    groups = range(2)

    projected = [
        (dot_nn(inputs_full, project_ws[g]) + project_biases[g]).astype(jnp.bfloat16)
        for g in groups
    ]
    attended = [attend(projected[g]) for g in groups]
    mixed = [a[0] for a in attended]
    log_total = [a[1] for a in attended]
    branch = scatter_cores(sum(dot_nt(mixed[g], output_ws[g]) for g in groups))
    first, normed_first, inverse_first = norm_forward(
        inputs_mine.astype(jnp.float32) + branch + attention_output_bias, first_gain, first_shift
    )
    first_full = gather_cores(first)
    preact = [dot_nn(first_full, up_ws[g]) + up_biases[g] for g in groups]
    gelu_pairs = [jax.vjp(gelu_exact, preact[g]) for g in groups]
    hidden = [p[0].astype(jnp.bfloat16) for p in gelu_pairs]
    feed = scatter_cores(sum(dot_nt(hidden[g], down_ws[g]) for g in groups))
    second, normed_second, inverse_second = norm_forward(
        first + feed + feed_output_bias, second_gain, second_shift
    )
    out_mine = second.astype(jnp.bfloat16)
    out_other = to_chip_partner(out_mine[block_rows:])
    out_own = out_mine[:block_rows]
    on_left = chip_side == 0
    layer_output = jnp.stack(
        [jnp.where(on_left, out_own, out_other), jnp.where(on_left, out_other, out_own)], axis=1
    )

    cot = cot_mine.astype(jnp.float32)
    second_gain_part = jnp.sum(cot * normed_second, axis=0)
    second_shift_part = jnp.sum(cot, axis=0)
    grad_second = norm_backward(cot, normed_second, inverse_second, second_gain)
    down_bias_part = jnp.sum(grad_second, axis=0)
    grad_feed_full = gather_cores(grad_second)
    grad_hidden = [dot_nn(grad_feed_full, down_ws[g]) for g in groups]
    down_grads = [dot_tn(grad_feed_full, hidden[g]) for g in groups]
    grad_preact = [gelu_pairs[g][1](grad_hidden[g])[0].astype(jnp.bfloat16) for g in groups]
    up_grads = [dot_tn(first_full, grad_preact[g]) for g in groups]
    up_bias_sums = [jnp.sum(grad_preact[g], axis=0, dtype=jnp.float32) for g in groups]
    grad_first = grad_second + scatter_cores(sum(dot_nt(grad_preact[g], up_ws[g]) for g in groups))
    first_gain_part = jnp.sum(grad_first * normed_first, axis=0)
    first_shift_part = jnp.sum(grad_first, axis=0)
    grad_residual = norm_backward(grad_first, normed_first, inverse_first, first_gain)
    output_bias_part = jnp.sum(grad_residual, axis=0)
    branch_grad_full = gather_cores(grad_residual)
    grad_mixed = [dot_nn(branch_grad_full, output_ws[g]).astype(jnp.bfloat16) for g in groups]
    output_grads = [dot_tn(branch_grad_full, mixed[g]) for g in groups]
    grad_projected = [attend_back(projected[g], log_total[g], grad_mixed[g]) for g in groups]
    project_grads = [dot_tn(inputs_full, grad_projected[g]) for g in groups]
    qkv_bias_sums = [jnp.sum(grad_projected[g], axis=0, dtype=jnp.float32) for g in groups]
    grad_inputs = grad_residual + scatter_cores(
        sum(dot_nt(grad_projected[g], project_ws[g]) for g in groups)
    )

    def reduce_weights(own_parts, partner_parts):
        own = jnp.concatenate(own_parts, axis=1)
        sent = to_chip_partner(jnp.concatenate(partner_parts, axis=1).astype(jnp.bfloat16))
        total = (own + sent.astype(jnp.float32)).astype(jnp.bfloat16)
        return lax.psum_scatter(total, "dp", scatter_dimension=0, tiled=True).astype(jnp.float32)

    feed_shard = reduce_weights([up_grads[0], down_grads[0]], [up_grads[1], down_grads[1]])
    attn_shard = reduce_weights(
        [project_grads[0], output_grads[0]], [project_grads[1], output_grads[1]]
    )
    up_shard = feed_shard[:, :hidden_cols]
    down_shard = feed_shard[:, hidden_cols:]
    project_shard = attn_shard[:, :project_cols]
    output_shard = attn_shard[:, project_cols:]

    def place(parts, part_len, total_len):
        blank = jnp.zeros((total_len,), jnp.float32)
        for g in groups:
            blank = lax.dynamic_update_slice_in_dim(blank, parts[g], slices[g] * part_len, 0)
        return blank

    vectors = (
        place([q[:head_cols] for q in qkv_bias_sums], head_cols, width),
        place([q[2 * head_cols :] for q in qkv_bias_sums], head_cols, width),
        output_bias_part,
        first_gain_part,
        first_shift_part,
        place(up_bias_sums, hidden_cols, hidden_cols * n_tensor),
        down_bias_part,
        second_gain_part,
        second_shift_part,
    )
    packed = jnp.concatenate([v.reshape(n_all, -1) for v in vectors], axis=1)
    reduced = lax.psum_scatter(packed, ("dp", "tensor"), scatter_dimension=0, tiled=True)[0]
    sizes = [v.shape[0] // n_all for v in vectors]
    offsets = [sum(sizes[:k]) for k in range(len(sizes) + 1)]
    small = [reduced[offsets[k] : offsets[k + 1]] for k in range(len(sizes))]

    grad_low = grad_inputs.astype(jnp.bfloat16)
    grad_other = to_chip_partner(grad_low[block_rows:])
    grad_own = grad_low[:block_rows]
    grad_here = jnp.stack(
        [jnp.where(on_left, grad_own, grad_other), jnp.where(on_left, grad_other, grad_own)],
        axis=1,
    )
    returned = lax.all_to_all(grad_here, "dp", split_axis=0, concat_axis=1, tiled=True)
    tokens_grad = jnp.einsum(
        "qs,pqd->psd", placing, returned, preferred_element_type=jnp.float32
    ).astype(jnp.bfloat16)

    return (
        layer_output,
        tokens_grad,
        project_shard,
        small[0],
        small[1],
        output_shard,
        small[2],
        small[3],
        small[4],
        up_shard,
        small[5],
        down_shard,
        small[6],
        small[7],
        small[8],
    )


def solution(mesh):
    in_specs = (
        P(("dp", "tensor"), None, None),
        P(),
        P(),
        P("dp", "tensor"),
        P(),
        P(),
        P("dp", "tensor"),
        P(),
        P(),
        P(),
        P("dp", "tensor"),
        P(),
        P("dp", "tensor"),
        P(),
        P(),
        P(),
        P(("dp", "tensor"), None, None),
    )
    out_specs = (
        P("tensor", "dp", None),
        P(("dp", "tensor"), None, None),
        P("dp", "tensor"),
        P(("dp", "tensor")),
        P(("dp", "tensor")),
        P("dp", "tensor"),
        P(("dp", "tensor")),
        P(("dp", "tensor")),
        P(("dp", "tensor")),
        P("dp", "tensor"),
        P(("dp", "tensor")),
        P("dp", "tensor"),
        P(("dp", "tensor")),
        P(("dp", "tensor")),
        P(("dp", "tensor")),
    )
    return jax.shard_map(
        on_device, mesh=mesh, in_specs=in_specs, out_specs=out_specs, check_vma=False
    )
```

time: 859 us -> 474 us (0.55)
  the two profiles are of different devices: /device:TPU:12 before, /device:TPU:0 now
where the time goes in v2:
time: 474 us; the launch traced here: 467 us
  waiting for transfers between devices  208 us (44%)
  matrix products  102 us (22%)
  blocking collectives  42.3 us (9%)
  other arithmetic  37.7 us (8%)
  local copies, waits for them, and re-layouts  36.3 us (8%)
  starting transfers between devices  24.6 us (5%)
  between operations  15.7 us (3%)
    ppermute x7, waiting for transfers between devices, to_chip_partner(): return lax.ppermute(value, 'tensor', across_chips)  103 us
    unnamed x1, blocking collectives  42.3 us
    unnamed x6, waiting for transfers between devices  41.4 us
    all_to_all x1, waiting for transfers between devices, on_device(): lax.all_to_all(send_both, 'dp', split_axis=1, concat_axis=0, tiled=True)  40.9 us
    dot_general x8, matrix products, dot_nn(): return jnp.dot(a, b, preferred_element_type=jnp.float32)  34.6 us
    unnamed x180, local copies, waits for them, and re-layouts  20 us
    dot_general x8, matrix products, dot_nt(): lax.dot_general(a, b, (((1,), (1,)), ((), ())), preferred_element_type=jn...  15.1 us
    dot_general x8, matrix products, dot_tn(): lax.dot_general(a, b, (((0,), (0,)), ((), ())), preferred_element_type=jn...  14.1 us
  transfers between devices with their start and end apart: 21, of which 14 were waited for; matrix products, arithmetic and copies ran while one was open for 28% of the time, Pallas kernels for 0%

profile of v2, /device:TPU:0, one launch (start us, length us, event | category | flops | bytes accessed | tf_op | source)
XLA Modules:
  0.0 466.7 jit_solution(13380619113759066026)
XLA Ops:
  11.3 7.3 %all-to-all-start = ((bf16[32,16,1536]{2,0,1:T(8,128)(2,1)}), bf16[32,16,1536]{2,0,1:T(8,128)(2,1)S(1)}, u32[]{:S(2)}, u32[]{:S(2)}) async-start(bf16[32,16,1536]{2,0,1:T(8,128)(2,1)} %copy.81), calls=%async_computation | async-start | bytes 3145728 | tf_op jit(solution)/shard_map/all_to_all | solution.py:105
  19.5 40.9 %all-to-all-done = bf16[32,16,1536]{2,0,1:T(8,128)(2,1)S(1)} async-done(((bf16[32,16,1536]{2,0,1:T(8,128)(2,1)}), bf16[32,16,1536]{2,0,1:T(8,128)(2,1)S(1)}, u32[]{:S(2)}, u32[]{:S(2)}) %all-to-all-start) | async-done | bytes 1572896 | tf_op jit(solution)/shard_map/all_to_all | solution.py:105
  62.3 11.0 %all-gather.3.cloned.1.call-done = bf16[768,768]{1,0:T(8,128)(2,1)} async-done(((bf16[96,768]{1,0:T(8,128)(2,1)}), bf16[768,768]{1,0:T(8,128)(2,1)}) %all-gather.3.cloned.1.call-update) | async-done | bytes 1179664 | tf_op jit(solution)/shard_map/all_gather | solution.py:131
  74.8 6.4 %collective-permute-done = bf16[256,1536]{1,0:T(8,128)(2,1)S(1)} collective-permute-done((bf16[256,1536]{1,0:T(8,128)(2,1)S(1)}, bf16[256,1536]{1,0:T(8,128)(2,1)S(1)}, u32[]{:S(2)}, u32[]{:S(2)}) %collective-permute-start) | collective-permute-done | bytes 786464 | tf_op jit(solution)/shard_map/ppermute | solution.py:86
  83.9 20.4 %collective-permute-done.2 = bf16[768,768]{1,0:T(8,128)(2,1)} collective-permute-done((bf16[768,768]{1,0:T(8,128)(2,1)}, bf16[768,768]{1,0:T(8,128)(2,1)}, u32[]{:S(2)}, u32[]{:S(2)}) %collective-permute-start.2) | collective-permute-done | bytes 1179680 | tf_op jit(solution)/shard_map/ppermute | solution.py:86
  107.8 2.7 add_convert_fusion.3
  114.7 2.8 copy-done
  124.2 2.8 copy-done.1
  127.0 2.7 fusion.56
  139.6 9.2 %multiply_convert_fusion.3 = (bf16[1024,768]{1,0:T(8,128)(2,1)S(1)}, f32[1024,768]{1,0:T(8,128)S(1)}, f32[1024,768]{1,0:T(8,128)S(1)}) fusion(f32[768]{0:T(1024)S(1)} %get-tuple-element.121, bf16[768,1536]{1,0:T(8,128)(2,1)} %all-gather.5.cloned.1.call-done, bf16[512,768]{1,0:T(8,128)(2,1)} %collective-permute-done.4, bf16[512,768]{1,0:T(8,128)(2,1)S(1)} %fusion.44), kind=kOutput, calls=%fused_computation.45 | convolution fusion | flops 1263009792 | bytes 10619904 | tf_op jit(solution)/shard_map/dot_general | solution.py:38
  150.2 41.0 %collective-permute-done.5 = bf16[768,1536]{1,0:T(8,128)(2,1)S(1)} collective-permute-done((bf16[768,1536]{1,0:T(8,128)(2,1)}, bf16[768,1536]{1,0:T(8,128)(2,1)S(1)}, u32[]{:S(2)}, u32[]{:S(2)}) %collective-permute-start.5) | collective-permute-done | bytes 2359328 | tf_op jit(solution)/shard_map/ppermute | solution.py:86
  191.1 8.8 %multiply_convert_fusion.2 = (bf16[1024,768]{1,0:T(8,128)(2,1)S(1)}, f32[1024,768]{1,0:T(8,128)S(1)}, f32[1024,768]{1,0:T(8,128)S(1)}) fusion(f32[768]{0:T(1024)S(1)} %get-tuple-element.120, bf16[768,1536]{1,0:T(8,128)(2,1)S(1)} %collective-permute-done.5, bf16[512,768]{1,0:T(8,128)(2,1)} %collective-permute-done.4, bf16[512,768]{1,0:T(8,128)(2,1)S(1)} %fusion.44), kind=kOutput, calls=%fused_computation.32 | convolution fusion | flops 1263009792 | bytes 10620928 | tf_op jit(solution)/shard_map/dot_general | solution.py:38
  210.9 3.8 convert_reduce_fusion.1
  216.2 3.8 convert_reduce_fusion
  228.2 3.4 convolution_convert_fusion.2
  236.8 2.8 fusion.53
  239.7 6.0 %multiply_reduce_fusion = (f32[3,1024]{1,0:T(4,128)S(1)}, f32[3,1024,1024]{1,2,0:T(8,128)}) fusion(f32[3,1024,1024]{1,2,0:T(8,128)S(1)} %bitcast.118, f32[3,1024]{1,0:T(4,128)S(1)} %log_add_fusion, bf16[1024,3,64]{0,2,1:T(8,128)(2,1)S(1)} %bitcast.145, bf16[1024,3,64]{0,2,1:T(8,128)(2,1)S(1)} %bitcast.149), kind=kOutput, calls=%fused_computation.1 | convolution fusion | flops 412087296 | bytes 25976832 | tf_op jit(solution)/shard_map/qhe,khe->hqk/dot_general | solution.py:185
  245.7 7.8 %multiply_convert_fusion = bf16[3,1024,1024]{1,2,0:T(8,128)(2,1)S(1)} fusion(f32[3,1024,1024]{1,2,0:T(8,128)} %get-tuple-element.139, f32[3,1024,1024]{1,2,0:T(8,128)S(1)} %bitcast.118, f32[3,1024]{1,0:T(4,128)S(1)} %get-tuple-element.138, f32[3,1024]{1,0:T(4,128)S(1)} %log_add_fusion), kind=kLoop, calls=%fused_computation | loop fusion | flops 12582912 | bytes 31481856 | tf_op jit(solution)/shard_map/convert_element_type | solution.py:189
  253.5 2.8 fusion.49
  260.2 2.8 multiply_reduce_fusion.1
  263.0 5.3 %multiply_convert_fusion.1 = bf16[3,1024,1024]{1,2,0:T(8,128)(2,1)} fusion(f32[3,1024,1024]{1,2,0:T(8,128)S(1)} %get-tuple-element.137, f32[3,1024,1024]{1,2,0:T(8,128)S(1)} %bitcast.116, f32[3,1024]{1,0:T(4,128)S(1)} %get-tuple-element.136, f32[3,1024]{1,0:T(4,128)S(1)} %log_add_fusion.1), kind=kLoop, calls=%fused_computation.3 | loop fusion | flops 12582912 | bytes 31481856 | tf_op jit(solution)/shard_map/convert_element_type | solution.py:189
  268.4 5.0 %fusion.47 = bf16[3,64,1024]{2,1,0:T(8,128)(2,1)S(1)} fusion(bf16[1024,3,64]{0,2,1:T(8,128)(2,1)S(1)} %bitcast.126, bf16[3,1024,1024]{1,2,0:T(8,128)(2,1)} %multiply_convert_fusion.1), kind=kOutput, calls=%fused_computation.128 | convolution fusion | flops 403046400 | bytes 7077888 | tf_op jit(solution)/shard_map/hqk,qhe->khe/dot_general | solution.py:195
  281.4 30.8 %collective-permute-done.13 = bf16[768,768]{0,1:T(8,128)(2,1)S(1)} collective-permute-done((bf16[768,768]{0,1:T(8,128)(2,1)S(1)}, bf16[768,768]{0,1:T(8,128)(2,1)S(1)}, u32[]{:S(2)}, u32[]{:S(2)}) %collective-permute-start.13) | collective-permute-done | bytes 1179680 | tf_op jit(solution)/shard_map/ppermute | solution.py:86
  314.1 3.5 fusion.110
  320.3 3.8 fusion.12
  324.1 4.5 copy.110
  328.6 3.0 fusion.78
  331.6 2.7 convolution_add_fusion
  346.4 4.7 collective-permute-done.12
  353.8 7.3 %all-to-all-start.1 = ((bf16[256,2,768]{2,1,0:T(2,128)(2,1)}), bf16[256,2,768]{2,1,0:T(2,128)(2,1)S(1)}, u32[]{:S(2)}, u32[]{:S(2)}) async-start(bf16[256,2,768]{2,1,0:T(2,128)(2,1)} %copy.91), calls=%async_computation.1 | async-start | bytes 1572864 | tf_op jit(solution)/shard_map/all_to_all | solution.py:313
  366.1 42.3 %all-reduce = f32[32,288]{1,0:T(8,128)S(1)} all-reduce(f32[32,288]{1,0:T(8,128)S(1)} %concatenate.69), channel_id=3, replica_groups=mesh['dp'=8,'tensor'=4] {'dp','tensor'}, use_global_device_ids=true, to_apply=%region_26.27.clone | all-reduce | flops 9216 | bytes 73728
  415.5 41.3 %reduce-scatter.9.cloned.1.call-done = bf16[96,1536]{1,0:T(8,128)(2,1)} async-done(((bf16[768,1536]{1,0:T(8,128)(2,1)}), bf16[96,1536]{1,0:T(8,128)(2,1)}) %reduce-scatter.9.cloned.1.call-update) | async-done | bytes 294928
  (319 shorter events, 107.7 us)
Async XLA Ops:
  11.3 49.2 %all-to-all-start = ((bf16[32,16,1536]{2,0,1:T(8,128)(2,1)}), bf16[32,16,1536]{2,0,1:T(8,128)(2,1)S(1)}, u32[]{:S(2)}, u32[]{:S(2)}) async-start(bf16[32,16,1536]{2,0,1:T(8,128)(2,1)} %copy.81), calls=%async_computation | async-start | bytes 3145728 | tf_op jit(solution)/shard_map/all_to_all | solution.py:105
  18.6 54.7 %all-gather.3.cloned.1.call-start = ((), (), s32[]{:S(2)}) async-start(), calls=%async_computation.4 | async-start | bytes 1327104 | tf_op jit(solution)/shard_map/all_gather | solution.py:131
  19.5 117.9 %all-gather.5.cloned.1.call-start = ((), (), s32[]{:S(2)}) async-start(), calls=%async_computation.5 | async-start | bytes 2654208 | tf_op jit(solution)/shard_map/all_gather | solution.py:132
  60.6 20.8 %copy-start.43 = (bf16[96,768]{1,0:T(8,128)(2,1)S(1)}, bf16[96,768]{1,0:T(8,128)(2,1)}, u32[]{:S(2)}) copy-start(bf16[96,768]{1,0:T(8,128)(2,1)} %param.29) | copy-start | bytes 442372
  60.6 20.8 %copy-start.44 = (bf16[96,768]{1,0:T(8,128)(2,1)S(1)}, bf16[96,768]{1,0:T(8,128)(2,1)}, u32[]{:S(2)}) copy-start(bf16[96,768]{1,0:T(8,128)(2,1)} %param.27) | copy-start | bytes 442372
  60.6 21.8 %copy-start.64 = (f32[768]{0:T(1024)S(1)}, f32[768]{0:T(1024)}, u32[]{:S(2)}) copy-start(f32[768]{0:T(1024)} %param.21) | copy-start | bytes 9220
  60.6 21.8 %copy-start.65 = (f32[768]{0:T(1024)S(1)}, f32[768]{0:T(1024)}, u32[]{:S(2)}) copy-start(f32[768]{0:T(1024)} %param.22) | copy-start | bytes 9220
  60.6 21.9 %copy-start.57 = (s32[16]{0:T(128)S(1)}, s32[16]{0:T(128)}, u32[]{:S(2)}) copy-start(s32[16]{0:T(128)} %param.19) | copy-start | bytes 196
  60.6 21.9 %copy-start.66 = (s32[16]{0:T(128)S(1)}, s32[16]{0:T(128)}, u32[]{:S(2)}) copy-start(s32[16]{0:T(128)} %param.18) | copy-start | bytes 196
  60.8 20.5 %collective-permute-start = (bf16[256,1536]{1,0:T(8,128)(2,1)S(1)}, bf16[256,1536]{1,0:T(8,128)(2,1)S(1)}, u32[]{:S(2)}, u32[]{:S(2)}) collective-permute-start(bf16[256,1536]{1,0:T(8,128)(2,1)S(1)} %get-tuple-element.98), channel_id=1, source_target_pairs={{0,2},{1,3},{2,0},{3,1},{4,6},{5,7},{6,4},{7,5},{8,10},{9,11},{10,... | collective-permute-start | bytes 2359304 | tf_op jit(solution)/shard_map/ppermute | solution.py:86
  73.4 31.0 %collective-permute-start.2 = (bf16[768,768]{1,0:T(8,128)(2,1)}, bf16[768,768]{1,0:T(8,128)(2,1)}, u32[]{:S(2)}, u32[]{:S(2)}) collective-permute-start(bf16[768,768]{1,0:T(8,128)(2,1)} %all-gather.3.cloned.1.call-done), channel_id=1, source_target_pairs={{0,2},{1,3},{2,0},{3,1},{4,6},{5,7},{6,4},{7,5},{8,10},{9,11},{10,... | collective-permute-start | bytes 3538952 | tf_op jit(solution)/shard_map/ppermute | solution.py:86
  81.3 26.4 %copy-start.17 = (bf16[256,1536]{1,0:T(8,128)(2,1)}, bf16[256,1536]{1,0:T(8,128)(2,1)S(1)}, u32[]{:S(2)}) copy-start(bf16[256,1536]{1,0:T(8,128)(2,1)S(1)} %collective-permute-done) | copy-start | bytes 2359300
  81.3 54.7 %copy-start.15 = (bf16[512,768]{1,0:T(8,128)(2,1)}, bf16[512,768]{1,0:T(8,128)(2,1)S(1)}, u32[]{:S(2)}) copy-start(bf16[512,768]{1,0:T(8,128)(2,1)S(1)} %fusion.81) | copy-start | bytes 2359300
  81.3 23.0 %collective-permute-start.1 = (bf16[512,768]{1,0:T(8,128)(2,1)S(1)}, bf16[512,768]{1,0:T(8,128)(2,1)S(1)}, u32[]{:S(2)}, u32[]{:S(2)}) collective-permute-start(bf16[512,768]{1,0:T(8,128)(2,1)S(1)} %fusion.81), channel_id=1, source_target_pairs={{0,1},{1,0},{2,3},{3,2},{4,5},{5,4},{6,7},{7,6},{8,9},{9,8},{10,11... | collective-permute-start | bytes 2359304 | tf_op jit(solution)/shard_map/ppermute | solution.py:89
  82.4 329.4 %reduce-scatter.7.cloned.1.call-start = ((), (), s32[]{:S(2)}) async-start(), calls=%async_computation.6 | async-start | bytes 1327104
  133.6 2.4 collective-permute-start.3
  137.1 54.1 %copy-start.32 = (bf16[512,768]{1,0:T(8,128)(2,1)}, bf16[512,768]{1,0:T(8,128)(2,1)S(1)}, u32[]{:S(2)}) copy-start(bf16[512,768]{1,0:T(8,128)(2,1)S(1)} %fusion.44) | copy-start | bytes 2359300
  137.1 2.5 collective-permute-start.4
  137.4 53.8 %collective-permute-start.5 = (bf16[768,1536]{1,0:T(8,128)(2,1)}, bf16[768,1536]{1,0:T(8,128)(2,1)S(1)}, u32[]{:S(2)}, u32[]{:S(2)}) collective-permute-start(bf16[768,1536]{1,0:T(8,128)(2,1)} %all-gather.5.cloned.1.call-done), channel_id=1, source_target_pairs={{0,2},{1,3},{2,0},{3,1},{4,6},{5,7},{6,4},{7,5},{8,10},{9,11},{10,... | collective-permute-start | bytes 7077896 | tf_op jit(solution)/shard_map/ppermute | solution.py:86
  201.5 2.4 collective-permute-start.6
  208.5 18.2 %copy-start.35 = (bf16[512,768]{1,0:T(8,128)(2,1)}, bf16[512,768]{1,0:T(8,128)(2,1)S(1)}, u32[]{:S(2)}) copy-start(bf16[512,768]{1,0:T(8,128)(2,1)S(1)} %convert_element_type.164) | copy-start | bytes 2359300
  208.5 2.4 collective-permute-start.8
  221.5 2.4 collective-permute-start.9
  226.5 8.3 %collective-permute-start.10 = (bf16[512,768]{1,0:T(8,128)(2,1)S(1)}, bf16[512,768]{1,0:T(8,128)(2,1)S(1)}, u32[]{:S(2)}, u32[]{:S(2)}) collective-permute-start(bf16[512,768]{1,0:T(8,128)(2,1)S(1)} %convert_element_type.168), channel_id=1, source_target_pairs={{0,1},{1,0},{2,3},{3,2},{4,5},{5,4},{6,7},{7,6},{8,9},{9,8},{10,11... | collective-permute-start | bytes 2359304 | tf_op jit(solution)/shard_map/ppermute | solution.py:89
  233.2 87.0 %collective-permute-start.14 = (bf16[768,1536]{0,1:T(8,128)(2,1)}, bf16[768,1536]{0,1:T(8,128)(2,1)}, u32[]{:S(2)}, u32[]{:S(2)}) collective-permute-start(bf16[768,1536]{0,1:T(8,128)(2,1)} %pad_maximum_fusion), channel_id=1, source_target_pairs={{0,2},{1,3},{2,0},{3,1},{4,6},{5,7},{6,4},{7,5},{8,10},{9,11},{10,... | collective-permute-start | bytes 7077896 | tf_op jit(solution)/shard_map/ppermute | solution.py:86
  275.1 37.1 %collective-permute-start.13 = (bf16[768,768]{0,1:T(8,128)(2,1)S(1)}, bf16[768,768]{0,1:T(8,128)(2,1)S(1)}, u32[]{:S(2)}, u32[]{:S(2)}) collective-permute-start(bf16[768,768]{0,1:T(8,128)(2,1)S(1)} %pad_maximum_fusion.7), channel_id=1, source_target_pairs={{0,2},{1,3},{2,0},{3,1},{4,6},{5,7},{6,4},{7,5},{8,10},{9,11},{10,... | collective-permute-start | bytes 3538952 | tf_op jit(solution)/shard_map/ppermute | solution.py:86
  314.0 142.7 %reduce-scatter.9.cloned.1.call-start = ((), (), s32[]{:S(2)}) async-start(), calls=%async_computation.7 | async-start | bytes 2654208
  334.4 2.4 collective-permute-start.11
  339.0 12.1 %collective-permute-start.12 = (bf16[256,768]{1,0:T(8,128)(2,1)S(1)}, bf16[256,768]{1,0:T(8,128)(2,1)S(1)}, u32[]{:S(2)}, u32[]{:S(2)}) collective-permute-start(bf16[256,768]{1,0:T(8,128)(2,1)S(1)} %slice.258), channel_id=1, source_target_pairs={{0,2},{1,3},{2,0},{3,1},{4,6},{5,7},{6,4},{7,5},{8,10},{9,11},{10,... | collective-permute-start | bytes 1179656 | tf_op jit(solution)/shard_map/ppermute | solution.py:86
  345.8 15.3 %collective-permute-start.7 = (bf16[256,768]{1,0:T(8,128)(2,1)}, bf16[256,768]{1,0:T(8,128)(2,1)}, u32[]{:S(2)}, u32[]{:S(2)}) collective-permute-start(bf16[256,768]{1,0:T(8,128)(2,1)} %slice.252), channel_id=1, source_target_pairs={{0,2},{1,3},{2,0},{3,1},{4,6},{5,7},{6,4},{7,5},{8,10},{9,11},{10,... | collective-permute-start | bytes 1179656 | tf_op jit(solution)/shard_map/ppermute | solution.py:86
  353.8 55.8 %all-to-all-start.1 = ((bf16[256,2,768]{2,1,0:T(2,128)(2,1)}), bf16[256,2,768]{2,1,0:T(2,128)(2,1)S(1)}, u32[]{:S(2)}, u32[]{:S(2)}) async-start(bf16[256,2,768]{2,1,0:T(2,128)(2,1)} %copy.91), calls=%async_computation.1 | async-start | bytes 1572864 | tf_op jit(solution)/shard_map/all_to_all | solution.py:313
  364.1 46.4 %copy-start.58 = (s32[16]{0:T(128)S(1)}, s32[16]{0:T(128)}, u32[]{:S(2)}) copy-start(s32[16]{0:T(128)} %param.19) | copy-start | bytes 196
  (74 other events, 383.3 us)
Sparse Core Ops, SparseCore 0:
  22.2 51.1 all-gather.2
  82.5 52.7 all-gather.4
  314.1 69.5 reduce-scatter.6
  387.1 69.5 reduce-scatter.8

commit v3 on v2

--- a/solution.py
+++ b/solution.py
@@ -88,6 +88,31 @@
     def to_core_partner(value):
         return lax.ppermute(value, "tensor", across_cores)
 
+    def gather_dp(block):
+        if n_data > 8:
+            return lax.all_gather(block, "dp", axis=0, tiled=True)
+        got = [block] + [
+            lax.ppermute(block, "dp", [(j, (j + k) % n_data) for j in range(n_data)])
+            for k in range(1, n_data)
+        ]
+        stacked = jnp.stack(got)
+        ordered = jnp.take(stacked, (data_index - jnp.arange(n_data)) % n_data, axis=0)
+        return ordered.reshape(n_data * block.shape[0], *block.shape[1:])
+
+    def scatter_dp(total):
+        if n_data > 8:
+            return lax.psum_scatter(
+                total.astype(jnp.bfloat16), "dp", scatter_dimension=0, tiled=True
+            ).astype(jnp.float32)
+        pieces = total.astype(jnp.bfloat16).reshape(n_data, -1, *total.shape[1:])
+        acc = lax.dynamic_index_in_dim(total.reshape(pieces.shape), data_index, 0, keepdims=False)
+        for k in range(1, n_data):
+            sent = lax.dynamic_index_in_dim(pieces, (data_index + k) % n_data, 0, keepdims=False)
+            acc = acc + lax.ppermute(
+                sent, "dp", [(j, (j + k) % n_data) for j in range(n_data)]
+            ).astype(jnp.float32)
+        return acc
+
     def gather_cores(mine):
         low = mine.astype(jnp.bfloat16)
         return jnp.concatenate([low, to_core_partner(low)], axis=0)
@@ -98,16 +123,17 @@
 
     slot_ids = jnp.arange(seq_total, dtype=jnp.int32)
     placing = (dealing[None, :] == slot_ids[:, None]).astype(jnp.bfloat16)
-    both = jnp.concatenate([tokens, output_grad], axis=-1)
-    send_both = jnp.einsum(
-        "qs,psd->pqd", placing, both, preferred_element_type=jnp.float32
-    ).astype(jnp.bfloat16)
-    here = lax.all_to_all(send_both, "dp", split_axis=1, concat_axis=0, tiled=True)
-    slot_mine = lax.dynamic_index_in_dim(here, chip_side, axis=1, keepdims=False)
-    slot_other = lax.dynamic_index_in_dim(here, 1 - chip_side, axis=1, keepdims=False)
-    mine_both = jnp.concatenate([slot_mine, to_chip_partner(slot_other)], axis=0)
-    inputs_mine = mine_both[:, :width]
-    cot_mine = mine_both[:, width:]
+    def deal(values):
+        sent = jnp.einsum(
+            "qs,psd->pqd", placing, values, preferred_element_type=jnp.float32
+        ).astype(jnp.bfloat16)
+        here = lax.all_to_all(sent, "dp", split_axis=1, concat_axis=0, tiled=True)
+        slot_mine = lax.dynamic_index_in_dim(here, chip_side, axis=1, keepdims=False)
+        slot_other = lax.dynamic_index_in_dim(here, 1 - chip_side, axis=1, keepdims=False)
+        return jnp.concatenate([slot_mine, to_chip_partner(slot_other)], axis=0)
+
+    inputs_mine = deal(tokens)
+    cot_mine = deal(output_grad)
     inputs_full = jnp.concatenate([inputs_mine, to_core_partner(inputs_mine)], axis=0)
 
     my_slot = data_index * seq_here + chip_side
@@ -128,8 +154,8 @@
 
     attn_w = jnp.concatenate([project_weight, attention_output_weight], axis=1)
     feed_w = jnp.concatenate([feed_input_weight, feed_output_weight], axis=1)
-    attn_own = lax.all_gather(attn_w, "dp", axis=0, tiled=True)
-    feed_own = lax.all_gather(feed_w, "dp", axis=0, tiled=True)
+    attn_own = gather_dp(attn_w)
+    feed_own = gather_dp(feed_w)
     attn_part = to_chip_partner(attn_own)
     feed_part = to_chip_partner(feed_own)
     slices = (tensor_index, partner_slice)
@@ -265,43 +291,81 @@
         sum(dot_nt(grad_projected[g], project_ws[g]) for g in groups)
     )
 
-    def reduce_weights(own_parts, partner_parts):
-        own = jnp.concatenate(own_parts, axis=1)
-        sent = to_chip_partner(jnp.concatenate(partner_parts, axis=1).astype(jnp.bfloat16))
-        total = (own + sent.astype(jnp.float32)).astype(jnp.bfloat16)
-        return lax.psum_scatter(total, "dp", scatter_dimension=0, tiled=True).astype(jnp.float32)
-
-    feed_shard = reduce_weights([up_grads[0], down_grads[0]], [up_grads[1], down_grads[1]])
-    attn_shard = reduce_weights(
-        [project_grads[0], output_grads[0]], [project_grads[1], output_grads[1]]
-    )
-    up_shard = feed_shard[:, :hidden_cols]
-    down_shard = feed_shard[:, hidden_cols:]
-    project_shard = attn_shard[:, :project_cols]
-    output_shard = attn_shard[:, project_cols:]
-
     def place(parts, part_len, total_len):
         blank = jnp.zeros((total_len,), jnp.float32)
         for g in groups:
             blank = lax.dynamic_update_slice_in_dim(blank, parts[g], slices[g] * part_len, 0)
         return blank
 
-    vectors = (
-        place([q[:head_cols] for q in qkv_bias_sums], head_cols, width),
-        place([q[2 * head_cols :] for q in qkv_bias_sums], head_cols, width),
-        output_bias_part,
-        first_gain_part,
-        first_shift_part,
-        place(up_bias_sums, hidden_cols, hidden_cols * n_tensor),
-        down_bias_part,
-        second_gain_part,
-        second_shift_part,
-    )
-    packed = jnp.concatenate([v.reshape(n_all, -1) for v in vectors], axis=1)
-    reduced = lax.psum_scatter(packed, ("dp", "tensor"), scatter_dimension=0, tiled=True)[0]
-    sizes = [v.shape[0] // n_all for v in vectors]
-    offsets = [sum(sizes[:k]) for k in range(len(sizes) + 1)]
-    small = [reduced[offsets[k] : offsets[k + 1]] for k in range(len(sizes))]
+    rows_block = width // n_data
+    vec_block = width // n_all
+
+    def reduce_weights(own_parts, partner_parts, extra=None):
+        own = jnp.concatenate(own_parts, axis=1)
+        partner = jnp.concatenate(partner_parts, axis=1)
+        if extra is not None:
+            extra = extra + to_core_partner(extra)
+            own = jnp.concatenate([own, extra], axis=1)
+            partner = jnp.concatenate([partner, extra], axis=1)
+        sent = to_chip_partner(partner.astype(jnp.bfloat16))
+        return scatter_dp(own + sent.astype(jnp.float32))
+
+    feed_shard = reduce_weights([up_grads[0], down_grads[0]], [up_grads[1], down_grads[1]])
+    up_placed = place(up_bias_sums, hidden_cols, hidden_cols * n_tensor)
+    up_columns = (
+        up_placed.reshape(n_data, n_tensor, rows_block).transpose(0, 2, 1).reshape(width, n_tensor)
+    )
+    early_columns = jnp.concatenate(
+        [
+            jnp.stack(
+                [
+                    output_bias_part,
+                    first_gain_part,
+                    first_shift_part,
+                    down_bias_part,
+                    second_gain_part,
+                    second_shift_part,
+                ],
+                axis=1,
+            ),
+            up_columns,
+        ],
+        axis=1,
+    )
+    output_shard_ext = reduce_weights([output_grads[0]], [output_grads[1]], early_columns)
+    late_columns = jnp.stack(
+        [
+            place([q[:head_cols] for q in qkv_bias_sums], head_cols, width),
+            place([q[2 * head_cols :] for q in qkv_bias_sums], head_cols, width),
+        ],
+        axis=1,
+    )
+    project_shard_ext = reduce_weights([project_grads[0]], [project_grads[1]], late_columns)
+    up_shard = feed_shard[:, :hidden_cols]
+    down_shard = feed_shard[:, hidden_cols:]
+    head_out = output_shard_ext.shape[1] - early_columns.shape[1]
+    output_shard = output_shard_ext[:, :head_out]
+    project_shard = project_shard_ext[:, :project_cols]
+
+    def mine_of(column):
+        return lax.dynamic_slice_in_dim(column, tensor_index * vec_block, vec_block)
+
+    early = [mine_of(output_shard_ext[:, head_out + k]) for k in range(6)]
+    up_bias_shard = lax.dynamic_index_in_dim(
+        output_shard_ext[:, head_out + 6 :], tensor_index, axis=1, keepdims=False
+    )
+    late = [mine_of(project_shard_ext[:, project_cols + k]) for k in range(2)]
+    small = [
+        late[0],
+        late[1],
+        early[0],
+        early[1],
+        early[2],
+        up_bias_shard,
+        early[3],
+        early[4],
+        early[5],
+    ]
 
     grad_low = grad_inputs.astype(jnp.bfloat16)
     grad_other = to_chip_partner(grad_low[block_rows:])

time: 474 us -> 505 us (1.065)
  the two profiles are of different devices: /device:TPU:0 before, /device:TPU:12 now
where the time goes in v3:
time: 505 us; the launch traced here: 496 us
  waiting for transfers between devices  177 us (35%)
  matrix products  120 us (24%)
  local copies, waits for them, and re-layouts  75.4 us (15%)
  starting transfers between devices  69.9 us (14%)
  other arithmetic  51.6 us (10%)
    ppermute x9, waiting for transfers between devices, to_chip_partner(): return lax.ppermute(value, 'tensor', across_chips)  62.2 us
    ppermute x14, waiting for transfers between devices, gather_dp(): lax.ppermute(block, 'dp', [(j, (j + k) % n_data) for j in range(n_data)])  58.2 us
    ppermute x21, waiting for transfers between devices, scatter_dp(): lax.ppermute(sent, 'dp', [(j, (j + k) % n_data) for j in range(n_data)])  55.1 us
    dot_general x8, matrix products, dot_nn(): return jnp.dot(a, b, preferred_element_type=jnp.float32)  40.6 us
    unnamed x231, local copies, waits for them, and re-layouts  28.6 us
    ppermute x21, starting transfers between devices, scatter_dp(): lax.ppermute(sent, 'dp', [(j, (j + k) % n_data) for j in range(n_data)])  24 us
    dot_general x8, matrix products, dot_tn(): lax.dot_general(a, b, (((0,), (0,)), ((), ())), preferred_element_type=jn...  21.3 us
    dot_general x8, matrix products, dot_nt(): lax.dot_general(a, b, (((1,), (1,)), ((), ())), preferred_element_type=jn...  18.8 us
  transfers between devices with their start and end apart: 57, of which 20 were waited for; matrix products, arithmetic and copies ran while one was open for 42% of the time, Pallas kernels for 0%

profile of v3, /device:TPU:12, one launch (start us, length us, event | category | flops | bytes accessed | tf_op | source)
XLA Modules:
  0.0 496.2 jit_solution(7278268905295535653)
XLA Ops:
  11.4 6.1 %all-to-all-start = ((bf16[32,16,768]{2,0,1:T(8,128)(2,1)}), bf16[32,16,768]{2,0,1:T(8,128)(2,1)S(1)}, u32[]{:S(2)}, u32[]{:S(2)}) async-start(bf16[32,16,768]{2,0,1:T(8,128)(2,1)} %copy.145), calls=%async_computation | async-start | bytes 1572864 | tf_op jit(solution)/shard_map/all_to_all | solution.py:130
  24.0 6.5 %collective-permute-done.4 = bf16[96,768]{1,0:T(8,128)(2,1)S(1)} collective-permute-done((bf16[96,768]{1,0:T(8,128)(2,1)S(1)}, bf16[96,768]{1,0:T(8,128)(2,1)S(1)}, u32[]{:S(2)}, u32[]{:S(2)}) %collective-permute-start.4) | collective-permute-done | bytes 147488 | tf_op jit(solution)/shard_map/ppermute | solution.py:95
  30.5 7.6 %collective-permute-done.5 = bf16[96,768]{1,0:T(8,128)(2,1)S(1)} collective-permute-done((bf16[96,768]{1,0:T(8,128)(2,1)S(1)}, bf16[96,768]{1,0:T(8,128)(2,1)S(1)}, u32[]{:S(2)}, u32[]{:S(2)}) %collective-permute-start.5) | collective-permute-done | bytes 147488 | tf_op jit(solution)/shard_map/ppermute | solution.py:95
  39.4 27.0 %collective-permute-done.7 = bf16[96,768]{1,0:T(8,128)(2,1)S(1)} collective-permute-done((bf16[96,768]{1,0:T(8,128)(2,1)S(1)}, bf16[96,768]{1,0:T(8,128)(2,1)S(1)}, u32[]{:S(2)}, u32[]{:S(2)}) %collective-permute-start.7) | collective-permute-done | bytes 147488 | tf_op jit(solution)/shard_map/ppermute | solution.py:95
  74.4 16.5 %collective-permute-done.14 = bf16[96,1536]{1,0:T(8,128)(2,1)} collective-permute-done((bf16[96,1536]{1,0:T(8,128)(2,1)}, bf16[96,1536]{1,0:T(8,128)(2,1)}, u32[]{:S(2)}, u32[]{:S(2)}) %collective-permute-start.14) | collective-permute-done | bytes 294944 | tf_op jit(solution)/shard_map/ppermute | solution.py:95
  94.1 13.0 %collective-permute-done = bf16[256,768]{1,0:T(8,128)(2,1)S(1)} collective-permute-done((bf16[256,768]{1,0:T(8,128)(2,1)S(1)}, bf16[256,768]{1,0:T(8,128)(2,1)S(1)}, u32[]{:S(2)}, u32[]{:S(2)}) %collective-permute-start) | collective-permute-done | bytes 393248 | tf_op jit(solution)/shard_map/ppermute | solution.py:86
  145.0 3.9 gather_fusion.1
  157.7 5.6 %all-to-all-start.1 = ((bf16[32,16,768]{2,0,1:T(8,128)(2,1)}), bf16[32,16,768]{2,0,1:T(8,128)(2,1)S(1)}, u32[]{:S(2)}, u32[]{:S(2)}) async-start(bf16[32,16,768]{2,0,1:T(8,128)(2,1)} %copy.150), calls=%async_computation.1 | async-start | bytes 1572864 | tf_op jit(solution)/shard_map/all_to_all | solution.py:130
  163.4 11.2 %multiply_convert_fusion.3 = (bf16[1024,768]{1,0:T(8,128)(2,1)S(1)}, f32[1024,768]{1,0:T(8,128)}, f32[1024,768]{1,0:T(8,128)}) fusion(f32[768]{0:T(1024)S(1)} %get-tuple-element.170, bf16[768,1536]{1,0:T(8,128)(2,1)} %bitcast_select_fusion, bf16[512,768]{1,0:T(8,128)(2,1)} %collective-permute-done.11, bf16[512,768]{1,0:T(8,128)(2,1)} %fusion.38), kind=kOutput, calls=%fused_computation.46 | convolution fusion | flops 1263009792 | bytes 10619904 | tf_op jit(solution)/shard_map/dot_general | solution.py:38
  174.7 33.8 %collective-permute-done.19 = bf16[768,1536]{1,0:T(8,128)(2,1)} collective-permute-done((bf16[768,1536]{1,0:T(8,128)(2,1)}, bf16[768,1536]{1,0:T(8,128)(2,1)}, u32[]{:S(2)}, u32[]{:S(2)}) %collective-permute-start.19) | collective-permute-done | bytes 2359328 | tf_op jit(solution)/shard_map/ppermute | solution.py:86
  208.5 11.6 %multiply_convert_fusion.2 = (bf16[1024,768]{1,0:T(8,128)(2,1)S(1)}, f32[1024,768]{1,0:T(8,128)}, f32[1024,768]{1,0:T(8,128)}) fusion(f32[768]{0:T(1024)S(1)} %get-tuple-element.169, bf16[768,1536]{1,0:T(8,128)(2,1)} %collective-permute-done.19, bf16[512,768]{1,0:T(8,128)(2,1)} %collective-permute-done.11, bf16[512,768]{1,0:T(8,128)(2,1)} %fusion.38), kind=kOutput, calls=%fused_computation.33 | convolution fusion | flops 1263009792 | bytes 10619904 | tf_op jit(solution)/shard_map/dot_general | solution.py:38
  233.6 6.9 %collective-permute-done.22 = bf16[256,768]{1,0:T(8,128)(2,1)S(1)} collective-permute-done((bf16[256,768]{1,0:T(8,128)(2,1)S(1)}, bf16[256,768]{1,0:T(8,128)(2,1)S(1)}, u32[]{:S(2)}, u32[]{:S(2)}) %collective-permute-start.22) | collective-permute-done | bytes 393248 | tf_op jit(solution)/shard_map/ppermute | solution.py:86
  246.2 7.7 %collective-permute-done.21 = bf16[256,768]{1,0:T(8,128)(2,1)S(1)} collective-permute-done((bf16[256,768]{1,0:T(8,128)(2,1)S(1)}, bf16[256,768]{1,0:T(8,128)(2,1)S(1)}, u32[]{:S(2)}, u32[]{:S(2)}) %collective-permute-start.21) | collective-permute-done | bytes 393248 | tf_op jit(solution)/shard_map/ppermute | solution.py:86
  255.7 4.7 convert_reduce_fusion.1
  264.2 4.6 convert_reduce_fusion
  286.5 4.2 fusion.129
  291.0 4.5 fusion.128
  298.2 6.1 %multiply_reduce_fusion.1 = (f32[3,1024]{1,0:T(4,128)S(1)}, f32[3,1024,1024]{1,2,0:T(8,128)S(1)}) fusion(f32[3,1024,1024]{1,2,0:T(8,128)} %copy-done.3, f32[3,1024]{1,0:T(4,128)S(1)} %copy-done.39, bf16[1024,3,64]{0,2,1:T(8,128)(2,1)S(1)} %bitcast.272, bf16[1024,3,64]{0,2,1:T(8,128)(2,1)S(1)} %bitcast.279), kind=kOutput, calls=%fused_computation.6 | convolution fusion | flops 412087296 | bytes 25976832 | tf_op jit(solution)/shard_map/qhe,khe->hqk/dot_general | solution.py:211
  306.5 5.7 %multiply_convert_fusion.1 = bf16[3,1024,1024]{1,2,0:T(8,128)(2,1)} fusion(f32[3,1024,1024]{1,2,0:T(8,128)S(1)} %get-tuple-element.188, f32[3,1024,1024]{1,2,0:T(8,128)S(1)} %bitcast.244, f32[3,1024]{1,0:T(4,128)S(1)} %get-tuple-element.187, f32[3,1024]{1,0:T(4,128)S(1)} %copy-done.39), kind=kLoop, calls=%fused_computation.5 | loop fusion | flops 12582912 | bytes 31481856 | tf_op jit(solution)/shard_map/convert_element_type | solution.py:215
  312.1 4.9 fusion.42
  327.4 5.3 %multiply_convert_fusion = bf16[3,1024,1024]{1,2,0:T(8,128)(2,1)} fusion(f32[3,1024,1024]{1,2,0:T(8,128)S(1)} %get-tuple-element.190, f32[3,1024,1024]{1,2,0:T(8,128)S(1)} %bitcast.242, f32[3,1024]{1,0:T(4,128)S(1)} %get-tuple-element.189, f32[3,1024]{1,0:T(4,128)S(1)} %log_add_fusion), kind=kLoop, calls=%fused_computation.2 | loop fusion | flops 12582912 | bytes 31481856 | tf_op jit(solution)/shard_map/convert_element_type | solution.py:215
  332.7 4.1 fusion.44
  363.9 3.6 collective-permute-start.41
  379.2 5.8 %fusion.131 = (bf16[768,1536]{0,1:T(8,128)(2,1)S(1)}, f32[768,1536]{0,1:T(8,128)}) fusion(bf16[768,1536]{0,1:T(8,128)(2,1)} %collective-permute-done.46, f32[768,768]{0,1:T(8,128)} %fusion.128, f32[768,768]{0,1:T(8,128)} %fusion.129), kind=kLoop, calls=%fused_computation.319 | loop fusion | flops 4718592 | bytes 14155776 | tf_op jit(solution)/shard_map/convert_element_type | solution.py:107
  413.1 7.3 %all-to-all-start.2 = ((bf16[256,2,768]{2,1,0:T(2,128)(2,1)}), bf16[256,2,768]{2,1,0:T(2,128)(2,1)S(1)}, u32[]{:S(2)}, u32[]{:S(2)}) async-start(bf16[256,2,768]{2,1,0:T(2,128)(2,1)} %copy.158), calls=%async_computation.2 | async-start | bytes 1572864 | tf_op jit(solution)/shard_map/all_to_all | solution.py:377
  420.5 6.7 %collective-permute-done.32 = bf16[96,578]{1,0:T(8,128)(2,1)} collective-permute-done((bf16[96,578]{1,0:T(8,128)(2,1)}, bf16[96,578]{1,0:T(8,128)(2,1)}, u32[]{:S(2)}, u32[]{:S(2)}) %collective-permute-start.32) | collective-permute-done | bytes 111008 | tf_op jit(solution)/shard_map/ppermute | solution.py:111
  427.2 8.4 %collective-permute-done.33 = bf16[96,578]{1,0:T(8,128)(2,1)} collective-permute-done((bf16[96,578]{1,0:T(8,128)(2,1)}, bf16[96,578]{1,0:T(8,128)(2,1)}, u32[]{:S(2)}, u32[]{:S(2)}) %collective-permute-start.33) | collective-permute-done | bytes 111008 | tf_op jit(solution)/shard_map/ppermute | solution.py:111
  440.3 6.1 %copy.171 = f32[768,1536]{1,0:T(8,128)} copy(f32[768,1536]{0,1:T(8,128)} %get-tuple-element.99) | data formatting | bytes 9437184 | tf_op jit(solution)/shard_map/add | solution.py:311
  451.6 12.8 %collective-permute-done.36 = bf16[96,578]{1,0:T(8,128)(2,1)} collective-permute-done((bf16[96,578]{1,0:T(8,128)(2,1)}, bf16[96,578]{1,0:T(8,128)(2,1)}, u32[]{:S(2)}, u32[]{:S(2)}) %collective-permute-start.36) | collective-permute-done | bytes 111008 | tf_op jit(solution)/shard_map/ppermute | solution.py:111
  467.2 6.7 %collective-permute-done.49 = bf16[96,1536]{1,0:T(8,128)(2,1)S(1)} collective-permute-done((bf16[96,1536]{1,0:T(8,128)(2,1)}, bf16[96,1536]{1,0:T(8,128)(2,1)S(1)}, u32[]{:S(2)}, u32[]{:S(2)}) %collective-permute-start.49) | collective-permute-done | bytes 294944 | tf_op jit(solution)/shard_map/ppermute | solution.py:111
  473.9 6.1 %collective-permute-done.50 = bf16[96,1536]{1,0:T(8,128)(2,1)S(1)} collective-permute-done((bf16[96,1536]{1,0:T(8,128)(2,1)}, bf16[96,1536]{1,0:T(8,128)(2,1)S(1)}, u32[]{:S(2)}, u32[]{:S(2)}) %collective-permute-start.50) | collective-permute-done | bytes 294944 | tf_op jit(solution)/shard_map/ppermute | solution.py:111
  482.2 9.3 %collective-permute-done.53 = bf16[96,1536]{1,0:T(8,128)(2,1)S(1)} collective-permute-done((bf16[96,1536]{1,0:T(8,128)(2,1)S(1)}, bf16[96,1536]{1,0:T(8,128)(2,1)S(1)}, u32[]{:S(2)}, u32[]{:S(2)}) %collective-permute-start.53) | collective-permute-done | bytes 294944 | tf_op jit(solution)/shard_map/ppermute | solution.py:111
  (488 shorter events, 219.1 us)
Async XLA Ops:
  1.8 21.1 %collective-permute-start.2 = (bf16[96,768]{1,0:T(8,128)(2,1)S(1)}, bf16[96,768]{1,0:T(8,128)(2,1)S(1)}, u32[]{:S(2)}, u32[]{:S(2)}) collective-permute-start(bf16[96,768]{1,0:T(8,128)(2,1)S(1)} %get-tuple-element.122), channel_id=1, source_target_pairs={{0,4},{4,8},{8,12},{12,16},{16,20},{20,24},{24,28},{28,0},{1,5},{5... | collective-permute-start | bytes 442376 | tf_op jit(solution)/shard_map/ppermute | solution.py:95
  3.4 20.7 %collective-permute-start.3 = (bf16[96,768]{1,0:T(8,128)(2,1)S(1)}, bf16[96,768]{1,0:T(8,128)(2,1)S(1)}, u32[]{:S(2)}, u32[]{:S(2)}) collective-permute-start(bf16[96,768]{1,0:T(8,128)(2,1)S(1)} %get-tuple-element.122), channel_id=1, source_target_pairs={{0,8},{4,12},{8,16},{12,20},{16,24},{20,28},{24,0},{28,4},{1,9},{5... | collective-permute-start | bytes 442376 | tf_op jit(solution)/shard_map/ppermute | solution.py:95
  4.9 25.6 %collective-permute-start.4 = (bf16[96,768]{1,0:T(8,128)(2,1)S(1)}, bf16[96,768]{1,0:T(8,128)(2,1)S(1)}, u32[]{:S(2)}, u32[]{:S(2)}) collective-permute-start(bf16[96,768]{1,0:T(8,128)(2,1)S(1)} %get-tuple-element.122), channel_id=1, source_target_pairs={{0,12},{4,16},{8,20},{12,24},{16,28},{20,0},{24,4},{28,8},{1,13},{... | collective-permute-start | bytes 442376 | tf_op jit(solution)/shard_map/ppermute | solution.py:95
  6.1 32.0 %collective-permute-start.5 = (bf16[96,768]{1,0:T(8,128)(2,1)S(1)}, bf16[96,768]{1,0:T(8,128)(2,1)S(1)}, u32[]{:S(2)}, u32[]{:S(2)}) collective-permute-start(bf16[96,768]{1,0:T(8,128)(2,1)S(1)} %get-tuple-element.122), channel_id=1, source_target_pairs={{0,16},{4,20},{8,24},{12,28},{16,0},{20,4},{24,8},{28,12},{1,17},{... | collective-permute-start | bytes 442376 | tf_op jit(solution)/shard_map/ppermute | solution.py:95
  7.8 31.1 %collective-permute-start.6 = (bf16[96,768]{1,0:T(8,128)(2,1)S(1)}, bf16[96,768]{1,0:T(8,128)(2,1)S(1)}, u32[]{:S(2)}, u32[]{:S(2)}) collective-permute-start(bf16[96,768]{1,0:T(8,128)(2,1)S(1)} %get-tuple-element.122), channel_id=1, source_target_pairs={{0,20},{4,24},{8,28},{12,0},{16,4},{20,8},{24,12},{28,16},{1,21},{... | collective-permute-start | bytes 442376 | tf_op jit(solution)/shard_map/ppermute | solution.py:95
  11.4 62.9 %all-to-all-start = ((bf16[32,16,768]{2,0,1:T(8,128)(2,1)}), bf16[32,16,768]{2,0,1:T(8,128)(2,1)S(1)}, u32[]{:S(2)}, u32[]{:S(2)}) async-start(bf16[32,16,768]{2,0,1:T(8,128)(2,1)} %copy.145), calls=%async_computation | async-start | bytes 1572864 | tf_op jit(solution)/shard_map/all_to_all | solution.py:130
  22.8 43.6 %collective-permute-start.7 = (bf16[96,768]{1,0:T(8,128)(2,1)S(1)}, bf16[96,768]{1,0:T(8,128)(2,1)S(1)}, u32[]{:S(2)}, u32[]{:S(2)}) collective-permute-start(bf16[96,768]{1,0:T(8,128)(2,1)S(1)} %get-tuple-element.122), channel_id=1, source_target_pairs={{0,24},{4,28},{8,0},{12,4},{16,8},{20,12},{24,16},{28,20},{1,25},{... | collective-permute-start | bytes 442376 | tf_op jit(solution)/shard_map/ppermute | solution.py:95
  24.0 42.4 %collective-permute-start.8 = (bf16[96,768]{1,0:T(8,128)(2,1)S(1)}, bf16[96,768]{1,0:T(8,128)(2,1)S(1)}, u32[]{:S(2)}, u32[]{:S(2)}) collective-permute-start(bf16[96,768]{1,0:T(8,128)(2,1)S(1)} %get-tuple-element.122), channel_id=1, source_target_pairs={{0,28},{4,0},{8,4},{12,8},{16,12},{20,16},{24,20},{28,24},{1,29},{... | collective-permute-start | bytes 442376 | tf_op jit(solution)/shard_map/ppermute | solution.py:95
  30.5 38.0 %collective-permute-start.12 = (bf16[96,1536]{1,0:T(8,128)(2,1)}, bf16[96,1536]{1,0:T(8,128)(2,1)}, u32[]{:S(2)}, u32[]{:S(2)}) collective-permute-start(bf16[96,1536]{1,0:T(8,128)(2,1)} %constant_dynamic-update-slice_fusion), channel_id=1, source_target_pairs={{0,4},{4,8},{8,12},{12,16},{16,20},{20,24},{24,28},{28,0},{1,5},{5... | collective-permute-start | bytes 884744 | tf_op jit(solution)/shard_map/ppermute | solution.py:95
  38.1 33.0 %collective-permute-start.13 = (bf16[96,1536]{1,0:T(8,128)(2,1)}, bf16[96,1536]{1,0:T(8,128)(2,1)}, u32[]{:S(2)}, u32[]{:S(2)}) collective-permute-start(bf16[96,1536]{1,0:T(8,128)(2,1)} %constant_dynamic-update-slice_fusion), channel_id=1, source_target_pairs={{0,8},{4,12},{8,16},{12,20},{16,24},{20,28},{24,0},{28,4},{1,9},{5... | collective-permute-start | bytes 884744 | tf_op jit(solution)/shard_map/ppermute | solution.py:95
  38.9 52.0 %collective-permute-start.14 = (bf16[96,1536]{1,0:T(8,128)(2,1)}, bf16[96,1536]{1,0:T(8,128)(2,1)}, u32[]{:S(2)}, u32[]{:S(2)}) collective-permute-start(bf16[96,1536]{1,0:T(8,128)(2,1)} %constant_dynamic-update-slice_fusion), channel_id=1, source_target_pairs={{0,12},{4,16},{8,20},{12,24},{16,28},{20,0},{24,4},{28,8},{1,13},{... | collective-permute-start | bytes 884744 | tf_op jit(solution)/shard_map/ppermute | solution.py:95
  66.4 44.0 %collective-permute-start.15 = (bf16[96,1536]{1,0:T(8,128)(2,1)}, bf16[96,1536]{1,0:T(8,128)(2,1)S(1)}, u32[]{:S(2)}, u32[]{:S(2)}) collective-permute-start(bf16[96,1536]{1,0:T(8,128)(2,1)} %constant_dynamic-update-slice_fusion), channel_id=1, source_target_pairs={{0,16},{4,20},{8,24},{12,28},{16,0},{20,4},{24,8},{28,12},{1,17},{... | collective-permute-start | bytes 884744 | tf_op jit(solution)/shard_map/ppermute | solution.py:95
  66.4 44.8 %collective-permute-start.16 = (bf16[96,1536]{1,0:T(8,128)(2,1)}, bf16[96,1536]{1,0:T(8,128)(2,1)}, u32[]{:S(2)}, u32[]{:S(2)}) collective-permute-start(bf16[96,1536]{1,0:T(8,128)(2,1)} %constant_dynamic-update-slice_fusion), channel_id=1, source_target_pairs={{0,20},{4,24},{8,28},{12,0},{16,4},{20,8},{24,12},{28,16},{1,21},{... | collective-permute-start | bytes 884744 | tf_op jit(solution)/shard_map/ppermute | solution.py:95
  68.5 73.1 %collective-permute-start.17 = (bf16[96,1536]{1,0:T(8,128)(2,1)}, bf16[96,1536]{1,0:T(8,128)(2,1)}, u32[]{:S(2)}, u32[]{:S(2)}) collective-permute-start(bf16[96,1536]{1,0:T(8,128)(2,1)} %constant_dynamic-update-slice_fusion), channel_id=1, source_target_pairs={{0,24},{4,28},{8,0},{12,4},{16,8},{20,12},{24,16},{28,20},{1,25},{... | collective-permute-start | bytes 884744 | tf_op jit(solution)/shard_map/ppermute | solution.py:95
  71.2 41.8 %collective-permute-start.9 = (bf16[768,768]{1,0:T(8,128)(2,1)}, bf16[768,768]{1,0:T(8,128)(2,1)S(1)}, u32[]{:S(2)}, u32[]{:S(2)}) collective-permute-start(bf16[768,768]{1,0:T(8,128)(2,1)} %bitcast_select_fusion.1), channel_id=1, source_target_pairs={{0,2},{1,3},{2,0},{3,1},{4,6},{5,7},{6,4},{7,5},{8,10},{9,11},{10,... | collective-permute-start | bytes 3538952 | tf_op jit(solution)/shard_map/ppermute | solution.py:86
  107.0 36.2 %collective-permute-start.18 = (bf16[96,1536]{1,0:T(8,128)(2,1)}, bf16[96,1536]{1,0:T(8,128)(2,1)}, u32[]{:S(2)}, u32[]{:S(2)}) collective-permute-start(bf16[96,1536]{1,0:T(8,128)(2,1)} %constant_dynamic-update-slice_fusion), channel_id=1, source_target_pairs={{0,28},{4,0},{8,4},{12,8},{16,12},{20,16},{24,20},{28,24},{1,29},{... | collective-permute-start | bytes 884744 | tf_op jit(solution)/shard_map/ppermute | solution.py:95
  154.6 53.9 %collective-permute-start.19 = (bf16[768,1536]{1,0:T(8,128)(2,1)}, bf16[768,1536]{1,0:T(8,128)(2,1)}, u32[]{:S(2)}, u32[]{:S(2)}) collective-permute-start(bf16[768,1536]{1,0:T(8,128)(2,1)} %bitcast_select_fusion), channel_id=1, source_target_pairs={{0,2},{1,3},{2,0},{3,1},{4,6},{5,7},{6,4},{7,5},{8,10},{9,11},{10,... | collective-permute-start | bytes 7077896 | tf_op jit(solution)/shard_map/ppermute | solution.py:86
  157.7 71.1 %all-to-all-start.1 = ((bf16[32,16,768]{2,0,1:T(8,128)(2,1)}), bf16[32,16,768]{2,0,1:T(8,128)(2,1)S(1)}, u32[]{:S(2)}, u32[]{:S(2)}) async-start(bf16[32,16,768]{2,0,1:T(8,128)(2,1)} %copy.150), calls=%async_computation.1 | async-start | bytes 1572864 | tf_op jit(solution)/shard_map/all_to_all | solution.py:130
  278.8 100.4 %collective-permute-start.46 = (bf16[768,1536]{0,1:T(8,128)(2,1)}, bf16[768,1536]{0,1:T(8,128)(2,1)}, u32[]{:S(2)}, u32[]{:S(2)}) collective-permute-start(bf16[768,1536]{0,1:T(8,128)(2,1)} %pad_maximum_fusion), channel_id=1, source_target_pairs={{0,2},{1,3},{2,0},{3,1},{4,6},{5,7},{6,4},{7,5},{8,10},{9,11},{10,... | collective-permute-start | bytes 7077896 | tf_op jit(solution)/shard_map/ppermute | solution.py:86
  374.1 18.8 %collective-permute-start.26 = (bf16[512,768]{1,0:T(8,128)(2,1)}, bf16[512,768]{1,0:T(8,128)(2,1)}, u32[]{:S(2)}, u32[]{:S(2)}) collective-permute-start(bf16[512,768]{1,0:T(8,128)(2,1)} %slice.292), channel_id=1, source_target_pairs={{0,1},{1,0},{2,3},{3,2},{4,5},{5,4},{6,7},{7,6},{8,9},{9,8},{10,11... | collective-permute-start | bytes 2359304 | tf_op jit(solution)/shard_map/ppermute | solution.py:89
  376.6 20.7 %collective-permute-start.29 = (bf16[768,578]{0,1:T(8,128)(2,1)}, bf16[768,578]{0,1:T(8,128)(2,1)}, u32[]{:S(2)}, u32[]{:S(2)}) collective-permute-start(bf16[768,578]{0,1:T(8,128)(2,1)} %pad_maximum_fusion.7), channel_id=1, source_target_pairs={{0,2},{1,3},{2,0},{3,1},{4,6},{5,7},{6,4},{7,5},{8,10},{9,11},{10,... | collective-permute-start | bytes 2663432 | tf_op jit(solution)/shard_map/ppermute | solution.py:86
  390.4 74.0 %collective-permute-start.47 = (bf16[96,1536]{1,0:T(8,128)(2,1)}, bf16[96,1536]{1,0:T(8,128)(2,1)}, u32[]{:S(2)}, u32[]{:S(2)}) collective-permute-start(bf16[96,1536]{1,0:T(8,128)(2,1)} %get-tuple-element.123), channel_id=1, source_target_pairs={{0,4},{4,8},{8,12},{12,16},{16,20},{20,24},{24,28},{28,0},{1,5},{5... | collective-permute-start | bytes 884744 | tf_op jit(solution)/shard_map/ppermute | solution.py:111
  391.2 73.1 %collective-permute-start.48 = (bf16[96,1536]{1,0:T(8,128)(2,1)}, bf16[96,1536]{1,0:T(8,128)(2,1)}, u32[]{:S(2)}, u32[]{:S(2)}) collective-permute-start(bf16[96,1536]{1,0:T(8,128)(2,1)} %get-tuple-element.129), channel_id=1, source_target_pairs={{0,8},{4,12},{8,16},{12,20},{16,24},{20,28},{24,0},{28,4},{1,9},{5... | collective-permute-start | bytes 884744 | tf_op jit(solution)/shard_map/ppermute | solution.py:111
  406.0 21.2 %collective-permute-start.32 = (bf16[96,578]{1,0:T(8,128)(2,1)}, bf16[96,578]{1,0:T(8,128)(2,1)}, u32[]{:S(2)}, u32[]{:S(2)}) collective-permute-start(bf16[96,578]{1,0:T(8,128)(2,1)} %get-tuple-element.146), channel_id=1, source_target_pairs={{0,12},{4,16},{8,20},{12,24},{16,28},{20,0},{24,4},{28,8},{1,13},{... | collective-permute-start | bytes 332936 | tf_op jit(solution)/shard_map/ppermute | solution.py:111
  409.8 25.8 %collective-permute-start.33 = (bf16[96,578]{1,0:T(8,128)(2,1)}, bf16[96,578]{1,0:T(8,128)(2,1)}, u32[]{:S(2)}, u32[]{:S(2)}) collective-permute-start(bf16[96,578]{1,0:T(8,128)(2,1)} %get-tuple-element.145), channel_id=1, source_target_pairs={{0,16},{4,20},{8,24},{12,28},{16,0},{20,4},{24,8},{28,12},{1,17},{... | collective-permute-start | bytes 332936 | tf_op jit(solution)/shard_map/ppermute | solution.py:111
  413.1 80.7 %all-to-all-start.2 = ((bf16[256,2,768]{2,1,0:T(2,128)(2,1)}), bf16[256,2,768]{2,1,0:T(2,128)(2,1)S(1)}, u32[]{:S(2)}, u32[]{:S(2)}) async-start(bf16[256,2,768]{2,1,0:T(2,128)(2,1)} %copy.158), calls=%async_computation.2 | async-start | bytes 1572864 | tf_op jit(solution)/shard_map/all_to_all | solution.py:377
  420.4 27.7 %collective-permute-start.34 = (bf16[96,578]{1,0:T(8,128)(2,1)}, bf16[96,578]{1,0:T(8,128)(2,1)S(1)}, u32[]{:S(2)}, u32[]{:S(2)}) collective-permute-start(bf16[96,578]{1,0:T(8,128)(2,1)} %get-tuple-element.144), channel_id=1, source_target_pairs={{0,20},{4,24},{8,28},{12,0},{16,4},{20,8},{24,12},{28,16},{1,21},{... | collective-permute-start | bytes 332936 | tf_op jit(solution)/shard_map/ppermute | solution.py:111
  427.2 21.0 %collective-permute-start.35 = (bf16[96,578]{1,0:T(8,128)(2,1)}, bf16[96,578]{1,0:T(8,128)(2,1)S(1)}, u32[]{:S(2)}, u32[]{:S(2)}) collective-permute-start(bf16[96,578]{1,0:T(8,128)(2,1)} %get-tuple-element.143), channel_id=1, source_target_pairs={{0,24},{4,28},{8,0},{12,4},{16,8},{20,12},{24,16},{28,20},{1,25},{... | collective-permute-start | bytes 332936 | tf_op jit(solution)/shard_map/ppermute | solution.py:111
  435.6 28.8 %collective-permute-start.36 = (bf16[96,578]{1,0:T(8,128)(2,1)}, bf16[96,578]{1,0:T(8,128)(2,1)}, u32[]{:S(2)}, u32[]{:S(2)}) collective-permute-start(bf16[96,578]{1,0:T(8,128)(2,1)} %get-tuple-element.142), channel_id=1, source_target_pairs={{0,28},{4,0},{8,4},{12,8},{16,12},{20,16},{24,20},{28,24},{1,29},{... | collective-permute-start | bytes 332936 | tf_op jit(solution)/shard_map/ppermute | solution.py:111
  448.1 25.8 %collective-permute-start.49 = (bf16[96,1536]{1,0:T(8,128)(2,1)}, bf16[96,1536]{1,0:T(8,128)(2,1)S(1)}, u32[]{:S(2)}, u32[]{:S(2)}) collective-permute-start(bf16[96,1536]{1,0:T(8,128)(2,1)} %get-tuple-element.128), channel_id=1, source_target_pairs={{0,12},{4,16},{8,20},{12,24},{16,28},{20,0},{24,4},{28,8},{1,13},{... | collective-permute-start | bytes 884744 | tf_op jit(solution)/shard_map/ppermute | solution.py:111
  448.1 31.9 %collective-permute-start.50 = (bf16[96,1536]{1,0:T(8,128)(2,1)}, bf16[96,1536]{1,0:T(8,128)(2,1)S(1)}, u32[]{:S(2)}, u32[]{:S(2)}) collective-permute-start(bf16[96,1536]{1,0:T(8,128)(2,1)} %get-tuple-element.127), channel_id=1, source_target_pairs={{0,16},{4,20},{8,24},{12,28},{16,0},{20,4},{24,8},{28,12},{1,17},{... | collective-permute-start | bytes 884744 | tf_op jit(solution)/shard_map/ppermute | solution.py:111
  464.4 27.0 %collective-permute-start.53 = (bf16[96,1536]{1,0:T(8,128)(2,1)S(1)}, bf16[96,1536]{1,0:T(8,128)(2,1)S(1)}, u32[]{:S(2)}, u32[]{:S(2)}) collective-permute-start(bf16[96,1536]{1,0:T(8,128)(2,1)S(1)} %copy-done.50), channel_id=1, source_target_pairs={{0,28},{4,0},{8,4},{12,8},{16,12},{20,16},{24,20},{28,24},{1,29},{... | collective-permute-start | bytes 884744 | tf_op jit(solution)/shard_map/ppermute | solution.py:111
  (133 other events, 1190.6 us)

commit v4 on v3

--- a/solution.py
+++ b/solution.py
@@ -89,29 +89,12 @@
         return lax.ppermute(value, "tensor", across_cores)
 
     def gather_dp(block):
-        if n_data > 8:
-            return lax.all_gather(block, "dp", axis=0, tiled=True)
-        got = [block] + [
-            lax.ppermute(block, "dp", [(j, (j + k) % n_data) for j in range(n_data)])
-            for k in range(1, n_data)
-        ]
-        stacked = jnp.stack(got)
-        ordered = jnp.take(stacked, (data_index - jnp.arange(n_data)) % n_data, axis=0)
-        return ordered.reshape(n_data * block.shape[0], *block.shape[1:])
+        return lax.all_gather(block, "dp", axis=0, tiled=True)
 
     def scatter_dp(total):
-        if n_data > 8:
-            return lax.psum_scatter(
-                total.astype(jnp.bfloat16), "dp", scatter_dimension=0, tiled=True
-            ).astype(jnp.float32)
-        pieces = total.astype(jnp.bfloat16).reshape(n_data, -1, *total.shape[1:])
-        acc = lax.dynamic_index_in_dim(total.reshape(pieces.shape), data_index, 0, keepdims=False)
-        for k in range(1, n_data):
-            sent = lax.dynamic_index_in_dim(pieces, (data_index + k) % n_data, 0, keepdims=False)
-            acc = acc + lax.ppermute(
-                sent, "dp", [(j, (j + k) % n_data) for j in range(n_data)]
-            ).astype(jnp.float32)
-        return acc
+        return lax.psum_scatter(
+            total.astype(jnp.bfloat16), "dp", scatter_dimension=0, tiled=True
+        ).astype(jnp.float32)
 
     def gather_cores(mine):
         low = mine.astype(jnp.bfloat16)
@@ -332,7 +315,6 @@
         ],
         axis=1,
     )
-    output_shard_ext = reduce_weights([output_grads[0]], [output_grads[1]], early_columns)
     late_columns = jnp.stack(
         [
             place([q[:head_cols] for q in qkv_bias_sums], head_cols, width),
@@ -340,21 +322,26 @@
         ],
         axis=1,
     )
-    project_shard_ext = reduce_weights([project_grads[0]], [project_grads[1]], late_columns)
+    attn_shard = reduce_weights(
+        [project_grads[0], output_grads[0]],
+        [project_grads[1], output_grads[1]],
+        jnp.concatenate([early_columns, late_columns], axis=1),
+    )
     up_shard = feed_shard[:, :hidden_cols]
     down_shard = feed_shard[:, hidden_cols:]
-    head_out = output_shard_ext.shape[1] - early_columns.shape[1]
-    output_shard = output_shard_ext[:, :head_out]
-    project_shard = project_shard_ext[:, :project_cols]
+    head_out = project_cols + head_cols
+    project_shard = attn_shard[:, :project_cols]
+    output_shard = attn_shard[:, project_cols:head_out]
+    late_at = head_out + early_columns.shape[1]
 
     def mine_of(column):
         return lax.dynamic_slice_in_dim(column, tensor_index * vec_block, vec_block)
 
-    early = [mine_of(output_shard_ext[:, head_out + k]) for k in range(6)]
+    early = [mine_of(attn_shard[:, head_out + k]) for k in range(6)]
     up_bias_shard = lax.dynamic_index_in_dim(
-        output_shard_ext[:, head_out + 6 :], tensor_index, axis=1, keepdims=False
-    )
-    late = [mine_of(project_shard_ext[:, project_cols + k]) for k in range(2)]
+        attn_shard[:, head_out + 6 : late_at], tensor_index, axis=1, keepdims=False
+    )
+    late = [mine_of(attn_shard[:, late_at + k]) for k in range(2)]
     small = [
         late[0],
         late[1],

time: 505 us -> 471 us (0.933)
  waiting for transfers between devices: 177 us -> 230 us
  starting transfers between devices: 69.9 us -> 30.6 us
  local copies, waits for them, and re-layouts: 75.4 us -> 45.6 us
  other arithmetic: 51.6 us -> 33.9 us
  between operations: 2.79 us -> 15.9 us
  matrix products: 120 us -> 107 us
    ppermute x35 -> x0, waiting for transfers between devices: 113 us -> none  [the longest x14 58.2 us: gather_dp(): lax.ppermute(block, 'dp', [(j, (j + k) % n_data) for j in range(n_data)])]
    ppermute x9 -> x8, waiting for transfers between devices: 62.2 us -> 137 us  [to_chip_partner(): return lax.ppermute(value, 'tensor', across_chips)]
    ppermute x35 -> x0, starting transfers between devices: 37.5 us -> none  [the longest x21 24 us: scatter_dp(): lax.ppermute(sent, 'dp', [(j, (j + k) % n_data) for j in range(n_data)])]
    unnamed x0 -> x6, waiting for transfers between devices: none -> 32.7 us
    all_to_all x1, waiting for transfers between devices: 0.01 us -> 20 us  [on_device(): lax.all_to_all(grad_here, 'dp', split_axis=0, concat_axis=1, tiled=True)]
    all_to_all x2, waiting for transfers between devices: 0.01 us -> 19.1 us  [deal(): here = lax.all_to_all(sent, 'dp', split_axis=1, concat_axis=0, tiled=True)]
    all_gather x0 -> x2, waiting for transfers between devices: none -> 12.4 us  [gather_dp(): return lax.all_gather(block, 'dp', axis=0, tiled=True)]
    ppermute x10 -> x9, waiting for transfers between devices: 1 us -> 8.97 us  [to_core_partner(): return lax.ppermute(value, 'tensor', across_cores)]
  transfers between devices with their start and end apart: 57 -> 24, of which waited for: 20 -> 18; matrix products, arithmetic and copies ran while one was open for 42% -> 23% of each run, Pallas kernels for 0% -> 0%
where the time goes in v4:
time: 471 us; the launch traced here: 463 us
  waiting for transfers between devices  230 us (49%)
  matrix products  107 us (23%)
  local copies, waits for them, and re-layouts  45.6 us (10%)
  other arithmetic  33.9 us (7%)
  starting transfers between devices  30.6 us (6%)
  between operations  15.9 us (3%)
    ppermute x8, waiting for transfers between devices, to_chip_partner(): return lax.ppermute(value, 'tensor', across_chips)  137 us
    dot_general x8, matrix products, dot_nn(): return jnp.dot(a, b, preferred_element_type=jnp.float32)  40.6 us
    unnamed x6, waiting for transfers between devices  32.7 us
    unnamed x203, local copies, waits for them, and re-layouts  30.7 us
    all_to_all x1, waiting for transfers between devices, on_device(): lax.all_to_all(grad_here, 'dp', split_axis=0, concat_axis=1, tiled=True)  20 us
    all_to_all x2, waiting for transfers between devices, deal(): here = lax.all_to_all(sent, 'dp', split_axis=1, concat_axis=0, tiled=True)  19.1 us
    dot_general x8, matrix products, dot_tn(): lax.dot_general(a, b, (((0,), (0,)), ((), ())), preferred_element_type=jn...  17.2 us
    all_gather x2, waiting for transfers between devices, gather_dp(): return lax.all_gather(block, 'dp', axis=0, tiled=True)  12.4 us
  transfers between devices with their start and end apart: 24, of which 18 were waited for; matrix products, arithmetic and copies ran while one was open for 23% of the time, Pallas kernels for 0%

profile of v4, /device:TPU:12, one launch (start us, length us, event | category | flops | bytes accessed | tf_op | source)
XLA Modules:
  0.0 462.9 jit_solution(9259465110559571940)
XLA Ops:
  10.6 6.4 %all-to-all-start = ((bf16[32,16,768]{2,0,1:T(8,128)(2,1)}), bf16[32,16,768]{2,0,1:T(8,128)(2,1)S(1)}, u32[]{:S(2)}, u32[]{:S(2)}) async-start(bf16[32,16,768]{2,0,1:T(8,128)(2,1)} %copy.90), calls=%async_computation | async-start | bytes 1572864 | tf_op jit(solution)/shard_map/all_to_all | solution.py:113
  17.9 19.1 %all-to-all-done = bf16[32,16,768]{2,0,1:T(8,128)(2,1)S(1)} async-done(((bf16[32,16,768]{2,0,1:T(8,128)(2,1)}), bf16[32,16,768]{2,0,1:T(8,128)(2,1)S(1)}, u32[]{:S(2)}, u32[]{:S(2)}) %all-to-all-start) | async-done | bytes 786464 | tf_op jit(solution)/shard_map/all_to_all | solution.py:113
  38.7 9.2 %collective-permute-done = bf16[256,768]{1,0:T(8,128)(2,1)S(1)} collective-permute-done((bf16[256,768]{1,0:T(8,128)(2,1)S(1)}, bf16[256,768]{1,0:T(8,128)(2,1)S(1)}, u32[]{:S(2)}, u32[]{:S(2)}) %collective-permute-start) | collective-permute-done | bytes 393248 | tf_op jit(solution)/shard_map/ppermute | solution.py:86
  50.3 11.4 %all-gather.3.cloned.1.call-done = bf16[768,768]{1,0:T(8,128)(2,1)} async-done(((bf16[96,768]{1,0:T(8,128)(2,1)}), bf16[768,768]{1,0:T(8,128)(2,1)}) %all-gather.3.cloned.1.call-update) | async-done | bytes 1179664 | tf_op jit(solution)/shard_map/all_gather | solution.py:92
  70.1 2.8 copy-done.2
  77.3 11.5 %collective-permute-done.2 = bf16[768,768]{1,0:T(8,128)(2,1)S(1)} collective-permute-done((bf16[768,768]{1,0:T(8,128)(2,1)}, bf16[768,768]{1,0:T(8,128)(2,1)S(1)}, u32[]{:S(2)}, u32[]{:S(2)}) %collective-permute-start.2) | collective-permute-done | bytes 1179680 | tf_op jit(solution)/shard_map/ppermute | solution.py:86
  88.8 2.7 add_convert_fusion.2
  95.7 2.9 copy-done.3
  108.1 5.3 %all-to-all-start.1 = ((bf16[32,16,768]{2,0,1:T(8,128)(2,1)}), bf16[32,16,768]{2,0,1:T(8,128)(2,1)S(1)}, u32[]{:S(2)}, u32[]{:S(2)}) async-start(bf16[32,16,768]{2,0,1:T(8,128)(2,1)} %copy.95), calls=%async_computation.1 | async-start | bytes 1572864 | tf_op jit(solution)/shard_map/all_to_all | solution.py:113
  117.2 11.5 %multiply_convert_fusion.3 = (bf16[1024,768]{1,0:T(8,128)(2,1)S(1)}, f32[1024,768]{1,0:T(8,128)}, f32[1024,768]{1,0:T(8,128)}) fusion(f32[768]{0:T(1024)} %get-tuple-element.124, bf16[768,1536]{1,0:T(8,128)(2,1)} %all-gather.5.cloned.1.call-done, bf16[512,768]{1,0:T(8,128)(2,1)} %collective-permute-done.4, bf16[512,768]{1,0:T(8,128)(2,1)} %fusion.40), kind=kOutput, calls=%fused_computation.45 | convolution fusion | flops 1263009792 | bytes 10620928 | tf_op jit(solution)/shard_map/dot_general | solution.py:38
  130.2 38.1 %collective-permute-done.5 = bf16[768,1536]{1,0:T(8,128)(2,1)S(1)} collective-permute-done((bf16[768,1536]{1,0:T(8,128)(2,1)}, bf16[768,1536]{1,0:T(8,128)(2,1)S(1)}, u32[]{:S(2)}, u32[]{:S(2)}) %collective-permute-start.5) | collective-permute-done | bytes 2359328 | tf_op jit(solution)/shard_map/ppermute | solution.py:86
  168.2 11.8 %multiply_convert_fusion.2 = (bf16[1024,768]{1,0:T(8,128)(2,1)S(1)}, f32[1024,768]{1,0:T(8,128)}, f32[1024,768]{1,0:T(8,128)}) fusion(f32[768]{0:T(1024)S(1)} %copy-done.70, bf16[768,1536]{1,0:T(8,128)(2,1)S(1)} %collective-permute-done.5, bf16[512,768]{1,0:T(8,128)(2,1)} %collective-permute-done.4, bf16[512,768]{1,0:T(8,128)(2,1)} %fusion.40), kind=kOutput, calls=%fused_computation.32 | convolution fusion | flops 1263009792 | bytes 10620928 | tf_op jit(solution)/shard_map/dot_general | solution.py:38
  189.0 6.9 %collective-permute-done.8 = bf16[256,768]{1,0:T(8,128)(2,1)S(1)} collective-permute-done((bf16[256,768]{1,0:T(8,128)(2,1)S(1)}, bf16[256,768]{1,0:T(8,128)(2,1)S(1)}, u32[]{:S(2)}, u32[]{:S(2)}) %collective-permute-start.8) | collective-permute-done | bytes 393248 | tf_op jit(solution)/shard_map/ppermute | solution.py:86
  200.8 3.8 convert_reduce_fusion.1
  208.7 3.8 convert_reduce_fusion
  224.2 6.3 %multiply_reduce_fusion = (f32[3,1024]{1,0:T(4,128)S(1)}, f32[3,1024,1024]{1,2,0:T(8,128)S(1)}) fusion(f32[3,1024,1024]{1,2,0:T(8,128)} %copy-done.3, f32[3,1024]{1,0:T(4,128)S(1)} %log_add_fusion, bf16[1024,3,64]{0,2,1:T(8,128)(2,1)S(1)} %bitcast.163, bf16[1024,3,64]{0,2,1:T(8,128)(2,1)S(1)} %bitcast.170), kind=kOutput, calls=%fused_computation.1 | convolution fusion | flops 412087296 | bytes 25976832 | tf_op jit(solution)/shard_map/qhe,khe->hqk/dot_general | solution.py:194
  232.5 5.2 %multiply_convert_fusion = bf16[3,1024,1024]{1,2,0:T(8,128)(2,1)} fusion(f32[3,1024,1024]{1,2,0:T(8,128)S(1)} %get-tuple-element.144, f32[3,1024,1024]{1,2,0:T(8,128)S(1)} %bitcast.139, f32[3,1024]{1,0:T(4,128)S(1)} %get-tuple-element.143, f32[3,1024]{1,0:T(4,128)S(1)} %log_add_fusion), kind=kLoop, calls=%fused_computation | loop fusion | flops 12582912 | bytes 31481856 | tf_op jit(solution)/shard_map/convert_element_type | solution.py:198
  237.7 4.1 fusion.46
  248.8 2.8 multiply_reduce_fusion.1
  251.6 5.5 %multiply_convert_fusion.1 = bf16[3,1024,1024]{1,2,0:T(8,128)(2,1)} fusion(f32[3,1024,1024]{1,2,0:T(8,128)S(1)} %get-tuple-element.142, f32[3,1024,1024]{1,2,0:T(8,128)S(1)} %bitcast.137, f32[3,1024]{1,0:T(4,128)S(1)} %get-tuple-element.141, f32[3,1024]{1,0:T(4,128)S(1)} %log_add_fusion.1), kind=kLoop, calls=%fused_computation.3 | loop fusion | flops 12582912 | bytes 31481856 | tf_op jit(solution)/shard_map/convert_element_type | solution.py:198
  257.1 4.1 fusion.44
  273.5 2.8 convolution_convert_fusion.1
  284.2 17.2 %collective-permute-done.15 = bf16[768,780]{0,1:T(8,128)(2,1)S(1)} collective-permute-done((bf16[768,780]{0,1:T(8,128)(2,1)S(1)}, bf16[768,780]{0,1:T(8,128)(2,1)S(1)}, u32[]{:S(2)}, u32[]{:S(2)}) %collective-permute-start.15) | collective-permute-done | bytes 1198112 | tf_op jit(solution)/shard_map/ppermute | solution.py:86
  303.6 3.5 fusion.118
  313.6 37.6 %collective-permute-done.16 = bf16[768,1536]{0,1:T(8,128)(2,1)} collective-permute-done((bf16[768,1536]{0,1:T(8,128)(2,1)}, bf16[768,1536]{0,1:T(8,128)(2,1)}, u32[]{:S(2)}, u32[]{:S(2)}) %collective-permute-start.16) | collective-permute-done | bytes 2359328 | tf_op jit(solution)/shard_map/ppermute | solution.py:86
  351.2 3.8 fusion.12
  355.0 4.4 copy.125
  362.7 8.8 %collective-permute-done.13 = bf16[256,768]{1,0:T(8,128)(2,1)S(1)} collective-permute-done((bf16[256,768]{1,0:T(8,128)(2,1)S(1)}, bf16[256,768]{1,0:T(8,128)(2,1)S(1)}, u32[]{:S(2)}, u32[]{:S(2)}) %collective-permute-start.13) | collective-permute-done | bytes 393248 | tf_op jit(solution)/shard_map/ppermute | solution.py:86
  373.3 6.0 %all-to-all-start.2 = ((bf16[256,2,768]{2,1,0:T(2,128)(2,1)}), bf16[256,2,768]{2,1,0:T(2,128)(2,1)S(1)}, u32[]{:S(2)}, u32[]{:S(2)}) async-start(bf16[256,2,768]{2,1,0:T(2,128)(2,1)} %copy.103), calls=%async_computation.2 | async-start | bytes 1572864 | tf_op jit(solution)/shard_map/all_to_all | solution.py:364
  380.9 7.4 %collective-permute-done.7 = bf16[256,768]{1,0:T(8,128)(2,1)S(1)} collective-permute-done((bf16[256,768]{1,0:T(8,128)(2,1)S(1)}, bf16[256,768]{1,0:T(8,128)(2,1)S(1)}, u32[]{:S(2)}, u32[]{:S(2)}) %collective-permute-start.7) | collective-permute-done | bytes 393248 | tf_op jit(solution)/shard_map/ppermute | solution.py:86
  390.2 20.0 %all-to-all-done.2 = bf16[256,2,768]{2,1,0:T(2,128)(2,1)S(1)} async-done(((bf16[256,2,768]{2,1,0:T(2,128)(2,1)}), bf16[256,2,768]{2,1,0:T(2,128)(2,1)S(1)}, u32[]{:S(2)}, u32[]{:S(2)}) %all-to-all-start.2) | async-done | bytes 786464 | tf_op jit(solution)/shard_map/all_to_all | solution.py:364
  420.2 32.7 %reduce-scatter.9.cloned.1.call-done = bf16[96,1536]{1,0:T(8,128)(2,1)} async-done(((bf16[768,1536]{1,0:T(8,128)(2,1)}), bf16[96,1536]{1,0:T(8,128)(2,1)}) %reduce-scatter.9.cloned.1.call-update) | async-done | bytes 294928
  (363 shorter events, 127.4 us)
Async XLA Ops:
  10.6 37.4 %copy-start.45 = (bf16[96,768]{1,0:T(8,128)(2,1)S(1)}, bf16[96,768]{1,0:T(8,128)(2,1)}, u32[]{:S(2)}) copy-start(bf16[96,768]{1,0:T(8,128)(2,1)} %param.29) | copy-start | bytes 442372
  10.6 37.4 %copy-start.46 = (bf16[96,768]{1,0:T(8,128)(2,1)S(1)}, bf16[96,768]{1,0:T(8,128)(2,1)}, u32[]{:S(2)}) copy-start(bf16[96,768]{1,0:T(8,128)(2,1)} %param.27) | copy-start | bytes 442372
  10.6 26.4 %all-to-all-start = ((bf16[32,16,768]{2,0,1:T(8,128)(2,1)}), bf16[32,16,768]{2,0,1:T(8,128)(2,1)S(1)}, u32[]{:S(2)}, u32[]{:S(2)}) async-start(bf16[32,16,768]{2,0,1:T(8,128)(2,1)} %copy.90), calls=%async_computation | async-start | bytes 1572864 | tf_op jit(solution)/shard_map/all_to_all | solution.py:113
  16.9 32.0 %copy-start.66 = (s32[16]{0:T(128)S(1)}, s32[16]{0:T(128)}, u32[]{:S(2)}) copy-start(s32[16]{0:T(128)} %param.19) | copy-start | bytes 196
  16.9 32.0 %copy-start.78 = (s32[16]{0:T(128)S(1)}, s32[16]{0:T(128)}, u32[]{:S(2)}) copy-start(s32[16]{0:T(128)} %param.18) | copy-start | bytes 196
  17.0 44.8 %all-gather.3.cloned.1.call-start = ((), (), s32[]{:S(2)}) async-start(), calls=%async_computation.5 | async-start | bytes 1327104 | tf_op jit(solution)/shard_map/all_gather | solution.py:92
  17.8 98.0 %all-gather.5.cloned.1.call-start = ((), (), s32[]{:S(2)}) async-start(), calls=%async_computation.6 | async-start | bytes 2654208 | tf_op jit(solution)/shard_map/all_gather | solution.py:92
  37.1 67.3 %copy-start.15 = (bf16[256,768]{1,0:T(8,128)(2,1)}, bf16[256,768]{1,0:T(8,128)(2,1)S(1)}, u32[]{:S(2)}) copy-start(bf16[256,768]{1,0:T(8,128)(2,1)S(1)} %get-tuple-element.111) | copy-start | bytes 1179652
  37.1 10.8 %collective-permute-start = (bf16[256,768]{1,0:T(8,128)(2,1)S(1)}, bf16[256,768]{1,0:T(8,128)(2,1)S(1)}, u32[]{:S(2)}, u32[]{:S(2)}) collective-permute-start(bf16[256,768]{1,0:T(8,128)(2,1)S(1)} %get-tuple-element.112), channel_id=1, source_target_pairs={{0,2},{1,3},{2,0},{3,1},{4,6},{5,7},{6,4},{7,5},{8,10},{9,11},{10,... | collective-permute-start | bytes 1179656 | tf_op jit(solution)/shard_map/ppermute | solution.py:86
  47.9 56.5 %copy-start.24 = (bf16[256,768]{1,0:T(8,128)(2,1)}, bf16[256,768]{1,0:T(8,128)(2,1)S(1)}, u32[]{:S(2)}) copy-start(bf16[256,768]{1,0:T(8,128)(2,1)S(1)} %collective-permute-done) | copy-start | bytes 1179652
  47.9 15.3 %collective-permute-start.1 = (bf16[512,768]{1,0:T(8,128)(2,1)S(1)}, bf16[512,768]{1,0:T(8,128)(2,1)}, u32[]{:S(2)}, u32[]{:S(2)}) collective-permute-start(bf16[512,768]{1,0:T(8,128)(2,1)S(1)} %pad_maximum_fusion.8), channel_id=1, source_target_pairs={{0,1},{1,0},{2,3},{3,2},{4,5},{5,4},{6,7},{7,6},{8,9},{9,8},{10,11... | collective-permute-start | bytes 2359304 | tf_op jit(solution)/shard_map/ppermute | solution.py:89
  61.8 27.1 %collective-permute-start.2 = (bf16[768,768]{1,0:T(8,128)(2,1)}, bf16[768,768]{1,0:T(8,128)(2,1)S(1)}, u32[]{:S(2)}, u32[]{:S(2)}) collective-permute-start(bf16[768,768]{1,0:T(8,128)(2,1)} %all-gather.3.cloned.1.call-done), channel_id=1, source_target_pairs={{0,2},{1,3},{2,0},{3,1},{4,6},{5,7},{6,4},{7,5},{8,10},{9,11},{10,... | collective-permute-start | bytes 3538952 | tf_op jit(solution)/shard_map/ppermute | solution.py:86
  102.0 2.4 collective-permute-start.3
  106.4 10.9 %collective-permute-start.4 = (bf16[512,768]{1,0:T(8,128)(2,1)}, bf16[512,768]{1,0:T(8,128)(2,1)}, u32[]{:S(2)}, u32[]{:S(2)}) collective-permute-start(bf16[512,768]{1,0:T(8,128)(2,1)} %fusion.40), channel_id=1, source_target_pairs={{0,1},{1,0},{2,3},{3,2},{4,5},{5,4},{6,7},{7,6},{8,9},{9,8},{10,11... | collective-permute-start | bytes 2359304 | tf_op jit(solution)/shard_map/ppermute | solution.py:89
  108.1 76.0 %all-to-all-start.1 = ((bf16[32,16,768]{2,0,1:T(8,128)(2,1)}), bf16[32,16,768]{2,0,1:T(8,128)(2,1)S(1)}, u32[]{:S(2)}, u32[]{:S(2)}) async-start(bf16[32,16,768]{2,0,1:T(8,128)(2,1)} %copy.95), calls=%async_computation.1 | async-start | bytes 1572864 | tf_op jit(solution)/shard_map/all_to_all | solution.py:113
  113.4 298.9 %reduce-scatter.7.cloned.1.call-start = ((), (), s32[]{:S(2)}) async-start(), calls=%async_computation.7 | async-start | bytes 1548288
  115.8 52.5 %collective-permute-start.5 = (bf16[768,1536]{1,0:T(8,128)(2,1)}, bf16[768,1536]{1,0:T(8,128)(2,1)S(1)}, u32[]{:S(2)}, u32[]{:S(2)}) collective-permute-start(bf16[768,1536]{1,0:T(8,128)(2,1)} %all-gather.5.cloned.1.call-done), channel_id=1, source_target_pairs={{0,2},{1,3},{2,0},{3,1},{4,6},{5,7},{6,4},{7,5},{8,10},{9,11},{10,... | collective-permute-start | bytes 7077896 | tf_op jit(solution)/shard_map/ppermute | solution.py:86
  128.7 39.5 %copy-start.70 = (f32[768]{0:T(1024)S(1)}, f32[768]{0:T(1024)}, u32[]{:S(2)}) copy-start(f32[768]{0:T(1024)} %get-tuple-element.123) | copy-start | bytes 9220
  184.2 2.6 collective-permute-start.6
  184.3 11.6 %collective-permute-start.8 = (bf16[256,768]{1,0:T(8,128)(2,1)S(1)}, bf16[256,768]{1,0:T(8,128)(2,1)S(1)}, u32[]{:S(2)}, u32[]{:S(2)}) collective-permute-start(bf16[256,768]{1,0:T(8,128)(2,1)S(1)} %get-tuple-element.110), channel_id=1, source_target_pairs={{0,2},{1,3},{2,0},{3,1},{4,6},{5,7},{6,4},{7,5},{8,10},{9,11},{10,... | collective-permute-start | bytes 1179656 | tf_op jit(solution)/shard_map/ppermute | solution.py:86
  198.4 2.4 collective-permute-start.9
  214.1 2.4 collective-permute-start.10
  219.7 2.5 collective-permute-start.11
  267.2 4.6 collective-permute-start.14
  272.0 29.4 %collective-permute-start.15 = (bf16[768,780]{0,1:T(8,128)(2,1)S(1)}, bf16[768,780]{0,1:T(8,128)(2,1)S(1)}, u32[]{:S(2)}, u32[]{:S(2)}) collective-permute-start(bf16[768,780]{0,1:T(8,128)(2,1)S(1)} %pad_maximum_fusion.5), channel_id=1, source_target_pairs={{0,2},{1,3},{2,0},{3,1},{4,6},{5,7},{6,4},{7,5},{8,10},{9,11},{10,... | collective-permute-start | bytes 3594248 | tf_op jit(solution)/shard_map/ppermute | solution.py:86
  279.5 71.7 %collective-permute-start.16 = (bf16[768,1536]{0,1:T(8,128)(2,1)}, bf16[768,1536]{0,1:T(8,128)(2,1)}, u32[]{:S(2)}, u32[]{:S(2)}) collective-permute-start(bf16[768,1536]{0,1:T(8,128)(2,1)} %pad_maximum_fusion), channel_id=1, source_target_pairs={{0,2},{1,3},{2,0},{3,1},{4,6},{5,7},{6,4},{7,5},{8,10},{9,11},{10,... | collective-permute-start | bytes 7077896 | tf_op jit(solution)/shard_map/ppermute | solution.py:86
  303.6 149.3 %reduce-scatter.9.cloned.1.call-start = ((), (), s32[]{:S(2)}) async-start(), calls=%async_computation.8 | async-start | bytes 2654208
  313.5 46.0 %collective-permute-start.12 = (bf16[512,768]{1,0:T(8,128)(2,1)S(1)}, bf16[512,768]{1,0:T(8,128)(2,1)S(1)}, u32[]{:S(2)}, u32[]{:S(2)}) collective-permute-start(bf16[512,768]{1,0:T(8,128)(2,1)S(1)} %slice.288), channel_id=1, source_target_pairs={{0,1},{1,0},{2,3},{3,2},{4,5},{5,4},{6,7},{7,6},{8,9},{9,8},{10,11... | collective-permute-start | bytes 2359304 | tf_op jit(solution)/shard_map/ppermute | solution.py:89
  361.2 10.3 %collective-permute-start.13 = (bf16[256,768]{1,0:T(8,128)(2,1)S(1)}, bf16[256,768]{1,0:T(8,128)(2,1)S(1)}, u32[]{:S(2)}, u32[]{:S(2)}) collective-permute-start(bf16[256,768]{1,0:T(8,128)(2,1)S(1)} %slice.212), channel_id=1, source_target_pairs={{0,2},{1,3},{2,0},{3,1},{4,6},{5,7},{6,4},{7,5},{8,10},{9,11},{10,... | collective-permute-start | bytes 1179656 | tf_op jit(solution)/shard_map/ppermute | solution.py:86
  373.3 36.8 %all-to-all-start.2 = ((bf16[256,2,768]{2,1,0:T(2,128)(2,1)}), bf16[256,2,768]{2,1,0:T(2,128)(2,1)S(1)}, u32[]{:S(2)}, u32[]{:S(2)}) async-start(bf16[256,2,768]{2,1,0:T(2,128)(2,1)} %copy.103), calls=%async_computation.2 | async-start | bytes 1572864 | tf_op jit(solution)/shard_map/all_to_all | solution.py:364
  379.4 8.9 %collective-permute-start.7 = (bf16[256,768]{1,0:T(8,128)(2,1)S(1)}, bf16[256,768]{1,0:T(8,128)(2,1)S(1)}, u32[]{:S(2)}, u32[]{:S(2)}) collective-permute-start(bf16[256,768]{1,0:T(8,128)(2,1)S(1)} %slice.206), channel_id=1, source_target_pairs={{0,2},{1,3},{2,0},{3,1},{4,6},{5,7},{6,4},{7,5},{8,10},{9,11},{10,... | collective-permute-start | bytes 1179656 | tf_op jit(solution)/shard_map/ppermute | solution.py:86
  411.0 44.9 %copy-start.1 = (bf16[32,16,768]{2,1,0:T(8,128)(2,1)S(1)}, bf16[32,16,768]{2,1,0:T(8,128)(2,1)}, u32[]{:S(2)}) copy-start(bf16[32,16,768]{2,1,0:T(8,128)(2,1)} %param.17) | copy-start | bytes 2359300
  (89 other events, 490.0 us)
Sparse Core Ops, SparseCore 0:
  20.5 41.1 all-gather.2
  64.5 51.2 all-gather.4
  303.7 65.9 reduce-scatter.6
  373.0 79.8 reduce-scatter.8

commit v5 on v4

--- a/solution.py
+++ b/solution.py
@@ -96,6 +96,20 @@
             total.astype(jnp.bfloat16), "dp", scatter_dimension=0, tiled=True
         ).astype(jnp.float32)
 
+    def scatter_dp_permutes(total):
+        if n_data > 8:
+            return scatter_dp(total)
+        pieces = total.astype(jnp.bfloat16).reshape(n_data, -1, *total.shape[1:])
+        acc = lax.dynamic_index_in_dim(
+            total.reshape(pieces.shape), data_index, 0, keepdims=False
+        )
+        for k in range(1, n_data):
+            sent = lax.dynamic_index_in_dim(pieces, (data_index + k) % n_data, 0, keepdims=False)
+            acc = acc + lax.ppermute(
+                sent, "dp", [(j, (j + k) % n_data) for j in range(n_data)]
+            ).astype(jnp.float32)
+        return acc
+
     def gather_cores(mine):
         low = mine.astype(jnp.bfloat16)
         return jnp.concatenate([low, to_core_partner(low)], axis=0)
@@ -267,12 +281,6 @@
     branch_grad_full = gather_cores(grad_residual)
     grad_mixed = [dot_nn(branch_grad_full, output_ws[g]).astype(jnp.bfloat16) for g in groups]
     output_grads = [dot_tn(branch_grad_full, mixed[g]) for g in groups]
-    grad_projected = [attend_back(projected[g], log_total[g], grad_mixed[g]) for g in groups]
-    project_grads = [dot_tn(inputs_full, grad_projected[g]) for g in groups]
-    qkv_bias_sums = [jnp.sum(grad_projected[g], axis=0, dtype=jnp.float32) for g in groups]
-    grad_inputs = grad_residual + scatter_cores(
-        sum(dot_nt(grad_projected[g], project_ws[g]) for g in groups)
-    )
 
     def place(parts, part_len, total_len):
         blank = jnp.zeros((total_len,), jnp.float32)
@@ -282,18 +290,6 @@
 
     rows_block = width // n_data
     vec_block = width // n_all
-
-    def reduce_weights(own_parts, partner_parts, extra=None):
-        own = jnp.concatenate(own_parts, axis=1)
-        partner = jnp.concatenate(partner_parts, axis=1)
-        if extra is not None:
-            extra = extra + to_core_partner(extra)
-            own = jnp.concatenate([own, extra], axis=1)
-            partner = jnp.concatenate([partner, extra], axis=1)
-        sent = to_chip_partner(partner.astype(jnp.bfloat16))
-        return scatter_dp(own + sent.astype(jnp.float32))
-
-    feed_shard = reduce_weights([up_grads[0], down_grads[0]], [up_grads[1], down_grads[1]])
     up_placed = place(up_bias_sums, hidden_cols, hidden_cols * n_tensor)
     up_columns = (
         up_placed.reshape(n_data, n_tensor, rows_block).transpose(0, 2, 1).reshape(width, n_tensor)
@@ -315,6 +311,33 @@
         ],
         axis=1,
     )
+    early_columns = early_columns + to_core_partner(early_columns)
+    early_own = jnp.concatenate([up_grads[0], down_grads[0], output_grads[0]], axis=1)
+    early_partner = jnp.concatenate([up_grads[1], down_grads[1], output_grads[1]], axis=1)
+    early_cols = early_own.shape[1]
+    early_pack = jnp.concatenate([early_own, early_partner, early_columns], axis=1).astype(
+        jnp.bfloat16
+    )
+    early_pack, grad_mixed = lax.optimization_barrier((early_pack, grad_mixed))
+    early_reduced = lax.psum_scatter(
+        early_pack, "dp", scatter_dimension=0, tiled=True
+    ).astype(jnp.float32)
+    early_sent = to_chip_partner(early_reduced[:, early_cols:].astype(jnp.bfloat16)).astype(
+        jnp.float32
+    )
+    early_shard = early_reduced[:, :early_cols] + early_sent[:, :early_cols]
+    early_small = early_reduced[:, 2 * early_cols :] + early_sent[:, early_cols:]
+    up_shard = early_shard[:, :hidden_cols]
+    down_shard = early_shard[:, hidden_cols : 2 * hidden_cols]
+    output_shard = early_shard[:, 2 * hidden_cols :]
+
+    grad_projected = [attend_back(projected[g], log_total[g], grad_mixed[g]) for g in groups]
+    project_grads = [dot_tn(inputs_full, grad_projected[g]) for g in groups]
+    qkv_bias_sums = [jnp.sum(grad_projected[g], axis=0, dtype=jnp.float32) for g in groups]
+    grad_inputs = grad_residual + scatter_cores(
+        sum(dot_nt(grad_projected[g], project_ws[g]) for g in groups)
+    )
+
     late_columns = jnp.stack(
         [
             place([q[:head_cols] for q in qkv_bias_sums], head_cols, width),
@@ -322,26 +345,19 @@
         ],
         axis=1,
     )
-    attn_shard = reduce_weights(
-        [project_grads[0], output_grads[0]],
-        [project_grads[1], output_grads[1]],
-        jnp.concatenate([early_columns, late_columns], axis=1),
-    )
-    up_shard = feed_shard[:, :hidden_cols]
-    down_shard = feed_shard[:, hidden_cols:]
-    head_out = project_cols + head_cols
-    project_shard = attn_shard[:, :project_cols]
-    output_shard = attn_shard[:, project_cols:head_out]
-    late_at = head_out + early_columns.shape[1]
+    late_columns = late_columns + to_core_partner(late_columns)
+    late_own = jnp.concatenate([project_grads[0], late_columns], axis=1)
+    late_partner = jnp.concatenate([project_grads[1], late_columns], axis=1)
+    late_total = late_own + to_chip_partner(late_partner.astype(jnp.bfloat16)).astype(jnp.float32)
+    late_shard = scatter_dp_permutes(late_total)
+    project_shard = late_shard[:, :project_cols]
 
     def mine_of(column):
         return lax.dynamic_slice_in_dim(column, tensor_index * vec_block, vec_block)
 
-    early = [mine_of(attn_shard[:, head_out + k]) for k in range(6)]
-    up_bias_shard = lax.dynamic_index_in_dim(
-        attn_shard[:, head_out + 6 : late_at], tensor_index, axis=1, keepdims=False
-    )
-    late = [mine_of(attn_shard[:, late_at + k]) for k in range(2)]
+    early = [mine_of(early_small[:, k]) for k in range(6)]
+    up_bias_shard = lax.dynamic_index_in_dim(early_small[:, 6:], tensor_index, axis=1, keepdims=False)
+    late = [mine_of(late_shard[:, project_cols + k]) for k in range(2)]
     small = [
         late[0],
         late[1],

time: 471 us -> 427 us (0.907)
  waiting for transfers between devices: 230 us -> 157 us
  local copies, waits for them, and re-layouts: 45.6 us -> 57.4 us
  starting transfers between devices: 30.6 us -> 39.8 us
  matrix products: 107 us -> 113 us
    ppermute x8, waiting for transfers between devices: 137 us -> 86.5 us  [to_chip_partner(): return lax.ppermute(value, 'tensor', across_chips)]
    unnamed x6 -> x4, waiting for transfers between devices: 32.7 us -> 0.07 us
    ppermute x0 -> x7, waiting for transfers between devices: none -> 31.1 us  [scatter_dp_permutes(): lax.ppermute(sent, 'dp', [(j, (j + k) % n_data) for j in range(n_data)])]
    all_to_all x1, waiting for transfers between devices: 20 us -> 0.01 us  [on_device(): lax.all_to_all(grad_here, 'dp', split_axis=0, concat_axis=1, tiled=True)]
    ppermute x0 -> x7, starting transfers between devices: none -> 9.14 us  [scatter_dp_permutes(): lax.ppermute(sent, 'dp', [(j, (j + k) % n_data) for j in range(n_data)])]
    dot_general x8, matrix products: 17.2 us -> 23.1 us  [dot_tn(): lax.dot_general(a, b, (((0,), (0,)), ((), ())), preferred_element_type=jn...]
    unnamed x203 -> x216, local copies, waits for them, and re-layouts: 30.7 us -> 34.1 us
  transfers between devices with their start and end apart: 24 -> 31, of which waited for: 18 -> 19; matrix products, arithmetic and copies ran while one was open for 23% -> 37% of each run, Pallas kernels for 0% -> 0%
where the time goes in v5:
time: 427 us; the launch traced here: 420 us
  waiting for transfers between devices  157 us (37%)
  matrix products  113 us (26%)
  local copies, waits for them, and re-layouts  57.4 us (13%)
  starting transfers between devices  39.8 us (9%)
  other arithmetic  36.6 us (9%)
  between operations  15.9 us (4%)
    ppermute x8, waiting for transfers between devices, to_chip_partner(): return lax.ppermute(value, 'tensor', across_chips)  86.5 us
    dot_general x8, matrix products, dot_nn(): return jnp.dot(a, b, preferred_element_type=jnp.float32)  40.7 us
    unnamed x216, local copies, waits for them, and re-layouts  34.1 us
    ppermute x7, waiting for transfers between devices, scatter_dp_permutes(): lax.ppermute(sent, 'dp', [(j, (j + k) % n_data) for j in range(n_data)])  31.1 us
    dot_general x8, matrix products, dot_tn(): lax.dot_general(a, b, (((0,), (0,)), ((), ())), preferred_element_type=jn...  23.1 us
    all_to_all x2, waiting for transfers between devices, deal(): here = lax.all_to_all(sent, 'dp', split_axis=1, concat_axis=0, tiled=True)  19.1 us
    all_gather x2, waiting for transfers between devices, gather_dp(): return lax.all_gather(block, 'dp', axis=0, tiled=True)  12.9 us
    convert_element_type x2, other arithmetic, attend_back(): grad_scores = (weights * (grad_weights - inner_sum)).astype(jnp.bfloat16)  12.5 us
  transfers between devices with their start and end apart: 31, of which 19 were waited for; matrix products, arithmetic and copies ran while one was open for 37% of the time, Pallas kernels for 0%

profile of v5, /device:TPU:12, one launch (start us, length us, event | category | flops | bytes accessed | tf_op | source)
XLA Modules:
  0.0 420.3 jit_solution(8091369660859109881)
XLA Ops:
  10.6 6.4 %all-to-all-start = ((bf16[32,16,768]{2,0,1:T(8,128)(2,1)}), bf16[32,16,768]{2,0,1:T(8,128)(2,1)S(1)}, u32[]{:S(2)}, u32[]{:S(2)}) async-start(bf16[32,16,768]{2,0,1:T(8,128)(2,1)} %copy.99), calls=%async_computation | async-start | bytes 1572864 | tf_op jit(solution)/shard_map/all_to_all | solution.py:127
  17.9 19.1 %all-to-all-done = bf16[32,16,768]{2,0,1:T(8,128)(2,1)S(1)} async-done(((bf16[32,16,768]{2,0,1:T(8,128)(2,1)}), bf16[32,16,768]{2,0,1:T(8,128)(2,1)S(1)}, u32[]{:S(2)}, u32[]{:S(2)}) %all-to-all-start) | async-done | bytes 786464 | tf_op jit(solution)/shard_map/all_to_all | solution.py:127
  38.7 9.2 %collective-permute-done = bf16[256,768]{1,0:T(8,128)(2,1)S(1)} collective-permute-done((bf16[256,768]{1,0:T(8,128)(2,1)S(1)}, bf16[256,768]{1,0:T(8,128)(2,1)S(1)}, u32[]{:S(2)}, u32[]{:S(2)}) %collective-permute-start) | collective-permute-done | bytes 393248 | tf_op jit(solution)/shard_map/ppermute | solution.py:86
  50.3 11.4 %all-gather.3.cloned.1.call-done = bf16[768,768]{1,0:T(8,128)(2,1)} async-done(((bf16[96,768]{1,0:T(8,128)(2,1)}), bf16[768,768]{1,0:T(8,128)(2,1)}) %all-gather.3.cloned.1.call-update) | async-done | bytes 1179664 | tf_op jit(solution)/shard_map/all_gather | solution.py:92
  63.2 2.6 add_convert_fusion.3
  70.1 2.9 copy-done.2
  77.5 11.3 %collective-permute-done.2 = bf16[768,768]{1,0:T(8,128)(2,1)S(1)} collective-permute-done((bf16[768,768]{1,0:T(8,128)(2,1)}, bf16[768,768]{1,0:T(8,128)(2,1)S(1)}, u32[]{:S(2)}, u32[]{:S(2)}) %collective-permute-start.2) | collective-permute-done | bytes 1179680 | tf_op jit(solution)/shard_map/ppermute | solution.py:86
  88.8 2.7 add_convert_fusion.2
  95.8 2.9 copy-done.3
  108.2 5.3 %all-to-all-start.1 = ((bf16[32,16,768]{2,0,1:T(8,128)(2,1)}), bf16[32,16,768]{2,0,1:T(8,128)(2,1)S(1)}, u32[]{:S(2)}, u32[]{:S(2)}) async-start(bf16[32,16,768]{2,0,1:T(8,128)(2,1)} %copy.104), calls=%async_computation.1 | async-start | bytes 1572864 | tf_op jit(solution)/shard_map/all_to_all | solution.py:127
  117.2 11.5 %multiply_convert_fusion.3 = (bf16[1024,768]{1,0:T(8,128)(2,1)S(1)}, f32[1024,768]{1,0:T(8,128)}, f32[1024,768]{1,0:T(8,128)}) fusion(f32[768]{0:T(1024)S(1)} %get-tuple-element.133, bf16[768,1536]{1,0:T(8,128)(2,1)} %all-gather.5.cloned.1.call-done, bf16[512,768]{1,0:T(8,128)(2,1)} %collective-permute-done.4, bf16[512,768]{1,0:T(8,128)(2,1)} %fusion.42), kind=kOutput, calls=%fused_computation.43 | convolution fusion | flops 1263009792 | bytes 10619904 | tf_op jit(solution)/shard_map/dot_general | solution.py:38
  130.2 37.6 %collective-permute-done.5 = bf16[768,1536]{1,0:T(8,128)(2,1)S(1)} collective-permute-done((bf16[768,1536]{1,0:T(8,128)(2,1)}, bf16[768,1536]{1,0:T(8,128)(2,1)S(1)}, u32[]{:S(2)}, u32[]{:S(2)}) %collective-permute-start.5) | collective-permute-done | bytes 2359328 | tf_op jit(solution)/shard_map/ppermute | solution.py:86
  167.8 11.8 %multiply_convert_fusion.2 = (bf16[1024,768]{1,0:T(8,128)(2,1)S(1)}, f32[1024,768]{1,0:T(8,128)}, f32[1024,768]{1,0:T(8,128)}) fusion(f32[768]{0:T(1024)S(1)} %get-tuple-element.132, bf16[768,1536]{1,0:T(8,128)(2,1)S(1)} %collective-permute-done.5, bf16[512,768]{1,0:T(8,128)(2,1)} %collective-permute-done.4, bf16[512,768]{1,0:T(8,128)(2,1)} %fusion.42), kind=kOutput, calls=%fused_computation.30 | convolution fusion | flops 1263009792 | bytes 10620928 | tf_op jit(solution)/shard_map/dot_general | solution.py:38
  188.0 7.5 %collective-permute-done.8 = bf16[256,768]{1,0:T(8,128)(2,1)S(1)} collective-permute-done((bf16[256,768]{1,0:T(8,128)(2,1)S(1)}, bf16[256,768]{1,0:T(8,128)(2,1)S(1)}, u32[]{:S(2)}, u32[]{:S(2)}) %collective-permute-start.8) | collective-permute-done | bytes 393248 | tf_op jit(solution)/shard_map/ppermute | solution.py:86
  199.8 3.8 convert_reduce_fusion.1
  207.8 3.8 convert_reduce_fusion
  220.6 4.5 %fusion.41 = bf16[768,3466]{0,1:T(8,128)(2,1)} fusion(bf16[1024,768]{1,0:T(8,128)(2,1)} %copy-done.94, bf16[512,768]{1,0:T(8,128)(2,1)} %collective-permute-done.4, bf16[512,768]{1,0:T(8,128)(2,1)} %fusion.42), kind=kOutput, calls=%fused_computation.110 | convolution fusion | flops 1211695104 | bytes 4325376 | tf_op jit(solution)/shard_map/dot_general | solution.py:34
  235.1 4.0 fusion.39
  244.6 8.0 %copy.133 = bf16[768,3466]{1,0:T(8,128)(2,1)} copy(bf16[768,3466]{0,1:T(8,128)(2,1)} %fusion.94) | data formatting | bytes 10647552
  252.7 6.1 %multiply_reduce_fusion.1 = (f32[3,1024]{1,0:T(4,128)S(1)}, f32[3,1024,1024]{1,2,0:T(8,128)S(1)}) fusion(f32[3,1024,1024]{1,2,0:T(8,128)} %copy-done.2, f32[3,1024]{1,0:T(4,128)S(1)} %log_add_fusion.1, bf16[1024,3,64]{0,2,1:T(8,128)(2,1)S(1)} %bitcast.193, bf16[1024,3,64]{0,2,1:T(8,128)(2,1)S(1)} %bitcast.196), kind=kOutput, calls=%fused_computation.4 | convolution fusion | flops 412087296 | bytes 25976832 | tf_op jit(solution)/shard_map/qhe,khe->hqk/dot_general | solution.py:208
  260.9 5.4 %multiply_convert_fusion.1 = bf16[3,1024,1024]{1,2,0:T(8,128)(2,1)} fusion(f32[3,1024,1024]{1,2,0:T(8,128)S(1)} %get-tuple-element.161, f32[3,1024,1024]{1,2,0:T(8,128)S(1)} %bitcast.163, f32[3,1024]{1,0:T(4,128)S(1)} %get-tuple-element.160, f32[3,1024]{1,0:T(4,128)S(1)} %log_add_fusion.1), kind=kLoop, calls=%fused_computation.3 | loop fusion | flops 12582912 | bytes 31481856 | tf_op jit(solution)/shard_map/convert_element_type | solution.py:212
  266.4 4.2 fusion.46
  278.6 6.1 %multiply_reduce_fusion = (f32[3,1024]{1,0:T(4,128)S(1)}, f32[3,1024,1024]{1,2,0:T(8,128)}) fusion(f32[3,1024,1024]{1,2,0:T(8,128)S(1)} %bitcast.165, f32[3,1024]{1,0:T(4,128)S(1)} %log_add_fusion, bf16[1024,3,64]{0,2,1:T(8,128)(2,1)S(1)} %bitcast.191, bf16[1024,3,64]{0,2,1:T(8,128)(2,1)S(1)} %bitcast.198), kind=kOutput, calls=%fused_computation.1 | convolution fusion | flops 412087296 | bytes 25976832 | tf_op jit(solution)/shard_map/qhe,khe->hqk/dot_general | solution.py:208
  284.7 7.1 %multiply_convert_fusion = bf16[3,1024,1024]{1,2,0:T(8,128)(2,1)S(1)} fusion(f32[3,1024,1024]{1,2,0:T(8,128)} %get-tuple-element.163, f32[3,1024,1024]{1,2,0:T(8,128)S(1)} %bitcast.165, f32[3,1024]{1,0:T(4,128)S(1)} %get-tuple-element.162, f32[3,1024]{1,0:T(4,128)S(1)} %log_add_fusion), kind=kLoop, calls=%fused_computation | loop fusion | flops 12582912 | bytes 31481856 | tf_op jit(solution)/shard_map/convert_element_type | solution.py:212
  304.7 2.6 convolution_convert_fusion.4
  314.8 7.1 %collective-permute-done.14 = bf16[256,768]{1,0:T(8,128)(2,1)} collective-permute-done((bf16[256,768]{1,0:T(8,128)(2,1)}, bf16[256,768]{1,0:T(8,128)(2,1)}, u32[]{:S(2)}, u32[]{:S(2)}) %collective-permute-start.14) | collective-permute-done | bytes 393248 | tf_op jit(solution)/shard_map/ppermute | solution.py:86
  324.7 6.0 %all-to-all-start.2 = ((bf16[256,2,768]{2,1,0:T(2,128)(2,1)}), bf16[256,2,768]{2,1,0:T(2,128)(2,1)S(1)}, u32[]{:S(2)}, u32[]{:S(2)}) async-start(bf16[256,2,768]{2,1,0:T(2,128)(2,1)} %copy.113), calls=%async_computation.2 | async-start | bytes 1572864 | tf_op jit(solution)/shard_map/all_to_all | solution.py:380
  332.9 8.1 %collective-permute-done.16 = bf16[768,578]{0,1:T(8,128)(2,1)} collective-permute-done((bf16[768,578]{0,1:T(8,128)(2,1)}, bf16[768,578]{0,1:T(8,128)(2,1)}, u32[]{:S(2)}, u32[]{:S(2)}) %collective-permute-start.16) | collective-permute-done | bytes 887840 | tf_op jit(solution)/shard_map/ppermute | solution.py:86
  346.0 2.9 collective-permute-start.17
  356.0 25.3 %collective-permute-done.17 = bf16[96,578]{1,0:T(8,128)(2,1)S(1)} collective-permute-done((bf16[96,578]{1,0:T(8,128)(2,1)S(1)}, bf16[96,578]{1,0:T(8,128)(2,1)S(1)}, u32[]{:S(2)}, u32[]{:S(2)}) %collective-permute-start.17) | collective-permute-done | bytes 111008 | tf_op jit(solution)/shard_map/ppermute | solution.py:108
  381.3 3.4 collective-permute-done.18
  399.9 5.5 %collective-permute-done.24 = bf16[96,1738]{0,1:T(8,128)(2,1)} collective-permute-done((bf16[96,1738]{0,1:T(8,128)(2,1)S(1)}, bf16[96,1738]{0,1:T(8,128)(2,1)}, u32[]{:S(2)}, u32[]{:S(2)}) %collective-permute-start.24) | collective-permute-done | bytes 333728 | tf_op jit(solution)/shard_map/ppermute | solution.py:86
  (398 shorter events, 148.1 us)
Async XLA Ops:
  10.6 26.4 %all-to-all-start = ((bf16[32,16,768]{2,0,1:T(8,128)(2,1)}), bf16[32,16,768]{2,0,1:T(8,128)(2,1)S(1)}, u32[]{:S(2)}, u32[]{:S(2)}) async-start(bf16[32,16,768]{2,0,1:T(8,128)(2,1)} %copy.99), calls=%async_computation | async-start | bytes 1572864 | tf_op jit(solution)/shard_map/all_to_all | solution.py:127
  17.0 44.8 %all-gather.3.cloned.1.call-start = ((), (), s32[]{:S(2)}) async-start(), calls=%async_computation.4 | async-start | bytes 1327104 | tf_op jit(solution)/shard_map/all_gather | solution.py:92
  17.8 98.0 %all-gather.5.cloned.1.call-start = ((), (), s32[]{:S(2)}) async-start(), calls=%async_computation.5 | async-start | bytes 2654208 | tf_op jit(solution)/shard_map/all_gather | solution.py:92
  37.1 10.8 %collective-permute-start = (bf16[256,768]{1,0:T(8,128)(2,1)S(1)}, bf16[256,768]{1,0:T(8,128)(2,1)S(1)}, u32[]{:S(2)}, u32[]{:S(2)}) collective-permute-start(bf16[256,768]{1,0:T(8,128)(2,1)S(1)} %get-tuple-element.129), channel_id=1, source_target_pairs={{0,2},{1,3},{2,0},{3,1},{4,6},{5,7},{6,4},{7,5},{8,10},{9,11},{10,... | collective-permute-start | bytes 1179656 | tf_op jit(solution)/shard_map/ppermute | solution.py:86
  47.9 15.3 %collective-permute-start.1 = (bf16[512,768]{1,0:T(8,128)(2,1)S(1)}, bf16[512,768]{1,0:T(8,128)(2,1)}, u32[]{:S(2)}, u32[]{:S(2)}) collective-permute-start(bf16[512,768]{1,0:T(8,128)(2,1)S(1)} %pad_maximum_fusion.7), channel_id=1, source_target_pairs={{0,1},{1,0},{2,3},{3,2},{4,5},{5,4},{6,7},{7,6},{8,9},{9,8},{10,11... | collective-permute-start | bytes 2359304 | tf_op jit(solution)/shard_map/ppermute | solution.py:89
  61.8 27.1 %collective-permute-start.2 = (bf16[768,768]{1,0:T(8,128)(2,1)}, bf16[768,768]{1,0:T(8,128)(2,1)S(1)}, u32[]{:S(2)}, u32[]{:S(2)}) collective-permute-start(bf16[768,768]{1,0:T(8,128)(2,1)} %all-gather.3.cloned.1.call-done), channel_id=1, source_target_pairs={{0,2},{1,3},{2,0},{3,1},{4,6},{5,7},{6,4},{7,5},{8,10},{9,11},{10,... | collective-permute-start | bytes 3538952 | tf_op jit(solution)/shard_map/ppermute | solution.py:86
  102.1 2.4 collective-permute-start.3
  106.4 10.8 %collective-permute-start.4 = (bf16[512,768]{1,0:T(8,128)(2,1)}, bf16[512,768]{1,0:T(8,128)(2,1)}, u32[]{:S(2)}, u32[]{:S(2)}) collective-permute-start(bf16[512,768]{1,0:T(8,128)(2,1)} %fusion.42), channel_id=1, source_target_pairs={{0,1},{1,0},{2,3},{3,2},{4,5},{5,4},{6,7},{7,6},{8,9},{9,8},{10,11... | collective-permute-start | bytes 2359304 | tf_op jit(solution)/shard_map/ppermute | solution.py:89
  108.2 75.6 %all-to-all-start.1 = ((bf16[32,16,768]{2,0,1:T(8,128)(2,1)}), bf16[32,16,768]{2,0,1:T(8,128)(2,1)S(1)}, u32[]{:S(2)}, u32[]{:S(2)}) async-start(bf16[32,16,768]{2,0,1:T(8,128)(2,1)} %copy.104), calls=%async_computation.1 | async-start | bytes 1572864 | tf_op jit(solution)/shard_map/all_to_all | solution.py:127
  113.4 279.4 %reduce-scatter.4.cloned.1.call-start = ((), (), s32[]{:S(2)}) async-start(), calls=%async_computation.6 | async-start | bytes 6193152
  115.8 52.1 %collective-permute-start.5 = (bf16[768,1536]{1,0:T(8,128)(2,1)}, bf16[768,1536]{1,0:T(8,128)(2,1)S(1)}, u32[]{:S(2)}, u32[]{:S(2)}) collective-permute-start(bf16[768,1536]{1,0:T(8,128)(2,1)} %all-gather.5.cloned.1.call-done), channel_id=1, source_target_pairs={{0,2},{1,3},{2,0},{3,1},{4,6},{5,7},{6,4},{7,5},{8,10},{9,11},{10,... | collective-permute-start | bytes 7077896 | tf_op jit(solution)/shard_map/ppermute | solution.py:86
  183.8 2.5 collective-permute-start.6
  183.9 11.6 %collective-permute-start.8 = (bf16[256,768]{1,0:T(8,128)(2,1)S(1)}, bf16[256,768]{1,0:T(8,128)(2,1)S(1)}, u32[]{:S(2)}, u32[]{:S(2)}) collective-permute-start(bf16[256,768]{1,0:T(8,128)(2,1)S(1)} %get-tuple-element.127), channel_id=1, source_target_pairs={{0,2},{1,3},{2,0},{3,1},{4,6},{5,7},{6,4},{7,5},{8,10},{9,11},{10,... | collective-permute-start | bytes 1179656 | tf_op jit(solution)/shard_map/ppermute | solution.py:86
  197.0 115.6 %copy-start.21 = (bf16[512,768]{1,0:T(8,128)(2,1)}, bf16[512,768]{1,0:T(8,128)(2,1)S(1)}, u32[]{:S(2)}) copy-start(bf16[512,768]{1,0:T(8,128)(2,1)S(1)} %get-tuple-element.106) | copy-start | bytes 2359300
  197.1 2.4 collective-permute-start.9
  213.1 2.4 collective-permute-start.10
  219.3 9.0 %collective-permute-start.11 = (bf16[512,768]{1,0:T(8,128)(2,1)S(1)}, bf16[512,768]{1,0:T(8,128)(2,1)}, u32[]{:S(2)}, u32[]{:S(2)}) collective-permute-start(bf16[512,768]{1,0:T(8,128)(2,1)S(1)} %convert_element_type.192), channel_id=1, source_target_pairs={{0,1},{1,0},{2,3},{3,2},{4,5},{5,4},{6,7},{7,6},{8,9},{9,8},{10,11... | collective-permute-start | bytes 2359304 | tf_op jit(solution)/shard_map/ppermute | solution.py:89
  227.9 16.1 %collective-permute-start.12 = (f32[768,10]{0,1:T(8,128)S(1)}, f32[768,10]{0,1:T(8,128)S(1)}, u32[]{:S(2)}, u32[]{:S(2)}) collective-permute-start(f32[768,10]{0,1:T(8,128)S(1)} %concatenate.63), channel_id=1, source_target_pairs={{0,1},{1,0},{2,3},{3,2},{4,5},{5,4},{6,7},{7,6},{8,9},{9,8},{10,11... | collective-permute-start | bytes 92168 | tf_op jit(solution)/shard_map/ppermute | solution.py:89
  301.3 6.0 %collective-permute-start.13 = (bf16[512,768]{1,0:T(8,128)(2,1)}, bf16[512,768]{1,0:T(8,128)(2,1)}, u32[]{:S(2)}, u32[]{:S(2)}) collective-permute-start(bf16[512,768]{1,0:T(8,128)(2,1)} %slice.318), channel_id=1, source_target_pairs={{0,1},{1,0},{2,3},{3,2},{4,5},{5,4},{6,7},{7,6},{8,9},{9,8},{10,11... | collective-permute-start | bytes 2359304 | tf_op jit(solution)/shard_map/ppermute | solution.py:89
  304.0 6.9 %collective-permute-start.15 = (f32[768,2]{0,1:T(2,128)S(1)}, f32[768,2]{0,1:T(2,128)S(1)}, u32[]{:S(2)}, u32[]{:S(2)}) collective-permute-start(f32[768,2]{0,1:T(2,128)S(1)} %pad_maximum_fusion.13), channel_id=1, source_target_pairs={{0,1},{1,0},{2,3},{3,2},{4,5},{5,4},{6,7},{7,6},{8,9},{9,8},{10,11... | collective-permute-start | bytes 18440 | tf_op jit(solution)/shard_map/ppermute | solution.py:89
  309.6 12.3 %collective-permute-start.14 = (bf16[256,768]{1,0:T(8,128)(2,1)}, bf16[256,768]{1,0:T(8,128)(2,1)}, u32[]{:S(2)}, u32[]{:S(2)}) collective-permute-start(bf16[256,768]{1,0:T(8,128)(2,1)} %slice.233), channel_id=1, source_target_pairs={{0,2},{1,3},{2,0},{3,1},{4,6},{5,7},{6,4},{7,5},{8,10},{9,11},{10,... | collective-permute-start | bytes 1179656 | tf_op jit(solution)/shard_map/ppermute | solution.py:86
  312.0 29.1 %collective-permute-start.16 = (bf16[768,578]{0,1:T(8,128)(2,1)}, bf16[768,578]{0,1:T(8,128)(2,1)}, u32[]{:S(2)}, u32[]{:S(2)}) collective-permute-start(bf16[768,578]{0,1:T(8,128)(2,1)} %pad_maximum_fusion.6), channel_id=1, source_target_pairs={{0,2},{1,3},{2,0},{3,1},{4,6},{5,7},{6,4},{7,5},{8,10},{9,11},{10,... | collective-permute-start | bytes 2663432 | tf_op jit(solution)/shard_map/ppermute | solution.py:86
  313.4 35.6 %collective-permute-start.7 = (bf16[256,768]{1,0:T(8,128)(2,1)}, bf16[256,768]{1,0:T(8,128)(2,1)}, u32[]{:S(2)}, u32[]{:S(2)}) collective-permute-start(bf16[256,768]{1,0:T(8,128)(2,1)} %slice.227), channel_id=1, source_target_pairs={{0,2},{1,3},{2,0},{3,1},{4,6},{5,7},{6,4},{7,5},{8,10},{9,11},{10,... | collective-permute-start | bytes 1179656 | tf_op jit(solution)/shard_map/ppermute | solution.py:86
  324.7 72.9 %all-to-all-start.2 = ((bf16[256,2,768]{2,1,0:T(2,128)(2,1)}), bf16[256,2,768]{2,1,0:T(2,128)(2,1)S(1)}, u32[]{:S(2)}, u32[]{:S(2)}) async-start(bf16[256,2,768]{2,1,0:T(2,128)(2,1)} %copy.113), calls=%async_computation.2 | async-start | bytes 1572864 | tf_op jit(solution)/shard_map/all_to_all | solution.py:380
  346.0 35.3 %collective-permute-start.17 = (bf16[96,578]{1,0:T(8,128)(2,1)S(1)}, bf16[96,578]{1,0:T(8,128)(2,1)S(1)}, u32[]{:S(2)}, u32[]{:S(2)}) collective-permute-start(bf16[96,578]{1,0:T(8,128)(2,1)S(1)} %get-tuple-element.117), channel_id=1, source_target_pairs={{0,4},{4,8},{8,12},{12,16},{16,20},{20,24},{24,28},{28,0},{1,5},{5... | collective-permute-start | bytes 332936 | tf_op jit(solution)/shard_map/ppermute | solution.py:108
  348.8 35.8 %collective-permute-start.18 = (bf16[96,578]{1,0:T(8,128)(2,1)S(1)}, bf16[96,578]{1,0:T(8,128)(2,1)S(1)}, u32[]{:S(2)}, u32[]{:S(2)}) collective-permute-start(bf16[96,578]{1,0:T(8,128)(2,1)S(1)} %get-tuple-element.123), channel_id=1, source_target_pairs={{0,8},{4,12},{8,16},{12,20},{16,24},{20,28},{24,0},{28,4},{1,9},{5... | collective-permute-start | bytes 332936 | tf_op jit(solution)/shard_map/ppermute | solution.py:108
  350.2 38.4 %collective-permute-start.19 = (bf16[96,578]{1,0:T(8,128)(2,1)}, bf16[96,578]{1,0:T(8,128)(2,1)S(1)}, u32[]{:S(2)}, u32[]{:S(2)}) collective-permute-start(bf16[96,578]{1,0:T(8,128)(2,1)} %get-tuple-element.122), channel_id=1, source_target_pairs={{0,12},{4,16},{8,20},{12,24},{16,28},{20,0},{24,4},{28,8},{1,13},{... | collective-permute-start | bytes 332936 | tf_op jit(solution)/shard_map/ppermute | solution.py:108
  352.1 36.9 %collective-permute-start.20 = (bf16[96,578]{1,0:T(8,128)(2,1)}, bf16[96,578]{1,0:T(8,128)(2,1)S(1)}, u32[]{:S(2)}, u32[]{:S(2)}) collective-permute-start(bf16[96,578]{1,0:T(8,128)(2,1)} %get-tuple-element.121), channel_id=1, source_target_pairs={{0,16},{4,20},{8,24},{12,28},{16,0},{20,4},{24,8},{28,12},{1,17},{... | collective-permute-start | bytes 332936 | tf_op jit(solution)/shard_map/ppermute | solution.py:108
  354.0 35.1 %collective-permute-start.21 = (bf16[96,578]{1,0:T(8,128)(2,1)}, bf16[96,578]{1,0:T(8,128)(2,1)S(1)}, u32[]{:S(2)}, u32[]{:S(2)}) collective-permute-start(bf16[96,578]{1,0:T(8,128)(2,1)} %get-tuple-element.120), channel_id=1, source_target_pairs={{0,20},{4,24},{8,28},{12,0},{16,4},{20,8},{24,12},{28,16},{1,21},{... | collective-permute-start | bytes 332936 | tf_op jit(solution)/shard_map/ppermute | solution.py:108
  381.3 9.6 %collective-permute-start.22 = (bf16[96,578]{1,0:T(8,128)(2,1)}, bf16[96,578]{1,0:T(8,128)(2,1)S(1)}, u32[]{:S(2)}, u32[]{:S(2)}) collective-permute-start(bf16[96,578]{1,0:T(8,128)(2,1)} %get-tuple-element.119), channel_id=1, source_target_pairs={{0,24},{4,28},{8,0},{12,4},{16,8},{20,12},{24,16},{28,20},{1,25},{... | collective-permute-start | bytes 332936 | tf_op jit(solution)/shard_map/ppermute | solution.py:108
  384.7 6.3 %collective-permute-start.23 = (bf16[96,578]{1,0:T(8,128)(2,1)}, bf16[96,578]{1,0:T(8,128)(2,1)S(1)}, u32[]{:S(2)}, u32[]{:S(2)}) collective-permute-start(bf16[96,578]{1,0:T(8,128)(2,1)} %get-tuple-element.118), channel_id=1, source_target_pairs={{0,28},{4,0},{8,4},{12,8},{16,12},{20,16},{24,20},{28,24},{1,29},{... | collective-permute-start | bytes 332936 | tf_op jit(solution)/shard_map/ppermute | solution.py:108
  394.8 10.6 %collective-permute-start.24 = (bf16[96,1738]{0,1:T(8,128)(2,1)S(1)}, bf16[96,1738]{0,1:T(8,128)(2,1)}, u32[]{:S(2)}, u32[]{:S(2)}) collective-permute-start(bf16[96,1738]{0,1:T(8,128)(2,1)S(1)} %slice.238), channel_id=1, source_target_pairs={{0,2},{1,3},{2,0},{3,1},{4,6},{5,7},{6,4},{7,5},{8,10},{9,11},{10,... | collective-permute-start | bytes 1001096 | tf_op jit(solution)/shard_map/ppermute | solution.py:86
  (104 other events, 945.4 us)
Sparse Core Ops, SparseCore 0:
  20.5 41.1 all-gather.2
  64.5 51.1 all-gather.4
  252.8 130.8 reduce-scatter.3

commit v6 on v5

--- a/solution.py
+++ b/solution.py
@@ -4,6 +4,7 @@
 import jax.numpy as jnp
 from jax import lax
 from jax.sharding import PartitionSpec as P
+
 
 HD = 64
 
@@ -77,7 +78,6 @@
     score_scale = HD ** (-0.5)
 
     chip_side = tensor_index // 2
-    core = tensor_index % 2
     partner_slice = tensor_index ^ 2
     across_chips = [(k, k ^ 2) for k in range(n_tensor)]
     across_cores = [(k, k ^ 1) for k in range(n_tensor)]
@@ -95,6 +95,17 @@
         return lax.psum_scatter(
             total.astype(jnp.bfloat16), "dp", scatter_dimension=0, tiled=True
         ).astype(jnp.float32)
+
+    def gather_dp_permutes(block):
+        if n_data > 8:
+            return gather_dp(block)
+        got = [block] + [
+            lax.ppermute(block, "dp", [(j, (j + k) % n_data) for j in range(n_data)])
+            for k in range(1, n_data)
+        ]
+        stacked = jnp.stack(got)
+        ordered = jnp.take(stacked, (data_index - jnp.arange(n_data)) % n_data, axis=0)
+        return ordered.reshape(n_data * block.shape[0], *block.shape[1:])
 
     def scatter_dp_permutes(total):
         if n_data > 8:
@@ -120,6 +131,7 @@
 
     slot_ids = jnp.arange(seq_total, dtype=jnp.int32)
     placing = (dealing[None, :] == slot_ids[:, None]).astype(jnp.bfloat16)
+
     def deal(values):
         sent = jnp.einsum(
             "qs,psd->pqd", placing, values, preferred_element_type=jnp.float32
@@ -151,9 +163,9 @@
 
     attn_w = jnp.concatenate([project_weight, attention_output_weight], axis=1)
     feed_w = jnp.concatenate([feed_input_weight, feed_output_weight], axis=1)
-    attn_own = gather_dp(attn_w)
+    attn_own = gather_dp_permutes(attn_w)
+    attn_part = to_chip_partner(attn_own)
     feed_own = gather_dp(feed_w)
-    attn_part = to_chip_partner(attn_own)
     feed_part = to_chip_partner(feed_own)
     slices = (tensor_index, partner_slice)
     attn_sets = (attn_own, attn_part)
@@ -331,8 +343,15 @@
     down_shard = early_shard[:, hidden_cols : 2 * hidden_cols]
     output_shard = early_shard[:, 2 * hidden_cols :]
 
-    grad_projected = [attend_back(projected[g], log_total[g], grad_mixed[g]) for g in groups]
-    project_grads = [dot_tn(inputs_full, grad_projected[g]) for g in groups]
+    grad_projected = [None, None]
+    grad_projected[1] = attend_back(projected[1], log_total[1], grad_mixed[1])
+    partner_project_grad = dot_tn(inputs_full, grad_projected[1])
+    partner_low, own_grad_mixed = lax.optimization_barrier(
+        (partner_project_grad.astype(jnp.bfloat16), grad_mixed[0])
+    )
+    crossed_project_grad = to_chip_partner(partner_low)
+    grad_projected[0] = attend_back(projected[0], log_total[0], own_grad_mixed)
+    own_project_grad = dot_tn(inputs_full, grad_projected[0])
     qkv_bias_sums = [jnp.sum(grad_projected[g], axis=0, dtype=jnp.float32) for g in groups]
     grad_inputs = grad_residual + scatter_cores(
         sum(dot_nt(grad_projected[g], project_ws[g]) for g in groups)
@@ -346,18 +365,20 @@
         axis=1,
     )
     late_columns = late_columns + to_core_partner(late_columns)
-    late_own = jnp.concatenate([project_grads[0], late_columns], axis=1)
-    late_partner = jnp.concatenate([project_grads[1], late_columns], axis=1)
-    late_total = late_own + to_chip_partner(late_partner.astype(jnp.bfloat16)).astype(jnp.float32)
+    late_total = jnp.concatenate(
+        [own_project_grad + crossed_project_grad.astype(jnp.float32), late_columns], axis=1
+    )
     late_shard = scatter_dp_permutes(late_total)
     project_shard = late_shard[:, :project_cols]
+    late_small = late_shard[:, project_cols:]
+    late_small = late_small + to_chip_partner(late_small)
 
     def mine_of(column):
         return lax.dynamic_slice_in_dim(column, tensor_index * vec_block, vec_block)
 
     early = [mine_of(early_small[:, k]) for k in range(6)]
     up_bias_shard = lax.dynamic_index_in_dim(early_small[:, 6:], tensor_index, axis=1, keepdims=False)
-    late = [mine_of(late_shard[:, project_cols + k]) for k in range(2)]
+    late = [mine_of(late_small[:, k]) for k in range(2)]
     small = [
         late[0],
         late[1],
@@ -438,6 +459,7 @@
         P(("dp", "tensor")),
         P(("dp", "tensor")),
     )
+
     return jax.shard_map(
         on_device, mesh=mesh, in_specs=in_specs, out_specs=out_specs, check_vma=False
     )

time: 427 us -> 455 us (1.066)
  waiting for transfers between devices: 157 us -> 175 us
  local copies, waits for them, and re-layouts: 57.4 us -> 51.8 us
  matrix products: 113 us -> 118 us
  starting transfers between devices: 39.8 us -> 44.8 us
  other arithmetic: 36.6 us -> 41.3 us
    ppermute x0 -> x7, waiting for transfers between devices: none -> 30.1 us  [gather_dp_permutes(): lax.ppermute(block, 'dp', [(j, (j + k) % n_data) for j in range(n_data)])]
    ppermute x8 -> x9, waiting for transfers between devices: 86.5 us -> 112 us  [to_chip_partner(): return lax.ppermute(value, 'tensor', across_chips)]
    all_to_all x2, waiting for transfers between devices: 19.1 us -> 0.01 us  [deal(): here = lax.all_to_all(sent, 'dp', split_axis=1, concat_axis=0, tiled=True)]
    all_gather x2 -> x1, waiting for transfers between devices: 12.9 us -> 0.01 us  [gather_dp(): return lax.all_gather(block, 'dp', axis=0, tiled=True)]
    ppermute x0 -> x7, starting transfers between devices: none -> 7.91 us  [gather_dp_permutes(): lax.ppermute(block, 'dp', [(j, (j + k) % n_data) for j in range(n_data)])]
    ppermute x7, waiting for transfers between devices: 31.1 us -> 25.2 us  [scatter_dp_permutes(): lax.ppermute(sent, 'dp', [(j, (j + k) % n_data) for j in range(n_data)])]
    unnamed x216 -> x198, local copies, waits for them, and re-layouts: 34.1 us -> 31 us
    ppermute x8 -> x9, starting transfers between devices: 10.9 us -> 11.4 us  [to_chip_partner(): return lax.ppermute(value, 'tensor', across_chips)]
  transfers between devices with their start and end apart: 31 -> 38, of which waited for: 19 -> 21; matrix products, arithmetic and copies ran while one was open for 37% -> 36% of each run, Pallas kernels for 0% -> 0%
where the time goes in v6:
time: 455 us; the launch traced here: 447 us
  waiting for transfers between devices  175 us (38%)
  matrix products  118 us (26%)
  local copies, waits for them, and re-layouts  51.8 us (11%)
  starting transfers between devices  44.8 us (10%)
  other arithmetic  41.3 us (9%)
  between operations  16 us (4%)
    ppermute x9, waiting for transfers between devices, to_chip_partner(): return lax.ppermute(value, 'tensor', across_chips)  112 us
    dot_general x8, matrix products, dot_nn(): return jnp.dot(a, b, preferred_element_type=jnp.float32)  39.6 us
    unnamed x198, local copies, waits for them, and re-layouts  31 us
    ppermute x7, waiting for transfers between devices, gather_dp_permutes(): lax.ppermute(block, 'dp', [(j, (j + k) % n_data) for j in range(n_data)])  30.1 us
    dot_general x8, matrix products, dot_tn(): lax.dot_general(a, b, (((0,), (0,)), ((), ())), preferred_element_type=jn...  26.2 us
    ppermute x7, waiting for transfers between devices, scatter_dp_permutes(): lax.ppermute(sent, 'dp', [(j, (j + k) % n_data) for j in range(n_data)])  25.2 us
    dot_general x2, matrix products, attend_back(): jnp.einsum('qhe,khe->hqk', grad_heads, value_rows, preferred_element_type...  13.2 us
    dot_general x8, matrix products, dot_nt(): lax.dot_general(a, b, (((1,), (1,)), ((), ())), preferred_element_type=jn...  12.6 us
  transfers between devices with their start and end apart: 38, of which 21 were waited for; matrix products, arithmetic and copies ran while one was open for 36% of the time, Pallas kernels for 0%

profile of v6, /device:TPU:12, one launch (start us, length us, event | category | flops | bytes accessed | tf_op | source)
XLA Modules:
  0.0 447.0 jit_solution(3911006042461675247)
XLA Ops:
  17.9 6.1 %all-to-all-start = ((bf16[32,16,768]{2,0,1:T(8,128)(2,1)}), bf16[32,16,768]{2,0,1:T(8,128)(2,1)S(1)}, u32[]{:S(2)}, u32[]{:S(2)}) async-start(bf16[32,16,768]{2,0,1:T(8,128)(2,1)} %copy.101), calls=%async_computation | async-start | bytes 1572864 | tf_op jit(solution)/shard_map/all_to_all | solution.py:139
  24.8 5.7 %collective-permute-done.3 = bf16[96,768]{1,0:T(8,128)(2,1)S(1)} collective-permute-done((bf16[96,768]{1,0:T(8,128)(2,1)S(1)}, bf16[96,768]{1,0:T(8,128)(2,1)S(1)}, u32[]{:S(2)}, u32[]{:S(2)}) %collective-permute-start.3) | collective-permute-done | bytes 147488 | tf_op jit(solution)/shard_map/ppermute | solution.py:103
  30.5 6.5 %collective-permute-done.4 = bf16[96,768]{1,0:T(8,128)(2,1)S(1)} collective-permute-done((bf16[96,768]{1,0:T(8,128)(2,1)S(1)}, bf16[96,768]{1,0:T(8,128)(2,1)S(1)}, u32[]{:S(2)}, u32[]{:S(2)}) %collective-permute-start.4) | collective-permute-done | bytes 147488 | tf_op jit(solution)/shard_map/ppermute | solution.py:103
  37.0 7.6 %collective-permute-done.5 = bf16[96,768]{1,0:T(8,128)(2,1)S(1)} collective-permute-done((bf16[96,768]{1,0:T(8,128)(2,1)S(1)}, bf16[96,768]{1,0:T(8,128)(2,1)S(1)}, u32[]{:S(2)}, u32[]{:S(2)}) %collective-permute-start.5) | collective-permute-done | bytes 147488 | tf_op jit(solution)/shard_map/ppermute | solution.py:103
  44.7 9.2 %collective-permute-done.7 = bf16[96,768]{1,0:T(8,128)(2,1)S(1)} collective-permute-done((bf16[96,768]{1,0:T(8,128)(2,1)S(1)}, bf16[96,768]{1,0:T(8,128)(2,1)S(1)}, u32[]{:S(2)}, u32[]{:S(2)}) %collective-permute-start.7) | collective-permute-done | bytes 147488 | tf_op jit(solution)/shard_map/ppermute | solution.py:103
  59.2 8.7 %collective-permute-done = bf16[256,768]{1,0:T(8,128)(2,1)S(1)} collective-permute-done((bf16[256,768]{1,0:T(8,128)(2,1)S(1)}, bf16[256,768]{1,0:T(8,128)(2,1)S(1)}, u32[]{:S(2)}, u32[]{:S(2)}) %collective-permute-start) | collective-permute-done | bytes 393248 | tf_op jit(solution)/shard_map/ppermute | solution.py:86
  70.4 21.9 %collective-permute-done.9 = bf16[768,768]{1,0:T(8,128)(2,1)S(1)} collective-permute-done((bf16[768,768]{1,0:T(8,128)(2,1)}, bf16[768,768]{1,0:T(8,128)(2,1)S(1)}, u32[]{:S(2)}, u32[]{:S(2)}) %collective-permute-start.9) | collective-permute-done | bytes 1179680 | tf_op jit(solution)/shard_map/ppermute | solution.py:86
  95.1 3.0 add_convert_fusion.3
  102.4 2.9 copy-done.3
  105.4 2.8 fusion.56
  112.4 2.9 copy-done.2
  126.6 4.2 all-to-all-start.1
  132.4 11.5 %multiply_convert_fusion.3 = (bf16[1024,768]{1,0:T(8,128)(2,1)S(1)}, f32[1024,768]{1,0:T(8,128)}, f32[1024,768]{1,0:T(8,128)}) fusion(f32[768]{0:T(1024)S(1)} %get-tuple-element.136, bf16[768,1536]{1,0:T(8,128)(2,1)} %all-gather.2.cloned.1.call-done, bf16[512,768]{1,0:T(8,128)(2,1)} %collective-permute-done.11, bf16[512,768]{1,0:T(8,128)(2,1)} %fusion.42), kind=kOutput, calls=%fused_computation.44 | convolution fusion | flops 1263009792 | bytes 10619904 | tf_op jit(solution)/shard_map/dot_general | solution.py:39
  145.4 38.7 %collective-permute-done.12 = bf16[768,1536]{1,0:T(8,128)(2,1)S(1)} collective-permute-done((bf16[768,1536]{1,0:T(8,128)(2,1)}, bf16[768,1536]{1,0:T(8,128)(2,1)S(1)}, u32[]{:S(2)}, u32[]{:S(2)}) %collective-permute-start.12) | collective-permute-done | bytes 2359328 | tf_op jit(solution)/shard_map/ppermute | solution.py:86
  184.1 11.6 %multiply_convert_fusion.2 = (bf16[1024,768]{1,0:T(8,128)(2,1)S(1)}, f32[1024,768]{1,0:T(8,128)}, f32[1024,768]{1,0:T(8,128)}) fusion(f32[768]{0:T(1024)S(1)} %get-tuple-element.135, bf16[768,1536]{1,0:T(8,128)(2,1)S(1)} %collective-permute-done.12, bf16[512,768]{1,0:T(8,128)(2,1)} %collective-permute-done.11, bf16[512,768]{1,0:T(8,128)(2,1)} %fusion.42), kind=kOutput, calls=%fused_computation.31 | convolution fusion | flops 1263009792 | bytes 10620928 | tf_op jit(solution)/shard_map/dot_general | solution.py:39
  204.6 6.9 %collective-permute-done.15 = bf16[256,768]{1,0:T(8,128)(2,1)S(1)} collective-permute-done((bf16[256,768]{1,0:T(8,128)(2,1)S(1)}, bf16[256,768]{1,0:T(8,128)(2,1)S(1)}, u32[]{:S(2)}, u32[]{:S(2)}) %collective-permute-start.15) | collective-permute-done | bytes 393248 | tf_op jit(solution)/shard_map/ppermute | solution.py:86
  216.4 3.2 convert_reduce_fusion.1
  223.7 3.2 convert_reduce_fusion
  235.0 4.5 %fusion.41 = bf16[768,3466]{0,1:T(8,128)(2,1)} fusion(bf16[1024,768]{1,0:T(8,128)(2,1)} %copy-done.82, bf16[512,768]{1,0:T(8,128)(2,1)} %collective-permute-done.11, bf16[512,768]{1,0:T(8,128)(2,1)} %fusion.42), kind=kOutput, calls=%fused_computation.119 | convolution fusion | flops 1211695104 | bytes 4325376 | tf_op jit(solution)/shard_map/dot_general | solution.py:35
  249.4 4.1 fusion.39
  259.0 8.0 %copy.137 = bf16[768,3466]{1,0:T(8,128)(2,1)} copy(bf16[768,3466]{0,1:T(8,128)(2,1)} %constant_dynamic-update-slice_fusion) | data formatting | bytes 10647552
  267.1 10.4 %multiply_reduce_fusion.1 = (f32[3,1024]{1,0:T(4,128)S(1)}, f32[3,1024,1024]{1,2,0:T(8,128)}) fusion(f32[3,1024,1024]{1,2,0:T(8,128)} %copy-done.3, f32[3,1024]{1,0:T(4,128)S(1)} %log_add_fusion, bf16[1024,3,64]{0,2,1:T(8,128)(2,1)S(1)} %bitcast.215, bf16[1024,3,64]{0,2,1:T(8,128)(2,1)S(1)} %bitcast.220), kind=kOutput, calls=%fused_computation.4 | convolution fusion | flops 412087296 | bytes 25976832 | tf_op jit(solution)/shard_map/qhe,khe->hqk/dot_general | solution.py:220
  279.8 6.9 %multiply_convert_fusion.1 = bf16[3,1024,1024]{1,2,0:T(8,128)(2,1)S(1)} fusion(f32[3,1024,1024]{1,2,0:T(8,128)} %get-tuple-element.164, f32[3,1024,1024]{1,2,0:T(8,128)S(1)} %bitcast.186, f32[3,1024]{1,0:T(4,128)S(1)} %get-tuple-element.163, f32[3,1024]{1,0:T(4,128)S(1)} %log_add_fusion), kind=kLoop, calls=%fused_computation.3 | loop fusion | flops 12582912 | bytes 31481856 | tf_op jit(solution)/shard_map/convert_element_type | solution.py:224
  292.2 3.8 convolution_convert_fusion.4
  298.8 5.5 %multiply_convert_fusion = bf16[3,1024,1024]{1,2,0:T(8,128)(2,1)} fusion(f32[3,1024,1024]{1,2,0:T(8,128)S(1)} %get-tuple-element.166, f32[3,1024,1024]{1,2,0:T(8,128)S(1)} %bitcast.184, f32[3,1024]{1,0:T(4,128)S(1)} %get-tuple-element.165, f32[3,1024]{1,0:T(4,128)S(1)} %log_add_fusion.1), kind=kLoop, calls=%fused_computation.1 | loop fusion | flops 12582912 | bytes 31481856 | tf_op jit(solution)/shard_map/convert_element_type | solution.py:224
  304.3 4.2 fusion.48
  329.9 4.2 collective-permute-done.14
  336.3 24.5 %collective-permute-done.21 = bf16[256,768]{1,0:T(8,128)(2,1)} collective-permute-done((bf16[256,768]{1,0:T(8,128)(2,1)S(1)}, bf16[256,768]{1,0:T(8,128)(2,1)}, u32[]{:S(2)}, u32[]{:S(2)}) %collective-permute-start.21) | collective-permute-done | bytes 393248 | tf_op jit(solution)/shard_map/ppermute | solution.py:86
  363.6 6.0 %all-to-all-start.2 = ((bf16[256,2,768]{2,1,0:T(2,128)(2,1)}), bf16[256,2,768]{2,1,0:T(2,128)(2,1)S(1)}, u32[]{:S(2)}, u32[]{:S(2)}) async-start(bf16[256,2,768]{2,1,0:T(2,128)(2,1)} %copy.115), calls=%async_computation.2 | async-start | bytes 1572864 | tf_op jit(solution)/shard_map/all_to_all | solution.py:401
  369.6 4.0 fusion.166
  384.3 17.3 %collective-permute-done.24 = bf16[96,578]{1,0:T(8,128)(2,1)S(1)} collective-permute-done((bf16[96,578]{1,0:T(8,128)(2,1)S(1)}, bf16[96,578]{1,0:T(8,128)(2,1)S(1)}, u32[]{:S(2)}, u32[]{:S(2)}) %collective-permute-start.24) | collective-permute-done | bytes 111008 | tf_op jit(solution)/shard_map/ppermute | solution.py:119
  424.7 7.3 %collective-permute-done.32 = bf16[96,1738]{0,1:T(8,128)(2,1)} collective-permute-done((bf16[96,1738]{0,1:T(8,128)(2,1)}, bf16[96,1738]{0,1:T(8,128)(2,1)}, u32[]{:S(2)}, u32[]{:S(2)}) %collective-permute-start.32) | collective-permute-done | bytes 333728 | tf_op jit(solution)/shard_map/ppermute | solution.py:86
  (404 shorter events, 163.6 us)
Async XLA Ops:
  8.3 15.9 %collective-permute-start.2 = (bf16[96,768]{1,0:T(8,128)(2,1)S(1)}, bf16[96,768]{1,0:T(8,128)(2,1)S(1)}, u32[]{:S(2)}, u32[]{:S(2)}) collective-permute-start(bf16[96,768]{1,0:T(8,128)(2,1)S(1)} %get-tuple-element.109), channel_id=1, source_target_pairs={{0,4},{4,8},{8,12},{12,16},{16,20},{20,24},{24,28},{28,0},{1,5},{5... | collective-permute-start | bytes 442376 | tf_op jit(solution)/shard_map/ppermute | solution.py:103
  9.9 20.7 %collective-permute-start.3 = (bf16[96,768]{1,0:T(8,128)(2,1)S(1)}, bf16[96,768]{1,0:T(8,128)(2,1)S(1)}, u32[]{:S(2)}, u32[]{:S(2)}) collective-permute-start(bf16[96,768]{1,0:T(8,128)(2,1)S(1)} %get-tuple-element.109), channel_id=1, source_target_pairs={{0,8},{4,12},{8,16},{12,20},{16,24},{20,28},{24,0},{28,4},{1,9},{5... | collective-permute-start | bytes 442376 | tf_op jit(solution)/shard_map/ppermute | solution.py:103
  11.4 25.6 %collective-permute-start.4 = (bf16[96,768]{1,0:T(8,128)(2,1)S(1)}, bf16[96,768]{1,0:T(8,128)(2,1)S(1)}, u32[]{:S(2)}, u32[]{:S(2)}) collective-permute-start(bf16[96,768]{1,0:T(8,128)(2,1)S(1)} %get-tuple-element.109), channel_id=1, source_target_pairs={{0,12},{4,16},{8,20},{12,24},{16,28},{20,0},{24,4},{28,8},{1,13},{... | collective-permute-start | bytes 442376 | tf_op jit(solution)/shard_map/ppermute | solution.py:103
  12.6 32.0 %collective-permute-start.5 = (bf16[96,768]{1,0:T(8,128)(2,1)S(1)}, bf16[96,768]{1,0:T(8,128)(2,1)S(1)}, u32[]{:S(2)}, u32[]{:S(2)}) collective-permute-start(bf16[96,768]{1,0:T(8,128)(2,1)S(1)} %get-tuple-element.109), channel_id=1, source_target_pairs={{0,16},{4,20},{8,24},{12,28},{16,0},{20,4},{24,8},{28,12},{1,17},{... | collective-permute-start | bytes 442376 | tf_op jit(solution)/shard_map/ppermute | solution.py:103
  14.3 30.4 %collective-permute-start.6 = (bf16[96,768]{1,0:T(8,128)(2,1)S(1)}, bf16[96,768]{1,0:T(8,128)(2,1)S(1)}, u32[]{:S(2)}, u32[]{:S(2)}) collective-permute-start(bf16[96,768]{1,0:T(8,128)(2,1)S(1)} %get-tuple-element.109), channel_id=1, source_target_pairs={{0,20},{4,24},{8,28},{12,0},{16,4},{20,8},{24,12},{28,16},{1,21},{... | collective-permute-start | bytes 442376 | tf_op jit(solution)/shard_map/ppermute | solution.py:103
  17.9 37.8 %all-to-all-start = ((bf16[32,16,768]{2,0,1:T(8,128)(2,1)}), bf16[32,16,768]{2,0,1:T(8,128)(2,1)S(1)}, u32[]{:S(2)}, u32[]{:S(2)}) async-start(bf16[32,16,768]{2,0,1:T(8,128)(2,1)} %copy.101), calls=%async_computation | async-start | bytes 1572864 | tf_op jit(solution)/shard_map/all_to_all | solution.py:139
  24.0 107.0 %all-gather.2.cloned.1.call-start = ((), (), s32[]{:S(2)}) async-start(), calls=%async_computation.4 | async-start | bytes 2654208 | tf_op jit(solution)/shard_map/all_gather | solution.py:92
  24.2 29.7 %collective-permute-start.7 = (bf16[96,768]{1,0:T(8,128)(2,1)S(1)}, bf16[96,768]{1,0:T(8,128)(2,1)S(1)}, u32[]{:S(2)}, u32[]{:S(2)}) collective-permute-start(bf16[96,768]{1,0:T(8,128)(2,1)S(1)} %get-tuple-element.109), channel_id=1, source_target_pairs={{0,24},{4,28},{8,0},{12,4},{16,8},{20,12},{24,16},{28,20},{1,25},{... | collective-permute-start | bytes 442376 | tf_op jit(solution)/shard_map/ppermute | solution.py:103
  30.5 24.5 %collective-permute-start.8 = (bf16[96,768]{1,0:T(8,128)(2,1)S(1)}, bf16[96,768]{1,0:T(8,128)(2,1)S(1)}, u32[]{:S(2)}, u32[]{:S(2)}) collective-permute-start(bf16[96,768]{1,0:T(8,128)(2,1)S(1)} %get-tuple-element.109), channel_id=1, source_target_pairs={{0,28},{4,0},{8,4},{12,8},{16,12},{20,16},{24,20},{28,24},{1,29},{... | collective-permute-start | bytes 442376 | tf_op jit(solution)/shard_map/ppermute | solution.py:103
  55.9 12.1 %collective-permute-start = (bf16[256,768]{1,0:T(8,128)(2,1)S(1)}, bf16[256,768]{1,0:T(8,128)(2,1)S(1)}, u32[]{:S(2)}, u32[]{:S(2)}) collective-permute-start(bf16[256,768]{1,0:T(8,128)(2,1)S(1)} %get-tuple-element.132), channel_id=1, source_target_pairs={{0,2},{1,3},{2,0},{3,1},{4,6},{5,7},{6,4},{7,5},{8,10},{9,11},{10,... | collective-permute-start | bytes 1179656 | tf_op jit(solution)/shard_map/ppermute | solution.py:86
  58.7 33.6 %collective-permute-start.9 = (bf16[768,768]{1,0:T(8,128)(2,1)}, bf16[768,768]{1,0:T(8,128)(2,1)S(1)}, u32[]{:S(2)}, u32[]{:S(2)}) collective-permute-start(bf16[768,768]{1,0:T(8,128)(2,1)} %bitcast_select_fusion), channel_id=1, source_target_pairs={{0,2},{1,3},{2,0},{3,1},{4,6},{5,7},{6,4},{7,5},{8,10},{9,11},{10,... | collective-permute-start | bytes 3538952 | tf_op jit(solution)/shard_map/ppermute | solution.py:86
  68.0 24.3 %collective-permute-start.1 = (bf16[512,768]{1,0:T(8,128)(2,1)S(1)}, bf16[512,768]{1,0:T(8,128)(2,1)}, u32[]{:S(2)}, u32[]{:S(2)}) collective-permute-start(bf16[512,768]{1,0:T(8,128)(2,1)S(1)} %pad_maximum_fusion.7), channel_id=1, source_target_pairs={{0,1},{1,0},{2,3},{3,2},{4,5},{5,4},{6,7},{7,6},{8,9},{9,8},{10,11... | collective-permute-start | bytes 2359304 | tf_op jit(solution)/shard_map/ppermute | solution.py:89
  124.9 7.6 %collective-permute-start.11 = (bf16[512,768]{1,0:T(8,128)(2,1)}, bf16[512,768]{1,0:T(8,128)(2,1)}, u32[]{:S(2)}, u32[]{:S(2)}) collective-permute-start(bf16[512,768]{1,0:T(8,128)(2,1)} %fusion.42), channel_id=1, source_target_pairs={{0,1},{1,0},{2,3},{3,2},{4,5},{5,4},{6,7},{7,6},{8,9},{9,8},{10,11... | collective-permute-start | bytes 2359304 | tf_op jit(solution)/shard_map/ppermute | solution.py:89
  126.6 73.2 %all-to-all-start.1 = ((bf16[32,16,768]{2,0,1:T(8,128)(2,1)}), bf16[32,16,768]{2,0,1:T(8,128)(2,1)S(1)}, u32[]{:S(2)}, u32[]{:S(2)}) async-start(bf16[32,16,768]{2,0,1:T(8,128)(2,1)} %copy.106), calls=%async_computation.1 | async-start | bytes 1572864 | tf_op jit(solution)/shard_map/all_to_all | solution.py:139
  130.8 286.4 %reduce-scatter.4.cloned.1.call-start = ((), (), s32[]{:S(2)}) async-start(), calls=%async_computation.5 | async-start | bytes 6193152
  130.9 53.2 %collective-permute-start.12 = (bf16[768,1536]{1,0:T(8,128)(2,1)}, bf16[768,1536]{1,0:T(8,128)(2,1)S(1)}, u32[]{:S(2)}, u32[]{:S(2)}) collective-permute-start(bf16[768,1536]{1,0:T(8,128)(2,1)} %all-gather.2.cloned.1.call-done), channel_id=1, source_target_pairs={{0,2},{1,3},{2,0},{3,1},{4,6},{5,7},{6,4},{7,5},{8,10},{9,11},{10,... | collective-permute-start | bytes 7077896 | tf_op jit(solution)/shard_map/ppermute | solution.py:86
  200.0 11.6 %collective-permute-start.15 = (bf16[256,768]{1,0:T(8,128)(2,1)S(1)}, bf16[256,768]{1,0:T(8,128)(2,1)S(1)}, u32[]{:S(2)}, u32[]{:S(2)}) collective-permute-start(bf16[256,768]{1,0:T(8,128)(2,1)S(1)} %get-tuple-element.130), channel_id=1, source_target_pairs={{0,2},{1,3},{2,0},{3,1},{4,6},{5,7},{6,4},{7,5},{8,10},{9,11},{10,... | collective-permute-start | bytes 1179656 | tf_op jit(solution)/shard_map/ppermute | solution.py:86
  233.5 9.1 %collective-permute-start.18 = (bf16[512,768]{1,0:T(8,128)(2,1)S(1)}, bf16[512,768]{1,0:T(8,128)(2,1)}, u32[]{:S(2)}, u32[]{:S(2)}) collective-permute-start(bf16[512,768]{1,0:T(8,128)(2,1)S(1)} %convert_element_type.193), channel_id=1, source_target_pairs={{0,1},{1,0},{2,3},{3,2},{4,5},{5,4},{6,7},{7,6},{8,9},{9,8},{10,11... | collective-permute-start | bytes 2359304 | tf_op jit(solution)/shard_map/ppermute | solution.py:89
  242.2 16.2 %collective-permute-start.19 = (f32[768,10]{0,1:T(8,128)S(1)}, f32[768,10]{0,1:T(8,128)S(1)}, u32[]{:S(2)}, u32[]{:S(2)}) collective-permute-start(f32[768,10]{0,1:T(8,128)S(1)} %concatenate.67), channel_id=1, source_target_pairs={{0,1},{1,0},{2,3},{3,2},{4,5},{5,4},{6,7},{7,6},{8,9},{9,8},{10,11... | collective-permute-start | bytes 92168 | tf_op jit(solution)/shard_map/ppermute | solution.py:89
  321.8 12.3 %collective-permute-start.14 = (bf16[256,768]{1,0:T(8,128)(2,1)}, bf16[256,768]{1,0:T(8,128)(2,1)}, u32[]{:S(2)}, u32[]{:S(2)}) collective-permute-start(bf16[256,768]{1,0:T(8,128)(2,1)} %slice.233), channel_id=1, source_target_pairs={{0,2},{1,3},{2,0},{3,1},{4,6},{5,7},{6,4},{7,5},{8,10},{9,11},{10,... | collective-permute-start | bytes 1179656 | tf_op jit(solution)/shard_map/ppermute | solution.py:86
  323.2 46.3 %collective-permute-start.22 = (bf16[768,576]{0,1:T(8,128)(2,1)}, bf16[768,576]{0,1:T(8,128)(2,1)}, u32[]{:S(2)}, u32[]{:S(2)}) collective-permute-start(bf16[768,576]{0,1:T(8,128)(2,1)} %convolution_convert_fusion.4), channel_id=1, source_target_pairs={{0,2},{1,3},{2,0},{3,1},{4,6},{5,7},{6,4},{7,5},{8,10},{9,11},{10,... | collective-permute-start | bytes 2654216 | tf_op jit(solution)/shard_map/ppermute | solution.py:86
  326.3 9.7 %collective-permute-start.23 = (f32[768,2]{0,1:T(2,128)S(1)}, f32[768,2]{0,1:T(2,128)S(1)}, u32[]{:S(2)}, u32[]{:S(2)}) collective-permute-start(f32[768,2]{0,1:T(2,128)S(1)} %pad_maximum_fusion.13), channel_id=1, source_target_pairs={{0,1},{1,0},{2,3},{3,2},{4,5},{5,4},{6,7},{7,6},{8,9},{9,8},{10,11... | collective-permute-start | bytes 18440 | tf_op jit(solution)/shard_map/ppermute | solution.py:89
  328.3 32.4 %collective-permute-start.21 = (bf16[256,768]{1,0:T(8,128)(2,1)S(1)}, bf16[256,768]{1,0:T(8,128)(2,1)}, u32[]{:S(2)}, u32[]{:S(2)}) collective-permute-start(bf16[256,768]{1,0:T(8,128)(2,1)S(1)} %slice.239), channel_id=1, source_target_pairs={{0,2},{1,3},{2,0},{3,1},{4,6},{5,7},{6,4},{7,5},{8,10},{9,11},{10,... | collective-permute-start | bytes 1179656 | tf_op jit(solution)/shard_map/ppermute | solution.py:86
  363.6 58.9 %all-to-all-start.2 = ((bf16[256,2,768]{2,1,0:T(2,128)(2,1)}), bf16[256,2,768]{2,1,0:T(2,128)(2,1)S(1)}, u32[]{:S(2)}, u32[]{:S(2)}) async-start(bf16[256,2,768]{2,1,0:T(2,128)(2,1)} %copy.115), calls=%async_computation.2 | async-start | bytes 1572864 | tf_op jit(solution)/shard_map/all_to_all | solution.py:401
  375.9 25.6 %collective-permute-start.24 = (bf16[96,578]{1,0:T(8,128)(2,1)S(1)}, bf16[96,578]{1,0:T(8,128)(2,1)S(1)}, u32[]{:S(2)}, u32[]{:S(2)}) collective-permute-start(bf16[96,578]{1,0:T(8,128)(2,1)S(1)} %get-tuple-element.111), channel_id=1, source_target_pairs={{0,4},{4,8},{8,12},{12,16},{16,20},{20,24},{24,28},{28,0},{1,5},{5... | collective-permute-start | bytes 332936 | tf_op jit(solution)/shard_map/ppermute | solution.py:119
  377.4 26.8 %collective-permute-start.25 = (bf16[96,578]{1,0:T(8,128)(2,1)S(1)}, bf16[96,578]{1,0:T(8,128)(2,1)S(1)}, u32[]{:S(2)}, u32[]{:S(2)}) collective-permute-start(bf16[96,578]{1,0:T(8,128)(2,1)S(1)} %get-tuple-element.112), channel_id=1, source_target_pairs={{0,8},{4,12},{8,16},{12,20},{16,24},{20,28},{24,0},{28,4},{1,9},{5... | collective-permute-start | bytes 332936 | tf_op jit(solution)/shard_map/ppermute | solution.py:119
  378.9 28.0 %collective-permute-start.26 = (bf16[96,578]{1,0:T(8,128)(2,1)}, bf16[96,578]{1,0:T(8,128)(2,1)}, u32[]{:S(2)}, u32[]{:S(2)}) collective-permute-start(bf16[96,578]{1,0:T(8,128)(2,1)} %get-tuple-element.113), channel_id=1, source_target_pairs={{0,12},{4,16},{8,20},{12,24},{16,28},{20,0},{24,4},{28,8},{1,13},{... | collective-permute-start | bytes 332936 | tf_op jit(solution)/shard_map/ppermute | solution.py:119
  380.6 28.7 %collective-permute-start.27 = (bf16[96,578]{1,0:T(8,128)(2,1)S(1)}, bf16[96,578]{1,0:T(8,128)(2,1)}, u32[]{:S(2)}, u32[]{:S(2)}) collective-permute-start(bf16[96,578]{1,0:T(8,128)(2,1)S(1)} %get-tuple-element.114), channel_id=1, source_target_pairs={{0,16},{4,20},{8,24},{12,28},{16,0},{20,4},{24,8},{28,12},{1,17},{... | collective-permute-start | bytes 332936 | tf_op jit(solution)/shard_map/ppermute | solution.py:119
  382.0 27.3 %collective-permute-start.28 = (bf16[96,578]{1,0:T(8,128)(2,1)S(1)}, bf16[96,578]{1,0:T(8,128)(2,1)}, u32[]{:S(2)}, u32[]{:S(2)}) collective-permute-start(bf16[96,578]{1,0:T(8,128)(2,1)S(1)} %get-tuple-element.115), channel_id=1, source_target_pairs={{0,20},{4,24},{8,28},{12,0},{16,4},{20,8},{24,12},{28,16},{1,21},{... | collective-permute-start | bytes 332936 | tf_op jit(solution)/shard_map/ppermute | solution.py:119
  401.5 9.8 %collective-permute-start.29 = (bf16[96,578]{1,0:T(8,128)(2,1)S(1)}, bf16[96,578]{1,0:T(8,128)(2,1)S(1)}, u32[]{:S(2)}, u32[]{:S(2)}) collective-permute-start(bf16[96,578]{1,0:T(8,128)(2,1)S(1)} %get-tuple-element.116), channel_id=1, source_target_pairs={{0,24},{4,28},{8,0},{12,4},{16,8},{20,12},{24,16},{28,20},{1,25},{... | collective-permute-start | bytes 332936 | tf_op jit(solution)/shard_map/ppermute | solution.py:119
  404.2 7.2 %collective-permute-start.30 = (bf16[96,578]{1,0:T(8,128)(2,1)}, bf16[96,578]{1,0:T(8,128)(2,1)}, u32[]{:S(2)}, u32[]{:S(2)}) collective-permute-start(bf16[96,578]{1,0:T(8,128)(2,1)} %fusion.107), channel_id=1, source_target_pairs={{0,28},{4,0},{8,4},{12,8},{16,12},{20,16},{24,20},{28,24},{1,29},{... | collective-permute-start | bytes 332936 | tf_op jit(solution)/shard_map/ppermute | solution.py:119
  419.9 12.1 %collective-permute-start.32 = (bf16[96,1738]{0,1:T(8,128)(2,1)}, bf16[96,1738]{0,1:T(8,128)(2,1)}, u32[]{:S(2)}, u32[]{:S(2)}) collective-permute-start(bf16[96,1738]{0,1:T(8,128)(2,1)} %slice.245), channel_id=1, source_target_pairs={{0,2},{1,3},{2,0},{3,1},{4,6},{5,7},{6,4},{7,5},{8,10},{9,11},{10,... | collective-permute-start | bytes 1001096 | tf_op jit(solution)/shard_map/ppermute | solution.py:86
  (99 other events, 821.3 us)
Sparse Core Ops, SparseCore 0:
  69.0 50.0 all-gather.1
  267.2 110.5 reduce-scatter.3

commit v7 on v6

--- a/solution.py
+++ b/solution.py
@@ -96,17 +96,6 @@
             total.astype(jnp.bfloat16), "dp", scatter_dimension=0, tiled=True
         ).astype(jnp.float32)
 
-    def gather_dp_permutes(block):
-        if n_data > 8:
-            return gather_dp(block)
-        got = [block] + [
-            lax.ppermute(block, "dp", [(j, (j + k) % n_data) for j in range(n_data)])
-            for k in range(1, n_data)
-        ]
-        stacked = jnp.stack(got)
-        ordered = jnp.take(stacked, (data_index - jnp.arange(n_data)) % n_data, axis=0)
-        return ordered.reshape(n_data * block.shape[0], *block.shape[1:])
-
     def scatter_dp_permutes(total):
         if n_data > 8:
             return scatter_dp(total)
@@ -163,7 +152,7 @@
 
     attn_w = jnp.concatenate([project_weight, attention_output_weight], axis=1)
     feed_w = jnp.concatenate([feed_input_weight, feed_output_weight], axis=1)
-    attn_own = gather_dp_permutes(attn_w)
+    attn_own = gather_dp(attn_w)
     attn_part = to_chip_partner(attn_own)
     feed_own = gather_dp(feed_w)
     feed_part = to_chip_partner(feed_own)
@@ -285,7 +274,21 @@
     grad_preact = [gelu_pairs[g][1](grad_hidden[g])[0].astype(jnp.bfloat16) for g in groups]
     up_grads = [dot_tn(first_full, grad_preact[g]) for g in groups]
     up_bias_sums = [jnp.sum(grad_preact[g], axis=0, dtype=jnp.float32) for g in groups]
-    grad_first = grad_second + scatter_cores(sum(dot_nt(grad_preact[g], up_ws[g]) for g in groups))
+    feed_own_grad = jnp.concatenate([up_grads[0], down_grads[0]], axis=1)
+    feed_partner_grad = jnp.concatenate([up_grads[1], down_grads[1]], axis=1)
+    feed_cols = feed_own_grad.shape[1]
+    feed_pack = jnp.concatenate([feed_own_grad, feed_partner_grad], axis=1).astype(jnp.bfloat16)
+    first_partial = sum(dot_nt(grad_preact[g], up_ws[g]) for g in groups)
+    feed_pack, first_partial = lax.optimization_barrier((feed_pack, first_partial))
+    feed_reduced = lax.psum_scatter(
+        feed_pack, "dp", scatter_dimension=0, tiled=True
+    ).astype(jnp.float32)
+    feed_sent = to_chip_partner(feed_reduced[:, feed_cols:].astype(jnp.bfloat16))
+    feed_shard = feed_reduced[:, :feed_cols] + feed_sent.astype(jnp.float32)
+    up_shard = feed_shard[:, :hidden_cols]
+    down_shard = feed_shard[:, hidden_cols:]
+
+    grad_first = grad_second + scatter_cores(first_partial)
     first_gain_part = jnp.sum(grad_first * normed_first, axis=0)
     first_shift_part = jnp.sum(grad_first, axis=0)
     grad_residual = norm_backward(grad_first, normed_first, inverse_first, first_gain)
@@ -324,32 +327,15 @@
         axis=1,
     )
     early_columns = early_columns + to_core_partner(early_columns)
-    early_own = jnp.concatenate([up_grads[0], down_grads[0], output_grads[0]], axis=1)
-    early_partner = jnp.concatenate([up_grads[1], down_grads[1], output_grads[1]], axis=1)
-    early_cols = early_own.shape[1]
-    early_pack = jnp.concatenate([early_own, early_partner, early_columns], axis=1).astype(
-        jnp.bfloat16
-    )
-    early_pack, grad_mixed = lax.optimization_barrier((early_pack, grad_mixed))
-    early_reduced = lax.psum_scatter(
-        early_pack, "dp", scatter_dimension=0, tiled=True
-    ).astype(jnp.float32)
-    early_sent = to_chip_partner(early_reduced[:, early_cols:].astype(jnp.bfloat16)).astype(
-        jnp.float32
-    )
-    early_shard = early_reduced[:, :early_cols] + early_sent[:, :early_cols]
-    early_small = early_reduced[:, 2 * early_cols :] + early_sent[:, early_cols:]
-    up_shard = early_shard[:, :hidden_cols]
-    down_shard = early_shard[:, hidden_cols : 2 * hidden_cols]
-    output_shard = early_shard[:, 2 * hidden_cols :]
 
     grad_projected = [None, None]
     grad_projected[1] = attend_back(projected[1], log_total[1], grad_mixed[1])
     partner_project_grad = dot_tn(inputs_full, grad_projected[1])
-    partner_low, own_grad_mixed = lax.optimization_barrier(
-        (partner_project_grad.astype(jnp.bfloat16), grad_mixed[0])
-    )
-    crossed_project_grad = to_chip_partner(partner_low)
+    cross_pack = jnp.concatenate(
+        [partner_project_grad, output_grads[1], early_columns], axis=1
+    ).astype(jnp.bfloat16)
+    cross_pack, own_grad_mixed = lax.optimization_barrier((cross_pack, grad_mixed[0]))
+    crossed = to_chip_partner(cross_pack)
     grad_projected[0] = attend_back(projected[0], log_total[0], own_grad_mixed)
     own_project_grad = dot_tn(inputs_full, grad_projected[0])
     qkv_bias_sums = [jnp.sum(grad_projected[g], axis=0, dtype=jnp.float32) for g in groups]
@@ -366,11 +352,20 @@
     )
     late_columns = late_columns + to_core_partner(late_columns)
     late_total = jnp.concatenate(
-        [own_project_grad + crossed_project_grad.astype(jnp.float32), late_columns], axis=1
+        [
+            jnp.concatenate([own_project_grad, output_grads[0], early_columns], axis=1)
+            + crossed.astype(jnp.float32),
+            late_columns,
+        ],
+        axis=1,
     )
     late_shard = scatter_dp_permutes(late_total)
     project_shard = late_shard[:, :project_cols]
-    late_small = late_shard[:, project_cols:]
+    output_shard = late_shard[:, project_cols : project_cols + head_cols]
+    early_at = project_cols + head_cols
+    late_at = early_at + early_columns.shape[1]
+    early_small = late_shard[:, early_at:late_at]
+    late_small = late_shard[:, late_at:]
     late_small = late_small + to_chip_partner(late_small)
 
     def mine_of(column):

time: 455 us -> 442 us (0.971)
  the two profiles are of different devices: /device:TPU:12 before, /device:TPU:0 now
where the time goes in v7:
time: 442 us; the launch traced here: 435 us
  waiting for transfers between devices  160 us (36%)
  matrix products  111 us (25%)
  local copies, waits for them, and re-layouts  55.5 us (13%)
  other arithmetic  50.5 us (11%)
  starting transfers between devices  42.8 us (10%)
  between operations  15.6 us (4%)
    ppermute x9, waiting for transfers between devices, to_chip_partner(): return lax.ppermute(value, 'tensor', across_chips)  85.3 us
    dot_general x8, matrix products, dot_nn(): return jnp.dot(a, b, preferred_element_type=jnp.float32)  40.5 us
    ppermute x7, waiting for transfers between devices, scatter_dp_permutes(): lax.ppermute(sent, 'dp', [(j, (j + k) % n_data) for j in range(n_data)])  31.6 us
    unnamed x180, local copies, waits for them, and re-layouts  28.6 us
    all_to_all x2, waiting for transfers between devices, deal(): here = lax.all_to_all(sent, 'dp', split_axis=1, concat_axis=0, tiled=True)  22.6 us
    dot_general x8, matrix products, dot_tn(): lax.dot_general(a, b, (((0,), (0,)), ((), ())), preferred_element_type=jn...  20 us
    all_gather x2, waiting for transfers between devices, gather_dp(): return lax.all_gather(block, 'dp', axis=0, tiled=True)  14.5 us
    ppermute x7, starting transfers between devices, scatter_dp_permutes(): lax.ppermute(sent, 'dp', [(j, (j + k) % n_data) for j in range(n_data)])  14.4 us
  transfers between devices with their start and end apart: 32, of which 17 were waited for; matrix products, arithmetic and copies ran while one was open for 39% of the time, Pallas kernels for 0%

profile of v7, /device:TPU:0, one launch (start us, length us, event | category | flops | bytes accessed | tf_op | source)
XLA Modules:
  0.0 435.5 jit_solution(14519658223863351565)
XLA Ops:
  10.6 7.4 %all-to-all-start = ((bf16[32,16,768]{2,0,1:T(8,128)(2,1)}), bf16[32,16,768]{2,0,1:T(8,128)(2,1)S(1)}, u32[]{:S(2)}, u32[]{:S(2)}) async-start(bf16[32,16,768]{2,0,1:T(8,128)(2,1)} %copy.98), calls=%async_computation | async-start | bytes 1572864 | tf_op jit(solution)/shard_map/all_to_all | solution.py:128
  19.0 22.6 %all-to-all-done = bf16[32,16,768]{2,0,1:T(8,128)(2,1)S(1)} async-done(((bf16[32,16,768]{2,0,1:T(8,128)(2,1)}), bf16[32,16,768]{2,0,1:T(8,128)(2,1)S(1)}, u32[]{:S(2)}, u32[]{:S(2)}) %all-to-all-start) | async-done | bytes 786464 | tf_op jit(solution)/shard_map/all_to_all | solution.py:128
  43.2 7.1 %collective-permute-done = bf16[256,768]{1,0:T(8,128)(2,1)S(1)} collective-permute-done((bf16[256,768]{1,0:T(8,128)(2,1)S(1)}, bf16[256,768]{1,0:T(8,128)(2,1)S(1)}, u32[]{:S(2)}, u32[]{:S(2)}) %collective-permute-start) | collective-permute-done | bytes 393248 | tf_op jit(solution)/shard_map/ppermute | solution.py:86
  52.8 12.2 %all-gather.3.cloned.1.call-done = bf16[768,768]{1,0:T(8,128)(2,1)} async-done(((bf16[96,768]{1,0:T(8,128)(2,1)}), bf16[768,768]{1,0:T(8,128)(2,1)}) %all-gather.3.cloned.1.call-update) | async-done | bytes 1179664 | tf_op jit(solution)/shard_map/all_gather | solution.py:92
  81.1 10.6 %collective-permute-done.2 = bf16[768,768]{1,0:T(8,128)(2,1)S(1)} collective-permute-done((bf16[768,768]{1,0:T(8,128)(2,1)}, bf16[768,768]{1,0:T(8,128)(2,1)S(1)}, u32[]{:S(2)}, u32[]{:S(2)}) %collective-permute-start.2) | collective-permute-done | bytes 1179680 | tf_op jit(solution)/shard_map/ppermute | solution.py:86
  98.6 2.9 copy-done.3
  111.0 3.5 all-to-all-start.1
  119.9 11.5 %multiply_convert_fusion.3 = (bf16[1024,768]{1,0:T(8,128)(2,1)S(1)}, f32[1024,768]{1,0:T(8,128)}, f32[1024,768]{1,0:T(8,128)}) fusion(f32[768]{0:T(1024)} %get-tuple-element.144, bf16[768,1536]{1,0:T(8,128)(2,1)} %all-gather.5.cloned.1.call-done, bf16[512,768]{1,0:T(8,128)(2,1)} %collective-permute-done.4, bf16[512,768]{1,0:T(8,128)(2,1)} %fusion.37), kind=kOutput, calls=%fused_computation.51 | convolution fusion | flops 1263009792 | bytes 10620928 | tf_op jit(solution)/shard_map/dot_general | solution.py:39
  132.8 37.2 %collective-permute-done.5 = bf16[768,1536]{1,0:T(8,128)(2,1)S(1)} collective-permute-done((bf16[768,1536]{1,0:T(8,128)(2,1)}, bf16[768,1536]{1,0:T(8,128)(2,1)S(1)}, u32[]{:S(2)}, u32[]{:S(2)}) %collective-permute-start.5) | collective-permute-done | bytes 2359328 | tf_op jit(solution)/shard_map/ppermute | solution.py:86
  170.0 11.6 %multiply_convert_fusion.2 = (bf16[1024,768]{1,0:T(8,128)(2,1)S(1)}, f32[1024,768]{1,0:T(8,128)}, f32[1024,768]{1,0:T(8,128)}) fusion(f32[768]{0:T(1024)S(1)} %copy-done.67, bf16[768,1536]{1,0:T(8,128)(2,1)S(1)} %collective-permute-done.5, bf16[512,768]{1,0:T(8,128)(2,1)} %collective-permute-done.4, bf16[512,768]{1,0:T(8,128)(2,1)} %fusion.37), kind=kOutput, calls=%fused_computation.38 | convolution fusion | flops 1263009792 | bytes 10620928 | tf_op jit(solution)/shard_map/dot_general | solution.py:39
  190.5 6.9 %collective-permute-done.8 = bf16[256,768]{1,0:T(8,128)(2,1)S(1)} collective-permute-done((bf16[256,768]{1,0:T(8,128)(2,1)S(1)}, bf16[256,768]{1,0:T(8,128)(2,1)S(1)}, u32[]{:S(2)}, u32[]{:S(2)}) %collective-permute-start.8) | collective-permute-done | bytes 393248 | tf_op jit(solution)/shard_map/ppermute | solution.py:86
  207.6 3.8 convert_reduce_fusion
  211.4 3.0 convolution_convert_fusion.1
  215.4 3.8 convert_reduce_fusion.1
  232.6 3.6 multiply_reduce_fusion.2
  238.4 4.0 collective-permute-done.7
  248.0 6.6 %copy.133 = bf16[768,3072]{1,0:T(8,128)(2,1)} copy(bf16[768,3072]{0,1:T(8,128)(2,1)} %pad_maximum_fusion) | data formatting | bytes 9437184
  257.6 10.4 %multiply_reduce_fusion.1 = (f32[3,1024]{1,0:T(4,128)S(1)}, f32[3,1024,1024]{1,2,0:T(8,128)}) fusion(f32[3,1024,1024]{1,2,0:T(8,128)} %copy-done.3, f32[3,1024]{1,0:T(4,128)S(1)} %log_add_fusion, bf16[1024,3,64]{0,2,1:T(8,128)(2,1)S(1)} %bitcast.177, bf16[1024,3,64]{0,2,1:T(8,128)(2,1)S(1)} %bitcast.184), kind=kOutput, calls=%fused_computation.3 | convolution fusion | flops 412087296 | bytes 25976832 | tf_op jit(solution)/shard_map/qhe,khe->hqk/dot_general | solution.py:209
  270.3 6.9 %multiply_convert_fusion.1 = bf16[3,1024,1024]{1,2,0:T(8,128)(2,1)S(1)} fusion(f32[3,1024,1024]{1,2,0:T(8,128)} %get-tuple-element.166, f32[3,1024,1024]{1,2,0:T(8,128)S(1)} %bitcast.151, f32[3,1024]{1,0:T(4,128)S(1)} %get-tuple-element.165, f32[3,1024]{1,0:T(4,128)S(1)} %log_add_fusion), kind=kLoop, calls=%fused_computation.2 | loop fusion | flops 12582912 | bytes 31481856 | tf_op jit(solution)/shard_map/convert_element_type | solution.py:213
  284.4 3.0 convolution_convert_fusion.4
  293.7 5.5 %multiply_convert_fusion = bf16[3,1024,1024]{1,2,0:T(8,128)(2,1)} fusion(f32[3,1024,1024]{1,2,0:T(8,128)S(1)} %get-tuple-element.168, f32[3,1024,1024]{1,2,0:T(8,128)S(1)} %bitcast.149, f32[3,1024]{1,0:T(4,128)S(1)} %get-tuple-element.167, f32[3,1024]{1,0:T(4,128)S(1)} %log_add_fusion.1), kind=kLoop, calls=%fused_computation | loop fusion | flops 12582912 | bytes 31481856 | tf_op jit(solution)/shard_map/convert_element_type | solution.py:213
  299.2 5.1 %fusion.44 = bf16[3,64,1024]{2,1,0:T(8,128)(2,1)S(1)} fusion(bf16[1024,3,64]{0,2,1:T(8,128)(2,1)S(1)} %bitcast.157, bf16[3,1024,1024]{1,2,0:T(8,128)(2,1)} %multiply_convert_fusion), kind=kOutput, calls=%fused_computation.133 | convolution fusion | flops 403046400 | bytes 7077888 | tf_op jit(solution)/shard_map/hqk,qhe->khe/dot_general | solution.py:219
  319.2 3.6 fusion.126
  327.0 16.4 %collective-permute-done.15 = bf16[768,778]{0,1:T(8,128)(2,1)} collective-permute-done((bf16[768,778]{0,1:T(8,128)(2,1)}, bf16[768,778]{0,1:T(8,128)(2,1)}, u32[]{:S(2)}, u32[]{:S(2)}) %collective-permute-start.15) | collective-permute-done | bytes 1195040 | tf_op jit(solution)/shard_map/ppermute | solution.py:86
  343.4 3.2 fusion.127
  348.3 4.0 collective-permute-start.23
  357.8 4.2 all-to-all-start.2
  362.0 3.7 collective-permute-start.21
  375.4 4.3 collective-permute-done.21
  379.8 22.8 %collective-permute-done.20 = bf16[96,780]{1,0:T(8,128)(2,1)S(1)} collective-permute-done((bf16[96,780]{1,0:T(8,128)(2,1)}, bf16[96,780]{1,0:T(8,128)(2,1)S(1)}, u32[]{:S(2)}, u32[]{:S(2)}) %collective-permute-start.20) | collective-permute-done | bytes 149792 | tf_op jit(solution)/shard_map/ppermute | solution.py:108
  402.6 4.4 %collective-permute-done.19 = bf16[96,780]{1,0:T(8,128)(2,1)S(1)} collective-permute-done((bf16[96,780]{1,0:T(8,128)(2,1)}, bf16[96,780]{1,0:T(8,128)(2,1)S(1)}, u32[]{:S(2)}, u32[]{:S(2)}) %collective-permute-start.19) | collective-permute-done | bytes 149792 | tf_op jit(solution)/shard_map/ppermute | solution.py:108
  423.7 3.0 collective-permute-done.25
  (368 shorter events, 160.8 us)
Async XLA Ops:
  10.6 31.0 %all-to-all-start = ((bf16[32,16,768]{2,0,1:T(8,128)(2,1)}), bf16[32,16,768]{2,0,1:T(8,128)(2,1)S(1)}, u32[]{:S(2)}, u32[]{:S(2)}) async-start(bf16[32,16,768]{2,0,1:T(8,128)(2,1)} %copy.98), calls=%async_computation | async-start | bytes 1572864 | tf_op jit(solution)/shard_map/all_to_all | solution.py:128
  18.1 46.9 %all-gather.3.cloned.1.call-start = ((), (), s32[]{:S(2)}) async-start(), calls=%async_computation.4 | async-start | bytes 1327104 | tf_op jit(solution)/shard_map/all_gather | solution.py:92
  18.9 99.5 %all-gather.5.cloned.1.call-start = ((), (), s32[]{:S(2)}) async-start(), calls=%async_computation.5 | async-start | bytes 2654208 | tf_op jit(solution)/shard_map/all_gather | solution.py:92
  41.7 8.7 %collective-permute-start = (bf16[256,768]{1,0:T(8,128)(2,1)S(1)}, bf16[256,768]{1,0:T(8,128)(2,1)S(1)}, u32[]{:S(2)}, u32[]{:S(2)}) collective-permute-start(bf16[256,768]{1,0:T(8,128)(2,1)S(1)} %get-tuple-element.132), channel_id=1, source_target_pairs={{0,2},{1,3},{2,0},{3,1},{4,6},{5,7},{6,4},{7,5},{8,10},{9,11},{10,... | collective-permute-start | bytes 1179656 | tf_op jit(solution)/shard_map/ppermute | solution.py:86
  50.4 16.0 %collective-permute-start.1 = (bf16[512,768]{1,0:T(8,128)(2,1)S(1)}, bf16[512,768]{1,0:T(8,128)(2,1)}, u32[]{:S(2)}, u32[]{:S(2)}) collective-permute-start(bf16[512,768]{1,0:T(8,128)(2,1)S(1)} %pad_maximum_fusion.9), channel_id=1, source_target_pairs={{0,1},{1,0},{2,3},{3,2},{4,5},{5,4},{6,7},{7,6},{8,9},{9,8},{10,11... | collective-permute-start | bytes 2359304 | tf_op jit(solution)/shard_map/ppermute | solution.py:89
  65.0 26.7 %collective-permute-start.2 = (bf16[768,768]{1,0:T(8,128)(2,1)}, bf16[768,768]{1,0:T(8,128)(2,1)S(1)}, u32[]{:S(2)}, u32[]{:S(2)}) collective-permute-start(bf16[768,768]{1,0:T(8,128)(2,1)} %all-gather.3.cloned.1.call-done), channel_id=1, source_target_pairs={{0,2},{1,3},{2,0},{3,1},{4,6},{5,7},{6,4},{7,5},{8,10},{9,11},{10,... | collective-permute-start | bytes 3538952 | tf_op jit(solution)/shard_map/ppermute | solution.py:86
  104.9 2.4 collective-permute-start.3
  109.2 10.7 %collective-permute-start.4 = (bf16[512,768]{1,0:T(8,128)(2,1)}, bf16[512,768]{1,0:T(8,128)(2,1)}, u32[]{:S(2)}, u32[]{:S(2)}) collective-permute-start(bf16[512,768]{1,0:T(8,128)(2,1)} %fusion.37), channel_id=1, source_target_pairs={{0,1},{1,0},{2,3},{3,2},{4,5},{5,4},{6,7},{7,6},{8,9},{9,8},{10,11... | collective-permute-start | bytes 2359304 | tf_op jit(solution)/shard_map/ppermute | solution.py:89
  111.0 74.7 %all-to-all-start.1 = ((bf16[32,16,768]{2,0,1:T(8,128)(2,1)}), bf16[32,16,768]{2,0,1:T(8,128)(2,1)S(1)}, u32[]{:S(2)}, u32[]{:S(2)}) async-start(bf16[32,16,768]{2,0,1:T(8,128)(2,1)} %copy.103), calls=%async_computation.1 | async-start | bytes 1572864 | tf_op jit(solution)/shard_map/all_to_all | solution.py:128
  114.5 302.3 %reduce-scatter.4.cloned.1.call-start = ((), (), s32[]{:S(2)}) async-start(), calls=%async_computation.6 | async-start | bytes 5308416
  118.4 51.6 %collective-permute-start.5 = (bf16[768,1536]{1,0:T(8,128)(2,1)}, bf16[768,1536]{1,0:T(8,128)(2,1)S(1)}, u32[]{:S(2)}, u32[]{:S(2)}) collective-permute-start(bf16[768,1536]{1,0:T(8,128)(2,1)} %all-gather.5.cloned.1.call-done), channel_id=1, source_target_pairs={{0,2},{1,3},{2,0},{3,1},{4,6},{5,7},{6,4},{7,5},{8,10},{9,11},{10,... | collective-permute-start | bytes 7077896 | tf_op jit(solution)/shard_map/ppermute | solution.py:86
  185.7 2.6 collective-permute-start.6
  185.8 11.6 %collective-permute-start.8 = (bf16[256,768]{1,0:T(8,128)(2,1)S(1)}, bf16[256,768]{1,0:T(8,128)(2,1)S(1)}, u32[]{:S(2)}, u32[]{:S(2)}) collective-permute-start(bf16[256,768]{1,0:T(8,128)(2,1)S(1)} %get-tuple-element.130), channel_id=1, source_target_pairs={{0,2},{1,3},{2,0},{3,1},{4,6},{5,7},{6,4},{7,5},{8,10},{9,11},{10,... | collective-permute-start | bytes 1179656 | tf_op jit(solution)/shard_map/ppermute | solution.py:86
  200.1 2.4 collective-permute-start.9
  229.9 2.6 collective-permute-start.10
  230.9 11.5 %collective-permute-start.7 = (bf16[256,768]{1,0:T(8,128)(2,1)S(1)}, bf16[256,768]{1,0:T(8,128)(2,1)S(1)}, u32[]{:S(2)}, u32[]{:S(2)}) collective-permute-start(bf16[256,768]{1,0:T(8,128)(2,1)S(1)} %slice.231), channel_id=1, source_target_pairs={{0,2},{1,3},{2,0},{3,1},{4,6},{5,7},{6,4},{7,5},{8,10},{9,11},{10,... | collective-permute-start | bytes 1179656 | tf_op jit(solution)/shard_map/ppermute | solution.py:86
  238.2 17.1 %collective-permute-start.11 = (bf16[512,768]{1,0:T(8,128)(2,1)}, bf16[512,768]{1,0:T(8,128)(2,1)}, u32[]{:S(2)}, u32[]{:S(2)}) collective-permute-start(bf16[512,768]{1,0:T(8,128)(2,1)} %get-tuple-element.95), channel_id=1, source_target_pairs={{0,1},{1,0},{2,3},{3,2},{4,5},{5,4},{6,7},{7,6},{8,9},{9,8},{10,11... | collective-permute-start | bytes 2359304 | tf_op jit(solution)/shard_map/ppermute | solution.py:89
  246.1 8.5 %collective-permute-start.12 = (f32[768,10]{0,1:T(8,128)S(1)}, f32[768,10]{0,1:T(8,128)S(1)}, u32[]{:S(2)}, u32[]{:S(2)}) collective-permute-start(f32[768,10]{0,1:T(8,128)S(1)} %concatenate.76), channel_id=1, source_target_pairs={{0,1},{1,0},{2,3},{3,2},{4,5},{5,4},{6,7},{7,6},{8,9},{9,8},{10,11... | collective-permute-start | bytes 92168 | tf_op jit(solution)/shard_map/ppermute | solution.py:89
  313.1 10.6 %collective-permute-start.13 = (bf16[512,768]{1,0:T(8,128)(2,1)}, bf16[512,768]{1,0:T(8,128)(2,1)}, u32[]{:S(2)}, u32[]{:S(2)}) collective-permute-start(bf16[512,768]{1,0:T(8,128)(2,1)} %slice.315), channel_id=1, source_target_pairs={{0,1},{1,0},{2,3},{3,2},{4,5},{5,4},{6,7},{7,6},{8,9},{9,8},{10,11... | collective-permute-start | bytes 2359304 | tf_op jit(solution)/shard_map/ppermute | solution.py:89
  313.7 29.7 %collective-permute-start.15 = (bf16[768,778]{0,1:T(8,128)(2,1)}, bf16[768,778]{0,1:T(8,128)(2,1)}, u32[]{:S(2)}, u32[]{:S(2)}) collective-permute-start(bf16[768,778]{0,1:T(8,128)(2,1)} %pad_maximum_fusion.6), channel_id=1, source_target_pairs={{0,2},{1,3},{2,0},{3,1},{4,6},{5,7},{6,4},{7,5},{8,10},{9,11},{10,... | collective-permute-start | bytes 3585032 | tf_op jit(solution)/shard_map/ppermute | solution.py:86
  316.4 6.4 %collective-permute-start.16 = (f32[768,2]{0,1:T(2,128)S(1)}, f32[768,2]{0,1:T(2,128)S(1)}, u32[]{:S(2)}, u32[]{:S(2)}) collective-permute-start(f32[768,2]{0,1:T(2,128)S(1)} %pad_maximum_fusion.15), channel_id=1, source_target_pairs={{0,1},{1,0},{2,3},{3,2},{4,5},{5,4},{6,7},{7,6},{8,9},{9,8},{10,11... | collective-permute-start | bytes 18440 | tf_op jit(solution)/shard_map/ppermute | solution.py:89
  326.5 28.5 %collective-permute-start.14 = (bf16[256,768]{1,0:T(8,128)(2,1)}, bf16[256,768]{1,0:T(8,128)(2,1)}, u32[]{:S(2)}, u32[]{:S(2)}) collective-permute-start(bf16[256,768]{1,0:T(8,128)(2,1)} %slice.236), channel_id=1, source_target_pairs={{0,2},{1,3},{2,0},{3,1},{4,6},{5,7},{6,4},{7,5},{8,10},{9,11},{10,... | collective-permute-start | bytes 1179656 | tf_op jit(solution)/shard_map/ppermute | solution.py:86
  348.3 19.5 %collective-permute-start.23 = (bf16[96,780]{1,0:T(8,128)(2,1)S(1)}, bf16[96,780]{1,0:T(8,128)(2,1)S(1)}, u32[]{:S(2)}, u32[]{:S(2)}) collective-permute-start(bf16[96,780]{1,0:T(8,128)(2,1)S(1)} %fusion.100), channel_id=1, source_target_pairs={{0,28},{4,0},{8,4},{12,8},{16,12},{20,16},{24,20},{28,24},{1,29},{... | collective-permute-start | bytes 449288 | tf_op jit(solution)/shard_map/ppermute | solution.py:108
  354.2 16.0 %collective-permute-start.22 = (bf16[96,780]{1,0:T(8,128)(2,1)}, bf16[96,780]{1,0:T(8,128)(2,1)}, u32[]{:S(2)}, u32[]{:S(2)}) collective-permute-start(bf16[96,780]{1,0:T(8,128)(2,1)} %get-tuple-element.116), channel_id=1, source_target_pairs={{0,24},{4,28},{8,0},{12,4},{16,8},{20,12},{24,16},{28,20},{1,25},{... | collective-permute-start | bytes 449288 | tf_op jit(solution)/shard_map/ppermute | solution.py:108
  357.8 62.4 %all-to-all-start.2 = ((bf16[256,2,768]{2,1,0:T(2,128)(2,1)}), bf16[256,2,768]{2,1,0:T(2,128)(2,1)}, u32[]{:S(2)}, u32[]{:S(2)}) async-start(bf16[256,2,768]{2,1,0:T(2,128)(2,1)} %copy.112), calls=%async_computation.2 | async-start | bytes 1572864 | tf_op jit(solution)/shard_map/all_to_all | solution.py:396
  362.0 17.7 %collective-permute-start.21 = (bf16[96,780]{1,0:T(8,128)(2,1)}, bf16[96,780]{1,0:T(8,128)(2,1)S(1)}, u32[]{:S(2)}, u32[]{:S(2)}) collective-permute-start(bf16[96,780]{1,0:T(8,128)(2,1)} %get-tuple-element.115), channel_id=1, source_target_pairs={{0,20},{4,24},{8,28},{12,0},{16,4},{20,8},{24,12},{28,16},{1,21},{... | collective-permute-start | bytes 449288 | tf_op jit(solution)/shard_map/ppermute | solution.py:108
  365.8 36.8 %collective-permute-start.20 = (bf16[96,780]{1,0:T(8,128)(2,1)}, bf16[96,780]{1,0:T(8,128)(2,1)S(1)}, u32[]{:S(2)}, u32[]{:S(2)}) collective-permute-start(bf16[96,780]{1,0:T(8,128)(2,1)} %get-tuple-element.114), channel_id=1, source_target_pairs={{0,16},{4,20},{8,24},{12,28},{16,0},{20,4},{24,8},{28,12},{1,17},{... | collective-permute-start | bytes 449288 | tf_op jit(solution)/shard_map/ppermute | solution.py:108
  366.3 40.7 %collective-permute-start.19 = (bf16[96,780]{1,0:T(8,128)(2,1)}, bf16[96,780]{1,0:T(8,128)(2,1)S(1)}, u32[]{:S(2)}, u32[]{:S(2)}) collective-permute-start(bf16[96,780]{1,0:T(8,128)(2,1)} %get-tuple-element.113), channel_id=1, source_target_pairs={{0,12},{4,16},{8,20},{12,24},{16,28},{20,0},{24,4},{28,8},{1,13},{... | collective-permute-start | bytes 449288 | tf_op jit(solution)/shard_map/ppermute | solution.py:108
  367.8 39.2 %collective-permute-start.18 = (bf16[96,780]{1,0:T(8,128)(2,1)}, bf16[96,780]{1,0:T(8,128)(2,1)}, u32[]{:S(2)}, u32[]{:S(2)}) collective-permute-start(bf16[96,780]{1,0:T(8,128)(2,1)} %get-tuple-element.112), channel_id=1, source_target_pairs={{0,8},{4,12},{8,16},{12,20},{16,24},{20,28},{24,0},{28,4},{1,9},{5... | collective-permute-start | bytes 449288 | tf_op jit(solution)/shard_map/ppermute | solution.py:108
  370.2 36.9 %collective-permute-start.17 = (bf16[96,780]{1,0:T(8,128)(2,1)}, bf16[96,780]{1,0:T(8,128)(2,1)}, u32[]{:S(2)}, u32[]{:S(2)}) collective-permute-start(bf16[96,780]{1,0:T(8,128)(2,1)} %get-tuple-element.111), channel_id=1, source_target_pairs={{0,4},{4,8},{8,12},{12,16},{16,20},{20,24},{24,28},{28,0},{1,5},{5... | collective-permute-start | bytes 449288 | tf_op jit(solution)/shard_map/ppermute | solution.py:108
  410.7 6.0 %collective-permute-start.24 = (f32[96,2]{1,0:T(8,128)S(1)}, f32[96,2]{1,0:T(8,128)S(1)}, u32[]{:S(2)}, u32[]{:S(2)}) collective-permute-start(f32[96,2]{1,0:T(8,128)S(1)} %slice.238), channel_id=1, source_target_pairs={{0,2},{1,3},{2,0},{3,1},{4,6},{5,7},{6,4},{7,5},{8,10},{9,11},{10,... | collective-permute-start | bytes 2312 | tf_op jit(solution)/shard_map/ppermute | solution.py:86
  418.2 8.6 %collective-permute-start.25 = (bf16[96,1536]{0,1:T(8,128)(2,1)S(1)}, bf16[96,1536]{0,1:T(8,128)(2,1)S(1)}, u32[]{:S(2)}, u32[]{:S(2)}) collective-permute-start(bf16[96,1536]{0,1:T(8,128)(2,1)S(1)} %copy.136), channel_id=1, source_target_pairs={{0,2},{1,3},{2,0},{3,1},{4,6},{5,7},{6,4},{7,5},{8,10},{9,11},{10,... | collective-permute-start | bytes 884744 | tf_op jit(solution)/shard_map/ppermute | solution.py:86
  (87 other events, 917.9 us)
Sparse Core Ops, SparseCore 0:
  21.6 43.3 all-gather.2
  67.8 50.5 all-gather.4
  254.8 96.4 reduce-scatter.3

commit v8 on v5

--- a/solution.py
+++ b/solution.py
@@ -149,19 +149,23 @@
     position = (inner // piece_rows * n_tensor + owner) * piece_rows + inner % piece_rows
     key_valid = position < seq_length
 
-    attn_w = jnp.concatenate([project_weight, attention_output_weight], axis=1)
-    feed_w = jnp.concatenate([feed_input_weight, feed_output_weight], axis=1)
-    attn_own = gather_dp(attn_w)
-    feed_own = gather_dp(feed_w)
-    attn_part = to_chip_partner(attn_own)
-    feed_part = to_chip_partner(feed_own)
+    attn_both = gather_dp(
+        jnp.concatenate(
+            [project_weight, attention_output_weight, to_chip_partner(project_weight)], axis=1
+        )
+    )
+    feed_both = gather_dp(
+        jnp.concatenate(
+            [feed_input_weight, feed_output_weight, to_chip_partner(feed_input_weight)], axis=1
+        )
+    )
+    output_own = attn_both[:, project_cols : project_cols + head_cols]
+    down_own = feed_both[:, hidden_cols : 2 * hidden_cols]
     slices = (tensor_index, partner_slice)
-    attn_sets = (attn_own, attn_part)
-    feed_sets = (feed_own, feed_part)
-    project_ws = [a[:, :project_cols] for a in attn_sets]
-    output_ws = [a[:, project_cols:] for a in attn_sets]
-    up_ws = [f[:, :hidden_cols] for f in feed_sets]
-    down_ws = [f[:, hidden_cols:] for f in feed_sets]
+    project_ws = [attn_both[:, :project_cols], attn_both[:, project_cols + head_cols :]]
+    output_ws = [output_own, to_chip_partner(output_own)]
+    up_ws = [feed_both[:, :hidden_cols], feed_both[:, 2 * hidden_cols :]]
+    down_ws = [down_own, to_chip_partner(down_own)]
 
     def project_bias(k):
         query_part = lax.dynamic_slice_in_dim(query_projection_bias, k * head_cols, head_cols)

time: 427 us -> 439 us (1.028)
    ppermute x8 -> x10, waiting for transfers between devices: 86.5 us -> 43.8 us  [to_chip_partner(): return lax.ppermute(value, 'tensor', across_chips)]
    all_gather x2, waiting for transfers between devices: 12.9 us -> 50.5 us  [gather_dp(): return lax.all_gather(block, 'dp', axis=0, tiled=True)]
    all_to_all x2, waiting for transfers between devices: 19.1 us -> 24.7 us  [deal(): here = lax.all_to_all(sent, 'dp', split_axis=1, concat_axis=0, tiled=True)]
    unnamed x216 -> x202, local copies, waits for them, and re-layouts: 34.1 us -> 29.9 us
    ppermute x8 -> x10, starting transfers between devices: 10.9 us -> 13.2 us  [to_chip_partner(): return lax.ppermute(value, 'tensor', across_chips)]
  transfers between devices with their start and end apart: 31 -> 33, of which waited for: 19 -> 19; matrix products, arithmetic and copies ran while one was open for 37% -> 38% of each run, Pallas kernels for 0% -> 0%
where the time goes in v8:
time: 439 us; the launch traced here: 431 us
  waiting for transfers between devices  159 us (36%)
  matrix products  117 us (27%)
  local copies, waits for them, and re-layouts  59.1 us (13%)
  starting transfers between devices  43.3 us (10%)
  other arithmetic  36.9 us (8%)
  between operations  15.6 us (4%)
    all_gather x2, waiting for transfers between devices, gather_dp(): return lax.all_gather(block, 'dp', axis=0, tiled=True)  50.5 us
    ppermute x10, waiting for transfers between devices, to_chip_partner(): return lax.ppermute(value, 'tensor', across_chips)  43.8 us
    dot_general x8, matrix products, dot_nn(): return jnp.dot(a, b, preferred_element_type=jnp.float32)  38.7 us
    ppermute x7, waiting for transfers between devices, scatter_dp_permutes(): lax.ppermute(sent, 'dp', [(j, (j + k) % n_data) for j in range(n_data)])  32.6 us
    unnamed x202, local copies, waits for them, and re-layouts  29.9 us
    all_to_all x2, waiting for transfers between devices, deal(): here = lax.all_to_all(sent, 'dp', split_axis=1, concat_axis=0, tiled=True)  24.7 us
    dot_general x8, matrix products, dot_tn(): lax.dot_general(a, b, (((0,), (0,)), ((), ())), preferred_element_type=jn...  23.4 us
    dot_general x8, matrix products, dot_nt(): lax.dot_general(a, b, (((1,), (1,)), ((), ())), preferred_element_type=jn...  14.7 us
  transfers between devices with their start and end apart: 33, of which 19 were waited for; matrix products, arithmetic and copies ran while one was open for 38% of the time, Pallas kernels for 0%

profile of v8, /device:TPU:12, one launch (start us, length us, event | category | flops | bytes accessed | tf_op | source)
XLA Modules:
  0.0 430.8 jit_solution(6773801184089244820)
XLA Ops:
  8.8 3.8 collective-permute-done.2
  16.6 6.4 %all-to-all-start = ((bf16[32,16,768]{2,0,1:T(8,128)(2,1)}), bf16[32,16,768]{2,0,1:T(8,128)(2,1)S(1)}, u32[]{:S(2)}, u32[]{:S(2)}) async-start(bf16[32,16,768]{2,0,1:T(8,128)(2,1)} %copy.99), calls=%async_computation | async-start | bytes 1572864 | tf_op jit(solution)/shard_map/all_to_all | solution.py:127
  23.0 24.7 %all-to-all-done = bf16[32,16,768]{2,0,1:T(8,128)(2,1)S(1)} async-done(((bf16[32,16,768]{2,0,1:T(8,128)(2,1)}), bf16[32,16,768]{2,0,1:T(8,128)(2,1)S(1)}, u32[]{:S(2)}, u32[]{:S(2)}) %all-to-all-start) | async-done | bytes 786464 | tf_op jit(solution)/shard_map/all_to_all | solution.py:127
  50.6 9.3 %collective-permute-done = bf16[256,768]{1,0:T(8,128)(2,1)S(1)} collective-permute-done((bf16[256,768]{1,0:T(8,128)(2,1)S(1)}, bf16[256,768]{1,0:T(8,128)(2,1)S(1)}, u32[]{:S(2)}, u32[]{:S(2)}) %collective-permute-start) | collective-permute-done | bytes 393248 | tf_op jit(solution)/shard_map/ppermute | solution.py:86
  62.9 10.8 %all-gather.3.cloned.1.call-done = bf16[768,1344]{1,0:T(8,128)(2,1)} async-done(((bf16[96,1344]{1,0:T(8,128)(2,1)}), bf16[768,1344]{1,0:T(8,128)(2,1)}) %all-gather.3.cloned.1.call-update) | async-done | bytes 2064400 | tf_op jit(solution)/shard_map/all_gather | solution.py:92
  83.4 2.9 copy-done.2
  86.4 2.8 fusion.57
  93.4 2.9 copy-done.3
  106.4 4.9 %all-to-all-start.1 = ((bf16[32,16,768]{2,0,1:T(8,128)(2,1)}), bf16[32,16,768]{2,0,1:T(8,128)(2,1)S(1)}, u32[]{:S(2)}, u32[]{:S(2)}) async-start(bf16[32,16,768]{2,0,1:T(8,128)(2,1)} %copy.104), calls=%async_computation.1 | async-start | bytes 1572864 | tf_op jit(solution)/shard_map/all_to_all | solution.py:127
  112.8 39.7 %all-gather.5.cloned.1.call-done = bf16[768,2304]{1,0:T(8,128)(2,1)} async-done(((bf16[96,2304]{1,0:T(8,128)(2,1)}), bf16[768,2304]{1,0:T(8,128)(2,1)}) %all-gather.5.cloned.1.call-update) | async-done | bytes 3538960 | tf_op jit(solution)/shard_map/all_gather | solution.py:92
  155.3 11.5 %multiply_convert_fusion.3 = (bf16[1024,768]{1,0:T(8,128)(2,1)S(1)}, f32[1024,768]{1,0:T(8,128)}, f32[1024,768]{1,0:T(8,128)}) fusion(f32[768]{0:T(1024)} %get-tuple-element.132, bf16[768,2304]{1,0:T(8,128)(2,1)} %all-gather.5.cloned.1.call-done, bf16[512,768]{1,0:T(8,128)(2,1)} %collective-permute-done.5, bf16[512,768]{1,0:T(8,128)(2,1)} %fusion.42), kind=kOutput, calls=%fused_computation.43 | convolution fusion | flops 1263009792 | bytes 10620928 | tf_op jit(solution)/shard_map/dot_general | solution.py:38
  166.9 11.6 %multiply_convert_fusion.2 = (bf16[1024,768]{1,0:T(8,128)(2,1)S(1)}, f32[1024,768]{1,0:T(8,128)}, f32[1024,768]{1,0:T(8,128)}) fusion(f32[768]{0:T(1024)S(1)} %copy-done.72, bf16[768,2304]{1,0:T(8,128)(2,1)S(1)} %copy-done.15, bf16[512,768]{1,0:T(8,128)(2,1)} %collective-permute-done.5, bf16[512,768]{1,0:T(8,128)(2,1)} %fusion.42), kind=kOutput, calls=%fused_computation.30 | convolution fusion | flops 1263009792 | bytes 10620928 | tf_op jit(solution)/shard_map/dot_general | solution.py:38
  178.5 3.3 collective-permute-done.7
  192.1 6.9 %collective-permute-done.10 = bf16[256,768]{1,0:T(8,128)(2,1)S(1)} collective-permute-done((bf16[256,768]{1,0:T(8,128)(2,1)S(1)}, bf16[256,768]{1,0:T(8,128)(2,1)S(1)}, u32[]{:S(2)}, u32[]{:S(2)}) %collective-permute-start.10) | collective-permute-done | bytes 393248 | tf_op jit(solution)/shard_map/ppermute | solution.py:86
  203.0 3.8 convert_reduce_fusion
  210.3 3.8 convert_reduce_fusion.1
  224.0 4.5 %fusion.41 = bf16[768,3466]{0,1:T(8,128)(2,1)} fusion(bf16[1024,768]{1,0:T(8,128)(2,1)} %copy-done.29, bf16[512,768]{1,0:T(8,128)(2,1)} %collective-permute-done.5, bf16[512,768]{1,0:T(8,128)(2,1)} %fusion.42), kind=kOutput, calls=%fused_computation.110 | convolution fusion | flops 1211695104 | bytes 4325376 | tf_op jit(solution)/shard_map/dot_general | solution.py:34
  238.5 4.1 fusion.39
  248.1 7.9 %copy.133 = bf16[768,3466]{1,0:T(8,128)(2,1)} copy(bf16[768,3466]{0,1:T(8,128)(2,1)} %fusion.78) | data formatting | bytes 10647552
  256.1 10.6 %multiply_reduce_fusion = (f32[3,1024]{1,0:T(4,128)S(1)}, f32[3,1024,1024]{1,2,0:T(8,128)}) fusion(f32[3,1024,1024]{1,2,0:T(8,128)} %copy-done.3, f32[3,1024]{1,0:T(4,128)S(1)} %log_add_fusion, bf16[1024,3,64]{0,2,1:T(8,128)(2,1)S(1)} %bitcast.196, bf16[1024,3,64]{0,2,1:T(8,128)(2,1)S(1)} %bitcast.201), kind=kOutput, calls=%fused_computation.1 | convolution fusion | flops 412087296 | bytes 25976832 | tf_op jit(solution)/shard_map/qhe,khe->hqk/dot_general | solution.py:212
  268.8 6.7 %multiply_convert_fusion = bf16[3,1024,1024]{1,2,0:T(8,128)(2,1)S(1)} fusion(f32[3,1024,1024]{1,2,0:T(8,128)} %get-tuple-element.163, f32[3,1024,1024]{1,2,0:T(8,128)S(1)} %bitcast.169, f32[3,1024]{1,0:T(4,128)S(1)} %get-tuple-element.162, f32[3,1024]{1,0:T(4,128)S(1)} %log_add_fusion), kind=kLoop, calls=%fused_computation | loop fusion | flops 12582912 | bytes 31481856 | tf_op jit(solution)/shard_map/convert_element_type | solution.py:216
  280.9 4.9 %fusion.67 = f32[1024,768]{1,0:T(8,128)} fusion(bf16[768,1344]{1,0:T(8,128)(2,1)} %all-gather.3.cloned.1.call-done, bf16[1024,192]{0,1:T(8,128)(2,1)S(1)} %bitcast.202, bf16[1024,192]{0,1:T(8,128)(2,1)S(1)} %bitcast.208, bf16[1024,192]{0,1:T(8,128)(2,1)S(1)} %bitcast.205), kind=kOutput, calls=%fused_computation.151 | convolution fusion | flops 909508608 | bytes 5308416 | tf_op jit(solution)/shard_map/dot_general | solution.py:30
  285.8 2.8 multiply_reduce_fusion.1
  288.6 5.5 %multiply_convert_fusion.1 = bf16[3,1024,1024]{1,2,0:T(8,128)(2,1)} fusion(f32[3,1024,1024]{1,2,0:T(8,128)S(1)} %get-tuple-element.161, f32[3,1024,1024]{1,2,0:T(8,128)S(1)} %bitcast.167, f32[3,1024]{1,0:T(4,128)S(1)} %get-tuple-element.160, f32[3,1024]{1,0:T(4,128)S(1)} %log_add_fusion.1), kind=kLoop, calls=%fused_computation.3 | loop fusion | flops 12582912 | bytes 31481856 | tf_op jit(solution)/shard_map/convert_element_type | solution.py:216
  294.1 4.2 fusion.46
  312.6 2.8 convolution_convert_fusion.4
  322.9 7.0 %collective-permute-done.16 = bf16[256,768]{1,0:T(8,128)(2,1)} collective-permute-done((bf16[256,768]{1,0:T(8,128)(2,1)}, bf16[256,768]{1,0:T(8,128)(2,1)}, u32[]{:S(2)}, u32[]{:S(2)}) %collective-permute-start.16) | collective-permute-done | bytes 393248 | tf_op jit(solution)/shard_map/ppermute | solution.py:86
  332.7 7.3 %all-to-all-start.2 = ((bf16[256,2,768]{2,1,0:T(2,128)(2,1)}), bf16[256,2,768]{2,1,0:T(2,128)(2,1)}, u32[]{:S(2)}, u32[]{:S(2)}) async-start(bf16[256,2,768]{2,1,0:T(2,128)(2,1)} %copy.113), calls=%async_computation.2 | async-start | bytes 1572864 | tf_op jit(solution)/shard_map/all_to_all | solution.py:384
  342.3 6.8 %collective-permute-done.18 = bf16[768,578]{0,1:T(8,128)(2,1)} collective-permute-done((bf16[768,578]{0,1:T(8,128)(2,1)}, bf16[768,578]{0,1:T(8,128)(2,1)}, u32[]{:S(2)}, u32[]{:S(2)}) %collective-permute-start.18) | collective-permute-done | bytes 887840 | tf_op jit(solution)/shard_map/ppermute | solution.py:86
  358.9 3.3 collective-permute-start.21
  364.1 26.6 %collective-permute-done.19 = bf16[96,578]{1,0:T(8,128)(2,1)S(1)} collective-permute-done((bf16[96,578]{1,0:T(8,128)(2,1)S(1)}, bf16[96,578]{1,0:T(8,128)(2,1)S(1)}, u32[]{:S(2)}, u32[]{:S(2)}) %collective-permute-start.19) | collective-permute-done | bytes 111008 | tf_op jit(solution)/shard_map/ppermute | solution.py:108
  410.6 5.5 %collective-permute-done.26 = bf16[96,1738]{0,1:T(8,128)(2,1)} collective-permute-done((bf16[96,1738]{0,1:T(8,128)(2,1)S(1)}, bf16[96,1738]{0,1:T(8,128)(2,1)}, u32[]{:S(2)}, u32[]{:S(2)}) %collective-permute-start.26) | collective-permute-done | bytes 333728 | tf_op jit(solution)/shard_map/ppermute | solution.py:86
  (390 shorter events, 155.6 us)
Async XLA Ops:
  7.2 66.5 %all-gather.3.cloned.1.call-start = ((), (), s32[]{:S(2)}) async-start(), calls=%async_computation.4 | async-start | bytes 2433024 | tf_op jit(solution)/shard_map/all_gather | solution.py:92
  7.2 5.3 %collective-permute-start.2 = (bf16[96,576]{1,0:T(8,128)(2,1)}, bf16[96,576]{1,0:T(8,128)(2,1)S(1)}, u32[]{:S(2)}, u32[]{:S(2)}) collective-permute-start(bf16[96,576]{1,0:T(8,128)(2,1)} %param.20), channel_id=1, source_target_pairs={{0,2},{1,3},{2,0},{3,1},{4,6},{5,7},{6,4},{7,5},{8,10},{9,11},{10,... | collective-permute-start | bytes 331784 | tf_op jit(solution)/shard_map/ppermute | solution.py:86
  16.6 31.1 %all-to-all-start = ((bf16[32,16,768]{2,0,1:T(8,128)(2,1)}), bf16[32,16,768]{2,0,1:T(8,128)(2,1)S(1)}, u32[]{:S(2)}, u32[]{:S(2)}) async-start(bf16[32,16,768]{2,0,1:T(8,128)(2,1)} %copy.99), calls=%async_computation | async-start | bytes 1572864 | tf_op jit(solution)/shard_map/all_to_all | solution.py:127
  23.0 129.5 %all-gather.5.cloned.1.call-start = ((), (), s32[]{:S(2)}) async-start(), calls=%async_computation.5 | async-start | bytes 3981312 | tf_op jit(solution)/shard_map/all_gather | solution.py:92
  47.8 12.1 %collective-permute-start = (bf16[256,768]{1,0:T(8,128)(2,1)S(1)}, bf16[256,768]{1,0:T(8,128)(2,1)S(1)}, u32[]{:S(2)}, u32[]{:S(2)}) collective-permute-start(bf16[256,768]{1,0:T(8,128)(2,1)S(1)} %get-tuple-element.129), channel_id=1, source_target_pairs={{0,2},{1,3},{2,0},{3,1},{4,6},{5,7},{6,4},{7,5},{8,10},{9,11},{10,... | collective-permute-start | bytes 1179656 | tf_op jit(solution)/shard_map/ppermute | solution.py:86
  49.4 12.7 %collective-permute-start.6 = (bf16[96,768]{1,0:T(8,128)(2,1)S(1)}, bf16[96,768]{1,0:T(8,128)(2,1)S(1)}, u32[]{:S(2)}, u32[]{:S(2)}) collective-permute-start(bf16[96,768]{1,0:T(8,128)(2,1)S(1)} %copy-done.45), channel_id=1, source_target_pairs={{0,2},{1,3},{2,0},{3,1},{4,6},{5,7},{6,4},{7,5},{8,10},{9,11},{10,... | collective-permute-start | bytes 442376 | tf_op jit(solution)/shard_map/ppermute | solution.py:86
  59.9 3.0 collective-permute-start.1
  77.8 20.9 %collective-permute-start.3 = (bf16[768,192]{1,0:T(8,128)(2,1)S(1)}, bf16[768,192]{1,0:T(8,128)(2,1)S(1)}, u32[]{:S(2)}, u32[]{:S(2)}) collective-permute-start(bf16[768,192]{1,0:T(8,128)(2,1)S(1)} %slice.204), channel_id=1, source_target_pairs={{0,2},{1,3},{2,0},{3,1},{4,6},{5,7},{6,4},{7,5},{8,10},{9,11},{10,... | collective-permute-start | bytes 884744 | tf_op jit(solution)/shard_map/ppermute | solution.py:86
  100.3 2.4 collective-permute-start.4
  104.7 50.7 %collective-permute-start.5 = (bf16[512,768]{1,0:T(8,128)(2,1)}, bf16[512,768]{1,0:T(8,128)(2,1)}, u32[]{:S(2)}, u32[]{:S(2)}) collective-permute-start(bf16[512,768]{1,0:T(8,128)(2,1)} %fusion.42), channel_id=1, source_target_pairs={{0,1},{1,0},{2,3},{3,2},{4,5},{5,4},{6,7},{7,6},{8,9},{9,8},{10,11... | collective-permute-start | bytes 2359304 | tf_op jit(solution)/shard_map/ppermute | solution.py:89
  106.4 80.8 %all-to-all-start.1 = ((bf16[32,16,768]{2,0,1:T(8,128)(2,1)}), bf16[32,16,768]{2,0,1:T(8,128)(2,1)S(1)}, u32[]{:S(2)}, u32[]{:S(2)}) async-start(bf16[32,16,768]{2,0,1:T(8,128)(2,1)} %copy.104), calls=%async_computation.1 | async-start | bytes 1572864 | tf_op jit(solution)/shard_map/all_to_all | solution.py:127
  111.3 291.0 %reduce-scatter.4.cloned.1.call-start = ((), (), s32[]{:S(2)}) async-start(), calls=%async_computation.6 | async-start | bytes 6193152
  153.8 28.0 %collective-permute-start.7 = (bf16[768,768]{1,0:T(8,128)(2,1)S(1)}, bf16[768,768]{1,0:T(8,128)(2,1)S(1)}, u32[]{:S(2)}, u32[]{:S(2)}) collective-permute-start(bf16[768,768]{1,0:T(8,128)(2,1)S(1)} %slice.212), channel_id=1, source_target_pairs={{0,2},{1,3},{2,0},{3,1},{4,6},{5,7},{6,4},{7,5},{8,10},{9,11},{10,... | collective-permute-start | bytes 3538952 | tf_op jit(solution)/shard_map/ppermute | solution.py:86
  187.2 2.6 collective-permute-start.8
  187.4 11.6 %collective-permute-start.10 = (bf16[256,768]{1,0:T(8,128)(2,1)S(1)}, bf16[256,768]{1,0:T(8,128)(2,1)S(1)}, u32[]{:S(2)}, u32[]{:S(2)}) collective-permute-start(bf16[256,768]{1,0:T(8,128)(2,1)S(1)} %get-tuple-element.127), channel_id=1, source_target_pairs={{0,2},{1,3},{2,0},{3,1},{4,6},{5,7},{6,4},{7,5},{8,10},{9,11},{10,... | collective-permute-start | bytes 1179656 | tf_op jit(solution)/shard_map/ppermute | solution.py:86
  200.6 2.4 collective-permute-start.11
  221.8 10.0 %collective-permute-start.13 = (bf16[512,768]{1,0:T(8,128)(2,1)S(1)}, bf16[512,768]{1,0:T(8,128)(2,1)}, u32[]{:S(2)}, u32[]{:S(2)}) collective-permute-start(bf16[512,768]{1,0:T(8,128)(2,1)S(1)} %convert_element_type.192), channel_id=1, source_target_pairs={{0,1},{1,0},{2,3},{3,2},{4,5},{5,4},{6,7},{7,6},{8,9},{9,8},{10,11... | collective-permute-start | bytes 2359304 | tf_op jit(solution)/shard_map/ppermute | solution.py:89
  231.3 16.2 %collective-permute-start.14 = (f32[768,10]{0,1:T(8,128)S(1)}, f32[768,10]{0,1:T(8,128)S(1)}, u32[]{:S(2)}, u32[]{:S(2)}) collective-permute-start(f32[768,10]{0,1:T(8,128)S(1)} %concatenate.63), channel_id=1, source_target_pairs={{0,1},{1,0},{2,3},{3,2},{4,5},{5,4},{6,7},{7,6},{8,9},{9,8},{10,11... | collective-permute-start | bytes 92168 | tf_op jit(solution)/shard_map/ppermute | solution.py:89
  308.2 7.2 %collective-permute-start.15 = (bf16[512,768]{1,0:T(8,128)(2,1)}, bf16[512,768]{1,0:T(8,128)(2,1)}, u32[]{:S(2)}, u32[]{:S(2)}) collective-permute-start(bf16[512,768]{1,0:T(8,128)(2,1)} %slice.296), channel_id=1, source_target_pairs={{0,1},{1,0},{2,3},{3,2},{4,5},{5,4},{6,7},{7,6},{8,9},{9,8},{10,11... | collective-permute-start | bytes 2359304 | tf_op jit(solution)/shard_map/ppermute | solution.py:89
  311.9 7.2 %collective-permute-start.17 = (f32[768,2]{0,1:T(2,128)S(1)}, f32[768,2]{0,1:T(2,128)S(1)}, u32[]{:S(2)}, u32[]{:S(2)}) collective-permute-start(f32[768,2]{0,1:T(2,128)S(1)} %pad_maximum_fusion.12), channel_id=1, source_target_pairs={{0,1},{1,0},{2,3},{3,2},{4,5},{5,4},{6,7},{7,6},{8,9},{9,8},{10,11... | collective-permute-start | bytes 18440 | tf_op jit(solution)/shard_map/ppermute | solution.py:89
  317.6 12.3 %collective-permute-start.16 = (bf16[256,768]{1,0:T(8,128)(2,1)}, bf16[256,768]{1,0:T(8,128)(2,1)}, u32[]{:S(2)}, u32[]{:S(2)}) collective-permute-start(bf16[256,768]{1,0:T(8,128)(2,1)} %slice.223), channel_id=1, source_target_pairs={{0,2},{1,3},{2,0},{3,1},{4,6},{5,7},{6,4},{7,5},{8,10},{9,11},{10,... | collective-permute-start | bytes 1179656 | tf_op jit(solution)/shard_map/ppermute | solution.py:86
  320.1 29.1 %collective-permute-start.18 = (bf16[768,578]{0,1:T(8,128)(2,1)}, bf16[768,578]{0,1:T(8,128)(2,1)}, u32[]{:S(2)}, u32[]{:S(2)}) collective-permute-start(bf16[768,578]{0,1:T(8,128)(2,1)} %pad_maximum_fusion.6), channel_id=1, source_target_pairs={{0,2},{1,3},{2,0},{3,1},{4,6},{5,7},{6,4},{7,5},{8,10},{9,11},{10,... | collective-permute-start | bytes 2663432 | tf_op jit(solution)/shard_map/ppermute | solution.py:86
  321.4 36.4 %collective-permute-start.9 = (bf16[256,768]{1,0:T(8,128)(2,1)}, bf16[256,768]{1,0:T(8,128)(2,1)}, u32[]{:S(2)}, u32[]{:S(2)}) collective-permute-start(bf16[256,768]{1,0:T(8,128)(2,1)} %slice.217), channel_id=1, source_target_pairs={{0,2},{1,3},{2,0},{3,1},{4,6},{5,7},{6,4},{7,5},{8,10},{9,11},{10,... | collective-permute-start | bytes 1179656 | tf_op jit(solution)/shard_map/ppermute | solution.py:86
  332.7 74.5 %all-to-all-start.2 = ((bf16[256,2,768]{2,1,0:T(2,128)(2,1)}), bf16[256,2,768]{2,1,0:T(2,128)(2,1)}, u32[]{:S(2)}, u32[]{:S(2)}) async-start(bf16[256,2,768]{2,1,0:T(2,128)(2,1)} %copy.113), calls=%async_computation.2 | async-start | bytes 1572864 | tf_op jit(solution)/shard_map/all_to_all | solution.py:384
  354.0 36.7 %collective-permute-start.19 = (bf16[96,578]{1,0:T(8,128)(2,1)S(1)}, bf16[96,578]{1,0:T(8,128)(2,1)S(1)}, u32[]{:S(2)}, u32[]{:S(2)}) collective-permute-start(bf16[96,578]{1,0:T(8,128)(2,1)S(1)} %get-tuple-element.117), channel_id=1, source_target_pairs={{0,4},{4,8},{8,12},{12,16},{16,20},{20,24},{24,28},{28,0},{1,5},{5... | collective-permute-start | bytes 332936 | tf_op jit(solution)/shard_map/ppermute | solution.py:108
  355.1 38.3 %collective-permute-start.20 = (bf16[96,578]{1,0:T(8,128)(2,1)S(1)}, bf16[96,578]{1,0:T(8,128)(2,1)S(1)}, u32[]{:S(2)}, u32[]{:S(2)}) collective-permute-start(bf16[96,578]{1,0:T(8,128)(2,1)S(1)} %get-tuple-element.123), channel_id=1, source_target_pairs={{0,8},{4,12},{8,16},{12,20},{16,24},{20,28},{24,0},{28,4},{1,9},{5... | collective-permute-start | bytes 332936 | tf_op jit(solution)/shard_map/ppermute | solution.py:108
  358.9 38.3 %collective-permute-start.21 = (bf16[96,578]{1,0:T(8,128)(2,1)}, bf16[96,578]{1,0:T(8,128)(2,1)S(1)}, u32[]{:S(2)}, u32[]{:S(2)}) collective-permute-start(bf16[96,578]{1,0:T(8,128)(2,1)} %get-tuple-element.122), channel_id=1, source_target_pairs={{0,12},{4,16},{8,20},{12,24},{16,28},{20,0},{24,4},{28,8},{1,13},{... | collective-permute-start | bytes 332936 | tf_op jit(solution)/shard_map/ppermute | solution.py:108
  362.2 36.4 %collective-permute-start.22 = (bf16[96,578]{1,0:T(8,128)(2,1)}, bf16[96,578]{1,0:T(8,128)(2,1)S(1)}, u32[]{:S(2)}, u32[]{:S(2)}) collective-permute-start(bf16[96,578]{1,0:T(8,128)(2,1)} %get-tuple-element.121), channel_id=1, source_target_pairs={{0,16},{4,20},{8,24},{12,28},{16,0},{20,4},{24,8},{28,12},{1,17},{... | collective-permute-start | bytes 332936 | tf_op jit(solution)/shard_map/ppermute | solution.py:108
  362.2 36.4 %collective-permute-start.23 = (bf16[96,578]{1,0:T(8,128)(2,1)}, bf16[96,578]{1,0:T(8,128)(2,1)S(1)}, u32[]{:S(2)}, u32[]{:S(2)}) collective-permute-start(bf16[96,578]{1,0:T(8,128)(2,1)} %get-tuple-element.120), channel_id=1, source_target_pairs={{0,20},{4,24},{8,28},{12,0},{16,4},{20,8},{24,12},{28,16},{1,21},{... | collective-permute-start | bytes 332936 | tf_op jit(solution)/shard_map/ppermute | solution.py:108
  390.8 9.7 %collective-permute-start.24 = (bf16[96,578]{1,0:T(8,128)(2,1)}, bf16[96,578]{1,0:T(8,128)(2,1)S(1)}, u32[]{:S(2)}, u32[]{:S(2)}) collective-permute-start(bf16[96,578]{1,0:T(8,128)(2,1)} %get-tuple-element.119), channel_id=1, source_target_pairs={{0,24},{4,28},{8,0},{12,4},{16,8},{20,12},{24,16},{28,20},{1,25},{... | collective-permute-start | bytes 332936 | tf_op jit(solution)/shard_map/ppermute | solution.py:108
  393.4 7.1 %collective-permute-start.25 = (bf16[96,578]{1,0:T(8,128)(2,1)}, bf16[96,578]{1,0:T(8,128)(2,1)S(1)}, u32[]{:S(2)}, u32[]{:S(2)}) collective-permute-start(bf16[96,578]{1,0:T(8,128)(2,1)} %get-tuple-element.118), channel_id=1, source_target_pairs={{0,28},{4,0},{8,4},{12,8},{16,12},{20,16},{24,20},{28,24},{1,29},{... | collective-permute-start | bytes 332936 | tf_op jit(solution)/shard_map/ppermute | solution.py:108
  404.3 11.8 %collective-permute-start.26 = (bf16[96,1738]{0,1:T(8,128)(2,1)S(1)}, bf16[96,1738]{0,1:T(8,128)(2,1)}, u32[]{:S(2)}, u32[]{:S(2)}) collective-permute-start(bf16[96,1738]{0,1:T(8,128)(2,1)S(1)} %slice.228), channel_id=1, source_target_pairs={{0,2},{1,3},{2,0},{3,1},{4,6},{5,7},{6,4},{7,5},{8,10},{9,11},{10,... | collective-permute-start | bytes 1001096 | tf_op jit(solution)/shard_map/ppermute | solution.py:86
  (99 other events, 1082.9 us)
Sparse Core Ops, SparseCore 0:
  14.4 59.2 all-gather.2
  76.5 75.9 all-gather.4
  256.2 135.6 reduce-scatter.3

commit v9 on v5

--- a/solution.py
+++ b/solution.py
@@ -96,6 +96,17 @@
             total.astype(jnp.bfloat16), "dp", scatter_dimension=0, tiled=True
         ).astype(jnp.float32)
 
+    def gather_dp_permutes(block):
+        if n_data > 8:
+            return gather_dp(block)
+        got = [block] + [
+            lax.ppermute(block, "dp", [(j, (j + k) % n_data) for j in range(n_data)])
+            for k in range(1, n_data)
+        ]
+        stacked = jnp.stack(got)
+        ordered = jnp.take(stacked, (data_index - jnp.arange(n_data)) % n_data, axis=0)
+        return ordered.reshape(n_data * block.shape[0], *block.shape[1:])
+
     def scatter_dp_permutes(total):
         if n_data > 8:
             return scatter_dp(total)
@@ -151,7 +162,8 @@
 
     attn_w = jnp.concatenate([project_weight, attention_output_weight], axis=1)
     feed_w = jnp.concatenate([feed_input_weight, feed_output_weight], axis=1)
-    attn_own = gather_dp(attn_w)
+    attn_own = gather_dp_permutes(attn_w)
+    feed_w, attn_own = lax.optimization_barrier((feed_w, attn_own))
     feed_own = gather_dp(feed_w)
     attn_part = to_chip_partner(attn_own)
     feed_part = to_chip_partner(feed_own)

time: 427 us -> 451 us (1.056)
  waiting for transfers between devices: 157 us -> 165 us
  matrix products: 113 us -> 119 us
  starting transfers between devices: 39.8 us -> 44.7 us
    ppermute x0 -> x7, waiting for transfers between devices: none -> 29.4 us  [gather_dp_permutes(): lax.ppermute(block, 'dp', [(j, (j + k) % n_data) for j in range(n_data)])]
    all_to_all x2, waiting for transfers between devices: 19.1 us -> 0.01 us  [deal(): here = lax.all_to_all(sent, 'dp', split_axis=1, concat_axis=0, tiled=True)]
    all_gather x2 -> x1, waiting for transfers between devices: 12.9 us -> 0.01 us  [gather_dp(): return lax.all_gather(block, 'dp', axis=0, tiled=True)]
    ppermute x8, waiting for transfers between devices: 86.5 us -> 95.8 us  [to_chip_partner(): return lax.ppermute(value, 'tensor', across_chips)]
    ppermute x0 -> x7, starting transfers between devices: none -> 7.91 us  [gather_dp_permutes(): lax.ppermute(block, 'dp', [(j, (j + k) % n_data) for j in range(n_data)])]
    unnamed x216 -> x210, local copies, waits for them, and re-layouts: 34.1 us -> 31.4 us
  transfers between devices with their start and end apart: 31 -> 37, of which waited for: 19 -> 21; matrix products, arithmetic and copies ran while one was open for 37% -> 37% of each run, Pallas kernels for 0% -> 0%
where the time goes in v9:
time: 451 us; the launch traced here: 442 us
  waiting for transfers between devices  165 us (37%)
  matrix products  119 us (26%)
  local copies, waits for them, and re-layouts  58.3 us (13%)
  starting transfers between devices  44.7 us (10%)
  other arithmetic  39.4 us (9%)
  between operations  16.2 us (4%)
    ppermute x8, waiting for transfers between devices, to_chip_partner(): return lax.ppermute(value, 'tensor', across_chips)  95.8 us
    dot_general x8, matrix products, dot_nn(): return jnp.dot(a, b, preferred_element_type=jnp.float32)  41.3 us
    ppermute x7, waiting for transfers between devices, scatter_dp_permutes(): lax.ppermute(sent, 'dp', [(j, (j + k) % n_data) for j in range(n_data)])  32 us
    unnamed x210, local copies, waits for them, and re-layouts  31.4 us
    ppermute x7, waiting for transfers between devices, gather_dp_permutes(): lax.ppermute(block, 'dp', [(j, (j + k) % n_data) for j in range(n_data)])  29.4 us
    dot_general x8, matrix products, dot_tn(): lax.dot_general(a, b, (((0,), (0,)), ((), ())), preferred_element_type=jn...  23.6 us
    dot_general x8, matrix products, dot_nt(): lax.dot_general(a, b, (((1,), (1,)), ((), ())), preferred_element_type=jn...  14.8 us
    dot_general x2, matrix products, attend_back(): jnp.einsum('qhe,khe->hqk', grad_heads, value_rows, preferred_element_type...  13.2 us
  transfers between devices with their start and end apart: 37, of which 21 were waited for; matrix products, arithmetic and copies ran while one was open for 37% of the time, Pallas kernels for 0%

profile of v9, /device:TPU:12, one launch (start us, length us, event | category | flops | bytes accessed | tf_op | source)
XLA Modules:
  0.0 442.4 jit_solution(17521469727037496574)
XLA Ops:
  17.9 6.1 %all-to-all-start = ((bf16[32,16,768]{2,0,1:T(8,128)(2,1)}), bf16[32,16,768]{2,0,1:T(8,128)(2,1)S(1)}, u32[]{:S(2)}, u32[]{:S(2)}) async-start(bf16[32,16,768]{2,0,1:T(8,128)(2,1)} %copy.99), calls=%async_computation | async-start | bytes 1572864 | tf_op jit(solution)/shard_map/all_to_all | solution.py:138
  25.6 5.0 %collective-permute-done.3 = bf16[96,768]{1,0:T(8,128)(2,1)S(1)} collective-permute-done((bf16[96,768]{1,0:T(8,128)(2,1)S(1)}, bf16[96,768]{1,0:T(8,128)(2,1)S(1)}, u32[]{:S(2)}, u32[]{:S(2)}) %collective-permute-start.3) | collective-permute-done | bytes 147488 | tf_op jit(solution)/shard_map/ppermute | solution.py:103
  30.6 6.5 %collective-permute-done.4 = bf16[96,768]{1,0:T(8,128)(2,1)S(1)} collective-permute-done((bf16[96,768]{1,0:T(8,128)(2,1)S(1)}, bf16[96,768]{1,0:T(8,128)(2,1)S(1)}, u32[]{:S(2)}, u32[]{:S(2)}) %collective-permute-start.4) | collective-permute-done | bytes 147488 | tf_op jit(solution)/shard_map/ppermute | solution.py:103
  37.0 7.6 %collective-permute-done.5 = bf16[96,768]{1,0:T(8,128)(2,1)S(1)} collective-permute-done((bf16[96,768]{1,0:T(8,128)(2,1)S(1)}, bf16[96,768]{1,0:T(8,128)(2,1)S(1)}, u32[]{:S(2)}, u32[]{:S(2)}) %collective-permute-start.5) | collective-permute-done | bytes 147488 | tf_op jit(solution)/shard_map/ppermute | solution.py:103
  44.7 9.2 %collective-permute-done.7 = bf16[96,768]{1,0:T(8,128)(2,1)S(1)} collective-permute-done((bf16[96,768]{1,0:T(8,128)(2,1)S(1)}, bf16[96,768]{1,0:T(8,128)(2,1)S(1)}, u32[]{:S(2)}, u32[]{:S(2)}) %collective-permute-start.7) | collective-permute-done | bytes 147488 | tf_op jit(solution)/shard_map/ppermute | solution.py:103
  59.3 8.7 %collective-permute-done = bf16[256,768]{1,0:T(8,128)(2,1)S(1)} collective-permute-done((bf16[256,768]{1,0:T(8,128)(2,1)S(1)}, bf16[256,768]{1,0:T(8,128)(2,1)S(1)}, u32[]{:S(2)}, u32[]{:S(2)}) %collective-permute-start) | collective-permute-done | bytes 393248 | tf_op jit(solution)/shard_map/ppermute | solution.py:86
  69.6 22.6 %collective-permute-done.9 = bf16[768,768]{1,0:T(8,128)(2,1)S(1)} collective-permute-done((bf16[768,768]{1,0:T(8,128)(2,1)}, bf16[768,768]{1,0:T(8,128)(2,1)S(1)}, u32[]{:S(2)}, u32[]{:S(2)}) %collective-permute-start.9) | collective-permute-done | bytes 1179680 | tf_op jit(solution)/shard_map/ppermute | solution.py:86
  92.3 2.7 add_convert_fusion.2
  95.1 3.0 add_convert_fusion.3
  102.4 2.9 copy-done.2
  112.0 2.9 copy-done.3
  126.3 4.2 all-to-all-start.1
  133.5 11.5 %multiply_convert_fusion.3 = (bf16[1024,768]{1,0:T(8,128)(2,1)S(1)}, f32[1024,768]{1,0:T(8,128)}, f32[1024,768]{1,0:T(8,128)}) fusion(f32[768]{0:T(1024)} %get-tuple-element.139, bf16[768,1536]{1,0:T(8,128)(2,1)} %all-gather.2.cloned.1.call-done, bf16[512,768]{1,0:T(8,128)(2,1)} %collective-permute-done.11, bf16[512,768]{1,0:T(8,128)(2,1)} %fusion.42), kind=kOutput, calls=%fused_computation.44 | convolution fusion | flops 1263009792 | bytes 10620928 | tf_op jit(solution)/shard_map/dot_general | solution.py:38
  146.4 38.7 %collective-permute-done.12 = bf16[768,1536]{1,0:T(8,128)(2,1)S(1)} collective-permute-done((bf16[768,1536]{1,0:T(8,128)(2,1)}, bf16[768,1536]{1,0:T(8,128)(2,1)S(1)}, u32[]{:S(2)}, u32[]{:S(2)}) %collective-permute-start.12) | collective-permute-done | bytes 2359328 | tf_op jit(solution)/shard_map/ppermute | solution.py:86
  185.1 11.8 %multiply_convert_fusion.2 = (bf16[1024,768]{1,0:T(8,128)(2,1)S(1)}, f32[1024,768]{1,0:T(8,128)}, f32[1024,768]{1,0:T(8,128)}) fusion(f32[768]{0:T(1024)S(1)} %copy-done.74, bf16[768,1536]{1,0:T(8,128)(2,1)S(1)} %collective-permute-done.12, bf16[512,768]{1,0:T(8,128)(2,1)} %collective-permute-done.11, bf16[512,768]{1,0:T(8,128)(2,1)} %fusion.42), kind=kOutput, calls=%fused_computation.31 | convolution fusion | flops 1263009792 | bytes 10620928 | tf_op jit(solution)/shard_map/dot_general | solution.py:38
  205.8 6.9 %collective-permute-done.15 = bf16[256,768]{1,0:T(8,128)(2,1)S(1)} collective-permute-done((bf16[256,768]{1,0:T(8,128)(2,1)S(1)}, bf16[256,768]{1,0:T(8,128)(2,1)S(1)}, u32[]{:S(2)}, u32[]{:S(2)}) %collective-permute-start.15) | collective-permute-done | bytes 393248 | tf_op jit(solution)/shard_map/ppermute | solution.py:86
  217.1 3.8 convert_reduce_fusion.1
  225.0 3.8 convert_reduce_fusion
  239.7 4.5 %fusion.41 = bf16[768,3466]{0,1:T(8,128)(2,1)} fusion(bf16[1024,768]{1,0:T(8,128)(2,1)} %copy-done.88, bf16[512,768]{1,0:T(8,128)(2,1)} %collective-permute-done.11, bf16[512,768]{1,0:T(8,128)(2,1)} %fusion.42), kind=kOutput, calls=%fused_computation.111 | convolution fusion | flops 1211695104 | bytes 4325376 | tf_op jit(solution)/shard_map/dot_general | solution.py:34
  254.7 4.1 fusion.39
  264.5 8.0 %copy.133 = bf16[768,3466]{1,0:T(8,128)(2,1)} copy(bf16[768,3466]{0,1:T(8,128)(2,1)} %constant_dynamic-update-slice_fusion) | data formatting | bytes 10647552
  272.5 10.4 %multiply_reduce_fusion.1 = (f32[3,1024]{1,0:T(4,128)S(1)}, f32[3,1024,1024]{1,2,0:T(8,128)}) fusion(f32[3,1024,1024]{1,2,0:T(8,128)} %copy-done.3, f32[3,1024]{1,0:T(4,128)S(1)} %log_add_fusion.1, bf16[1024,3,64]{0,2,1:T(8,128)(2,1)S(1)} %bitcast.212, bf16[1024,3,64]{0,2,1:T(8,128)(2,1)S(1)} %bitcast.217), kind=kOutput, calls=%fused_computation.5 | convolution fusion | flops 412087296 | bytes 25976832 | tf_op jit(solution)/shard_map/qhe,khe->hqk/dot_general | solution.py:220
  285.2 6.9 %multiply_convert_fusion.1 = bf16[3,1024,1024]{1,2,0:T(8,128)(2,1)S(1)} fusion(f32[3,1024,1024]{1,2,0:T(8,128)} %get-tuple-element.167, f32[3,1024,1024]{1,2,0:T(8,128)S(1)} %bitcast.185, f32[3,1024]{1,0:T(4,128)S(1)} %get-tuple-element.166, f32[3,1024]{1,0:T(4,128)S(1)} %log_add_fusion.1), kind=kLoop, calls=%fused_computation.4 | loop fusion | flops 12582912 | bytes 31481856 | tf_op jit(solution)/shard_map/convert_element_type | solution.py:224
  297.5 4.9 %fusion.80 = f32[1024,768]{1,0:T(8,128)} fusion(bf16[768,768]{1,0:T(8,128)(2,1)} %bitcast_select_fusion, bf16[1024,192]{0,1:T(8,128)(2,1)S(1)} %bitcast.218, bf16[1024,192]{0,1:T(8,128)(2,1)S(1)} %bitcast.224, bf16[1024,192]{0,1:T(8,128)(2,1)S(1)} %bitcast.221), kind=kOutput, calls=%fused_computation.162 | convolution fusion | flops 909508608 | bytes 5308416 | tf_op jit(solution)/shard_map/dot_general | solution.py:30
  302.4 2.8 multiply_reduce_fusion
  305.2 5.5 %multiply_convert_fusion = bf16[3,1024,1024]{1,2,0:T(8,128)(2,1)} fusion(f32[3,1024,1024]{1,2,0:T(8,128)S(1)} %get-tuple-element.169, f32[3,1024,1024]{1,2,0:T(8,128)S(1)} %bitcast.183, f32[3,1024]{1,0:T(4,128)S(1)} %get-tuple-element.168, f32[3,1024]{1,0:T(4,128)S(1)} %log_add_fusion), kind=kLoop, calls=%fused_computation.1 | loop fusion | flops 12582912 | bytes 31481856 | tf_op jit(solution)/shard_map/convert_element_type | solution.py:224
  310.7 4.2 fusion.48
  337.3 7.1 %collective-permute-done.21 = bf16[256,768]{1,0:T(8,128)(2,1)} collective-permute-done((bf16[256,768]{1,0:T(8,128)(2,1)}, bf16[256,768]{1,0:T(8,128)(2,1)}, u32[]{:S(2)}, u32[]{:S(2)}) %collective-permute-start.21) | collective-permute-done | bytes 393248 | tf_op jit(solution)/shard_map/ppermute | solution.py:86
  347.2 6.2 %all-to-all-start.2 = ((bf16[256,2,768]{2,1,0:T(2,128)(2,1)}), bf16[256,2,768]{2,1,0:T(2,128)(2,1)}, u32[]{:S(2)}, u32[]{:S(2)}) async-start(bf16[256,2,768]{2,1,0:T(2,128)(2,1)} %copy.113), calls=%async_computation.2 | async-start | bytes 1572864 | tf_op jit(solution)/shard_map/all_to_all | solution.py:392
  355.6 8.0 %collective-permute-done.23 = bf16[768,578]{0,1:T(8,128)(2,1)} collective-permute-done((bf16[768,578]{0,1:T(8,128)(2,1)}, bf16[768,578]{0,1:T(8,128)(2,1)}, u32[]{:S(2)}, u32[]{:S(2)}) %collective-permute-start.23) | collective-permute-done | bytes 887840 | tf_op jit(solution)/shard_map/ppermute | solution.py:86
  377.4 27.0 %collective-permute-done.24 = bf16[96,578]{1,0:T(8,128)(2,1)S(1)} collective-permute-done((bf16[96,578]{1,0:T(8,128)(2,1)S(1)}, bf16[96,578]{1,0:T(8,128)(2,1)S(1)}, u32[]{:S(2)}, u32[]{:S(2)}) %collective-permute-start.24) | collective-permute-done | bytes 111008 | tf_op jit(solution)/shard_map/ppermute | solution.py:119
  423.3 3.9 collective-permute-done.31
  (411 shorter events, 165.0 us)
Async XLA Ops:
  8.3 16.6 %collective-permute-start.2 = (bf16[96,768]{1,0:T(8,128)(2,1)S(1)}, bf16[96,768]{1,0:T(8,128)(2,1)S(1)}, u32[]{:S(2)}, u32[]{:S(2)}) collective-permute-start(bf16[96,768]{1,0:T(8,128)(2,1)S(1)} %get-tuple-element.111), channel_id=1, source_target_pairs={{0,4},{4,8},{8,12},{12,16},{16,20},{20,24},{24,28},{28,0},{1,5},{5... | collective-permute-start | bytes 442376 | tf_op jit(solution)/shard_map/ppermute | solution.py:103
  9.9 20.7 %collective-permute-start.3 = (bf16[96,768]{1,0:T(8,128)(2,1)S(1)}, bf16[96,768]{1,0:T(8,128)(2,1)S(1)}, u32[]{:S(2)}, u32[]{:S(2)}) collective-permute-start(bf16[96,768]{1,0:T(8,128)(2,1)S(1)} %get-tuple-element.111), channel_id=1, source_target_pairs={{0,8},{4,12},{8,16},{12,20},{16,24},{20,28},{24,0},{28,4},{1,9},{5... | collective-permute-start | bytes 442376 | tf_op jit(solution)/shard_map/ppermute | solution.py:103
  11.5 25.6 %collective-permute-start.4 = (bf16[96,768]{1,0:T(8,128)(2,1)S(1)}, bf16[96,768]{1,0:T(8,128)(2,1)S(1)}, u32[]{:S(2)}, u32[]{:S(2)}) collective-permute-start(bf16[96,768]{1,0:T(8,128)(2,1)S(1)} %get-tuple-element.111), channel_id=1, source_target_pairs={{0,12},{4,16},{8,20},{12,24},{16,28},{20,0},{24,4},{28,8},{1,13},{... | collective-permute-start | bytes 442376 | tf_op jit(solution)/shard_map/ppermute | solution.py:103
  12.7 32.0 %collective-permute-start.5 = (bf16[96,768]{1,0:T(8,128)(2,1)S(1)}, bf16[96,768]{1,0:T(8,128)(2,1)S(1)}, u32[]{:S(2)}, u32[]{:S(2)}) collective-permute-start(bf16[96,768]{1,0:T(8,128)(2,1)S(1)} %get-tuple-element.111), channel_id=1, source_target_pairs={{0,16},{4,20},{8,24},{12,28},{16,0},{20,4},{24,8},{28,12},{1,17},{... | collective-permute-start | bytes 442376 | tf_op jit(solution)/shard_map/ppermute | solution.py:103
  14.3 30.4 %collective-permute-start.6 = (bf16[96,768]{1,0:T(8,128)(2,1)S(1)}, bf16[96,768]{1,0:T(8,128)(2,1)S(1)}, u32[]{:S(2)}, u32[]{:S(2)}) collective-permute-start(bf16[96,768]{1,0:T(8,128)(2,1)S(1)} %get-tuple-element.111), channel_id=1, source_target_pairs={{0,20},{4,24},{8,28},{12,0},{16,4},{20,8},{24,12},{28,16},{1,21},{... | collective-permute-start | bytes 442376 | tf_op jit(solution)/shard_map/ppermute | solution.py:103
  17.9 37.8 %all-to-all-start = ((bf16[32,16,768]{2,0,1:T(8,128)(2,1)}), bf16[32,16,768]{2,0,1:T(8,128)(2,1)S(1)}, u32[]{:S(2)}, u32[]{:S(2)}) async-start(bf16[32,16,768]{2,0,1:T(8,128)(2,1)} %copy.99), calls=%async_computation | async-start | bytes 1572864 | tf_op jit(solution)/shard_map/all_to_all | solution.py:138
  24.0 107.9 %all-gather.2.cloned.1.call-start = ((), (), s32[]{:S(2)}) async-start(), calls=%async_computation.4 | async-start | bytes 2654208 | tf_op jit(solution)/shard_map/all_gather | solution.py:92
  25.0 28.9 %collective-permute-start.7 = (bf16[96,768]{1,0:T(8,128)(2,1)S(1)}, bf16[96,768]{1,0:T(8,128)(2,1)S(1)}, u32[]{:S(2)}, u32[]{:S(2)}) collective-permute-start(bf16[96,768]{1,0:T(8,128)(2,1)S(1)} %get-tuple-element.111), channel_id=1, source_target_pairs={{0,24},{4,28},{8,0},{12,4},{16,8},{20,12},{24,16},{28,20},{1,25},{... | collective-permute-start | bytes 442376 | tf_op jit(solution)/shard_map/ppermute | solution.py:103
  30.6 24.5 %collective-permute-start.8 = (bf16[96,768]{1,0:T(8,128)(2,1)S(1)}, bf16[96,768]{1,0:T(8,128)(2,1)S(1)}, u32[]{:S(2)}, u32[]{:S(2)}) collective-permute-start(bf16[96,768]{1,0:T(8,128)(2,1)S(1)} %get-tuple-element.111), channel_id=1, source_target_pairs={{0,28},{4,0},{8,4},{12,8},{16,12},{20,16},{24,20},{28,24},{1,29},{... | collective-permute-start | bytes 442376 | tf_op jit(solution)/shard_map/ppermute | solution.py:103
  55.9 12.1 %collective-permute-start = (bf16[256,768]{1,0:T(8,128)(2,1)S(1)}, bf16[256,768]{1,0:T(8,128)(2,1)S(1)}, u32[]{:S(2)}, u32[]{:S(2)}) collective-permute-start(bf16[256,768]{1,0:T(8,128)(2,1)S(1)} %get-tuple-element.135), channel_id=1, source_target_pairs={{0,2},{1,3},{2,0},{3,1},{4,6},{5,7},{6,4},{7,5},{8,10},{9,11},{10,... | collective-permute-start | bytes 1179656 | tf_op jit(solution)/shard_map/ppermute | solution.py:86
  58.7 33.6 %collective-permute-start.9 = (bf16[768,768]{1,0:T(8,128)(2,1)}, bf16[768,768]{1,0:T(8,128)(2,1)S(1)}, u32[]{:S(2)}, u32[]{:S(2)}) collective-permute-start(bf16[768,768]{1,0:T(8,128)(2,1)} %bitcast_select_fusion), channel_id=1, source_target_pairs={{0,2},{1,3},{2,0},{3,1},{4,6},{5,7},{6,4},{7,5},{8,10},{9,11},{10,... | collective-permute-start | bytes 3538952 | tf_op jit(solution)/shard_map/ppermute | solution.py:86
  68.0 24.3 %collective-permute-start.1 = (bf16[512,768]{1,0:T(8,128)(2,1)S(1)}, bf16[512,768]{1,0:T(8,128)(2,1)}, u32[]{:S(2)}, u32[]{:S(2)}) collective-permute-start(bf16[512,768]{1,0:T(8,128)(2,1)S(1)} %pad_maximum_fusion.7), channel_id=1, source_target_pairs={{0,1},{1,0},{2,3},{3,2},{4,5},{5,4},{6,7},{7,6},{8,9},{9,8},{10,11... | collective-permute-start | bytes 2359304 | tf_op jit(solution)/shard_map/ppermute | solution.py:89
  124.5 8.9 %collective-permute-start.11 = (bf16[512,768]{1,0:T(8,128)(2,1)}, bf16[512,768]{1,0:T(8,128)(2,1)}, u32[]{:S(2)}, u32[]{:S(2)}) collective-permute-start(bf16[512,768]{1,0:T(8,128)(2,1)} %fusion.42), channel_id=1, source_target_pairs={{0,1},{1,0},{2,3},{3,2},{4,5},{5,4},{6,7},{7,6},{8,9},{9,8},{10,11... | collective-permute-start | bytes 2359304 | tf_op jit(solution)/shard_map/ppermute | solution.py:89
  126.3 74.7 %all-to-all-start.1 = ((bf16[32,16,768]{2,0,1:T(8,128)(2,1)}), bf16[32,16,768]{2,0,1:T(8,128)(2,1)S(1)}, u32[]{:S(2)}, u32[]{:S(2)}) async-start(bf16[32,16,768]{2,0,1:T(8,128)(2,1)} %copy.104), calls=%async_computation.1 | async-start | bytes 1572864 | tf_op jit(solution)/shard_map/all_to_all | solution.py:138
  130.5 284.5 %reduce-scatter.4.cloned.1.call-start = ((), (), s32[]{:S(2)}) async-start(), calls=%async_computation.5 | async-start | bytes 6193152
  131.9 53.1 %collective-permute-start.12 = (bf16[768,1536]{1,0:T(8,128)(2,1)}, bf16[768,1536]{1,0:T(8,128)(2,1)S(1)}, u32[]{:S(2)}, u32[]{:S(2)}) collective-permute-start(bf16[768,1536]{1,0:T(8,128)(2,1)} %all-gather.2.cloned.1.call-done), channel_id=1, source_target_pairs={{0,2},{1,3},{2,0},{3,1},{4,6},{5,7},{6,4},{7,5},{8,10},{9,11},{10,... | collective-permute-start | bytes 7077896 | tf_op jit(solution)/shard_map/ppermute | solution.py:86
  201.2 11.6 %collective-permute-start.15 = (bf16[256,768]{1,0:T(8,128)(2,1)S(1)}, bf16[256,768]{1,0:T(8,128)(2,1)S(1)}, u32[]{:S(2)}, u32[]{:S(2)}) collective-permute-start(bf16[256,768]{1,0:T(8,128)(2,1)S(1)} %get-tuple-element.133), channel_id=1, source_target_pairs={{0,2},{1,3},{2,0},{3,1},{4,6},{5,7},{6,4},{7,5},{8,10},{9,11},{10,... | collective-permute-start | bytes 1179656 | tf_op jit(solution)/shard_map/ppermute | solution.py:86
  237.4 10.0 %collective-permute-start.18 = (bf16[512,768]{1,0:T(8,128)(2,1)}, bf16[512,768]{1,0:T(8,128)(2,1)}, u32[]{:S(2)}, u32[]{:S(2)}) collective-permute-start(bf16[512,768]{1,0:T(8,128)(2,1)} %convert_element_type.192), channel_id=1, source_target_pairs={{0,1},{1,0},{2,3},{3,2},{4,5},{5,4},{6,7},{7,6},{8,9},{9,8},{10,11... | collective-permute-start | bytes 2359304 | tf_op jit(solution)/shard_map/ppermute | solution.py:89
  247.0 16.9 %collective-permute-start.19 = (f32[768,10]{0,1:T(8,128)S(1)}, f32[768,10]{0,1:T(8,128)S(1)}, u32[]{:S(2)}, u32[]{:S(2)}) collective-permute-start(f32[768,10]{0,1:T(8,128)S(1)} %concatenate.63), channel_id=1, source_target_pairs={{0,1},{1,0},{2,3},{3,2},{4,5},{5,4},{6,7},{7,6},{8,9},{9,8},{10,11... | collective-permute-start | bytes 92168 | tf_op jit(solution)/shard_map/ppermute | solution.py:89
  326.4 7.1 %collective-permute-start.22 = (f32[768,2]{0,1:T(2,128)S(1)}, f32[768,2]{0,1:T(2,128)S(1)}, u32[]{:S(2)}, u32[]{:S(2)}) collective-permute-start(f32[768,2]{0,1:T(2,128)S(1)} %pad_maximum_fusion.13), channel_id=1, source_target_pairs={{0,1},{1,0},{2,3},{3,2},{4,5},{5,4},{6,7},{7,6},{8,9},{9,8},{10,11... | collective-permute-start | bytes 18440 | tf_op jit(solution)/shard_map/ppermute | solution.py:89
  332.1 12.3 %collective-permute-start.21 = (bf16[256,768]{1,0:T(8,128)(2,1)}, bf16[256,768]{1,0:T(8,128)(2,1)}, u32[]{:S(2)}, u32[]{:S(2)}) collective-permute-start(bf16[256,768]{1,0:T(8,128)(2,1)} %slice.233), channel_id=1, source_target_pairs={{0,2},{1,3},{2,0},{3,1},{4,6},{5,7},{6,4},{7,5},{8,10},{9,11},{10,... | collective-permute-start | bytes 1179656 | tf_op jit(solution)/shard_map/ppermute | solution.py:86
  334.5 29.1 %collective-permute-start.23 = (bf16[768,578]{0,1:T(8,128)(2,1)}, bf16[768,578]{0,1:T(8,128)(2,1)}, u32[]{:S(2)}, u32[]{:S(2)}) collective-permute-start(bf16[768,578]{0,1:T(8,128)(2,1)} %pad_maximum_fusion.6), channel_id=1, source_target_pairs={{0,2},{1,3},{2,0},{3,1},{4,6},{5,7},{6,4},{7,5},{8,10},{9,11},{10,... | collective-permute-start | bytes 2663432 | tf_op jit(solution)/shard_map/ppermute | solution.py:86
  335.9 35.7 %collective-permute-start.14 = (bf16[256,768]{1,0:T(8,128)(2,1)}, bf16[256,768]{1,0:T(8,128)(2,1)}, u32[]{:S(2)}, u32[]{:S(2)}) collective-permute-start(bf16[256,768]{1,0:T(8,128)(2,1)} %slice.227), channel_id=1, source_target_pairs={{0,2},{1,3},{2,0},{3,1},{4,6},{5,7},{6,4},{7,5},{8,10},{9,11},{10,... | collective-permute-start | bytes 1179656 | tf_op jit(solution)/shard_map/ppermute | solution.py:86
  347.2 72.7 %all-to-all-start.2 = ((bf16[256,2,768]{2,1,0:T(2,128)(2,1)}), bf16[256,2,768]{2,1,0:T(2,128)(2,1)}, u32[]{:S(2)}, u32[]{:S(2)}) async-start(bf16[256,2,768]{2,1,0:T(2,128)(2,1)} %copy.113), calls=%async_computation.2 | async-start | bytes 1572864 | tf_op jit(solution)/shard_map/all_to_all | solution.py:392
  368.5 36.0 %collective-permute-start.24 = (bf16[96,578]{1,0:T(8,128)(2,1)S(1)}, bf16[96,578]{1,0:T(8,128)(2,1)S(1)}, u32[]{:S(2)}, u32[]{:S(2)}) collective-permute-start(bf16[96,578]{1,0:T(8,128)(2,1)S(1)} %get-tuple-element.123), channel_id=1, source_target_pairs={{0,4},{4,8},{8,12},{12,16},{16,20},{20,24},{24,28},{28,0},{1,5},{5... | collective-permute-start | bytes 332936 | tf_op jit(solution)/shard_map/ppermute | solution.py:119
  370.0 37.1 %collective-permute-start.25 = (bf16[96,578]{1,0:T(8,128)(2,1)S(1)}, bf16[96,578]{1,0:T(8,128)(2,1)S(1)}, u32[]{:S(2)}, u32[]{:S(2)}) collective-permute-start(bf16[96,578]{1,0:T(8,128)(2,1)S(1)} %get-tuple-element.129), channel_id=1, source_target_pairs={{0,8},{4,12},{8,16},{12,20},{16,24},{20,28},{24,0},{28,4},{1,9},{5... | collective-permute-start | bytes 332936 | tf_op jit(solution)/shard_map/ppermute | solution.py:119
  372.6 38.0 %collective-permute-start.26 = (bf16[96,578]{1,0:T(8,128)(2,1)}, bf16[96,578]{1,0:T(8,128)(2,1)S(1)}, u32[]{:S(2)}, u32[]{:S(2)}) collective-permute-start(bf16[96,578]{1,0:T(8,128)(2,1)} %get-tuple-element.128), channel_id=1, source_target_pairs={{0,12},{4,16},{8,20},{12,24},{16,28},{20,0},{24,4},{28,8},{1,13},{... | collective-permute-start | bytes 332936 | tf_op jit(solution)/shard_map/ppermute | solution.py:119
  374.5 36.8 %collective-permute-start.27 = (bf16[96,578]{1,0:T(8,128)(2,1)}, bf16[96,578]{1,0:T(8,128)(2,1)S(1)}, u32[]{:S(2)}, u32[]{:S(2)}) collective-permute-start(bf16[96,578]{1,0:T(8,128)(2,1)} %get-tuple-element.127), channel_id=1, source_target_pairs={{0,16},{4,20},{8,24},{12,28},{16,0},{20,4},{24,8},{28,12},{1,17},{... | collective-permute-start | bytes 332936 | tf_op jit(solution)/shard_map/ppermute | solution.py:119
  375.5 35.8 %collective-permute-start.28 = (bf16[96,578]{1,0:T(8,128)(2,1)}, bf16[96,578]{1,0:T(8,128)(2,1)S(1)}, u32[]{:S(2)}, u32[]{:S(2)}) collective-permute-start(bf16[96,578]{1,0:T(8,128)(2,1)} %get-tuple-element.126), channel_id=1, source_target_pairs={{0,20},{4,24},{8,28},{12,0},{16,4},{20,8},{24,12},{28,16},{1,21},{... | collective-permute-start | bytes 332936 | tf_op jit(solution)/shard_map/ppermute | solution.py:119
  404.4 8.6 %collective-permute-start.29 = (bf16[96,578]{1,0:T(8,128)(2,1)}, bf16[96,578]{1,0:T(8,128)(2,1)S(1)}, u32[]{:S(2)}, u32[]{:S(2)}) collective-permute-start(bf16[96,578]{1,0:T(8,128)(2,1)} %get-tuple-element.125), channel_id=1, source_target_pairs={{0,24},{4,28},{8,0},{12,4},{16,8},{20,12},{24,16},{28,20},{1,25},{... | collective-permute-start | bytes 332936 | tf_op jit(solution)/shard_map/ppermute | solution.py:119
  407.1 6.1 %collective-permute-start.30 = (bf16[96,578]{1,0:T(8,128)(2,1)}, bf16[96,578]{1,0:T(8,128)(2,1)S(1)}, u32[]{:S(2)}, u32[]{:S(2)}) collective-permute-start(bf16[96,578]{1,0:T(8,128)(2,1)} %get-tuple-element.124), channel_id=1, source_target_pairs={{0,28},{4,0},{8,4},{12,8},{16,12},{20,16},{24,20},{28,24},{1,29},{... | collective-permute-start | bytes 332936 | tf_op jit(solution)/shard_map/ppermute | solution.py:119
  417.0 10.2 %collective-permute-start.31 = (bf16[96,1738]{0,1:T(8,128)(2,1)S(1)}, bf16[96,1738]{0,1:T(8,128)(2,1)}, u32[]{:S(2)}, u32[]{:S(2)}) collective-permute-start(bf16[96,1738]{0,1:T(8,128)(2,1)S(1)} %slice.238), channel_id=1, source_target_pairs={{0,2},{1,3},{2,0},{3,1},{4,6},{5,7},{6,4},{7,5},{8,10},{9,11},{10,... | collective-permute-start | bytes 1001096 | tf_op jit(solution)/shard_map/ppermute | solution.py:86
  (104 other events, 1036.0 us)
Sparse Core Ops, SparseCore 0:
  69.8 50.1 all-gather.1
  272.6 133.0 reduce-scatter.3

commit v10 on v5

--- a/solution.py
+++ b/solution.py
@@ -4,6 +4,7 @@
 import jax.numpy as jnp
 from jax import lax
 from jax.sharding import PartitionSpec as P
+
 
 HD = 64
 
@@ -77,7 +78,6 @@
     score_scale = HD ** (-0.5)
 
     chip_side = tensor_index // 2
-    core = tensor_index % 2
     partner_slice = tensor_index ^ 2
     across_chips = [(k, k ^ 2) for k in range(n_tensor)]
     across_cores = [(k, k ^ 1) for k in range(n_tensor)]
@@ -120,17 +120,20 @@
 
     slot_ids = jnp.arange(seq_total, dtype=jnp.int32)
     placing = (dealing[None, :] == slot_ids[:, None]).astype(jnp.bfloat16)
-    def deal(values):
+
+    def deal(values, after=None):
         sent = jnp.einsum(
             "qs,psd->pqd", placing, values, preferred_element_type=jnp.float32
         ).astype(jnp.bfloat16)
+        if after is not None:
+            sent, after = lax.optimization_barrier((sent, after))
         here = lax.all_to_all(sent, "dp", split_axis=1, concat_axis=0, tiled=True)
         slot_mine = lax.dynamic_index_in_dim(here, chip_side, axis=1, keepdims=False)
         slot_other = lax.dynamic_index_in_dim(here, 1 - chip_side, axis=1, keepdims=False)
-        return jnp.concatenate([slot_mine, to_chip_partner(slot_other)], axis=0)
+        crossed = to_chip_partner(slot_other)
+        return jnp.concatenate([slot_mine, crossed], axis=0)
 
     inputs_mine = deal(tokens)
-    cot_mine = deal(output_grad)
     inputs_full = jnp.concatenate([inputs_mine, to_core_partner(inputs_mine)], axis=0)
 
     my_slot = data_index * seq_here + chip_side
@@ -155,6 +158,7 @@
     feed_own = gather_dp(feed_w)
     attn_part = to_chip_partner(attn_own)
     feed_part = to_chip_partner(feed_own)
+    cot_mine = deal(output_grad, feed_own)
     slices = (tensor_index, partner_slice)
     attn_sets = (attn_own, attn_part)
     feed_sets = (feed_own, feed_part)
@@ -247,9 +251,12 @@
         inputs_mine.astype(jnp.float32) + branch + attention_output_bias, first_gain, first_shift
     )
     first_full = gather_cores(first)
-    preact = [dot_nn(first_full, up_ws[g]) + up_biases[g] for g in groups]
-    gelu_pairs = [jax.vjp(gelu_exact, preact[g]) for g in groups]
-    hidden = [p[0].astype(jnp.bfloat16) for p in gelu_pairs]
+    preact = [dot_nn(first_full, up_ws[0]) + up_biases[0]]
+    gelu_pairs = [jax.vjp(gelu_exact, preact[0])]
+    hidden = [gelu_pairs[0][0].astype(jnp.bfloat16)]
+    preact.append(dot_nn(first_full, up_ws[1]) + up_biases[1])
+    gelu_pairs.append(jax.vjp(gelu_exact, preact[1]))
+    hidden.append(gelu_pairs[1][0].astype(jnp.bfloat16))
     feed = scatter_cores(sum(dot_nt(hidden[g], down_ws[g]) for g in groups))
     second, normed_second, inverse_second = norm_forward(
         first + feed + feed_output_bias, second_gain, second_shift
@@ -438,6 +445,7 @@
         P(("dp", "tensor")),
         P(("dp", "tensor")),
     )
+
     return jax.shard_map(
         on_device, mesh=mesh, in_specs=in_specs, out_specs=out_specs, check_vma=False
     )

time: 427 us -> 433 us (1.014)
  waiting for transfers between devices: 157 us -> 164 us
    all_gather x2, waiting for transfers between devices: 12.9 us -> 18.8 us  [gather_dp(): return lax.all_gather(block, 'dp', axis=0, tiled=True)]
  transfers between devices with their start and end apart: 31 -> 31, of which waited for: 19 -> 19; matrix products, arithmetic and copies ran while one was open for 37% -> 36% of each run, Pallas kernels for 0% -> 0%
where the time goes in v10:
time: 433 us; the launch traced here: 426 us
  waiting for transfers between devices  164 us (38%)
  matrix products  114 us (26%)
  local copies, waits for them, and re-layouts  57.5 us (13%)
  starting transfers between devices  38.4 us (9%)
  other arithmetic  36.5 us (8%)
  between operations  15.7 us (4%)
    ppermute x8, waiting for transfers between devices, to_chip_partner(): return lax.ppermute(value, 'tensor', across_chips)  85.9 us
    dot_general x8, matrix products, dot_nn(): return jnp.dot(a, b, preferred_element_type=jnp.float32)  40.4 us
    unnamed x216, local copies, waits for them, and re-layouts  34.1 us
    ppermute x7, waiting for transfers between devices, scatter_dp_permutes(): lax.ppermute(sent, 'dp', [(j, (j + k) % n_data) for j in range(n_data)])  32.1 us
    dot_general x8, matrix products, dot_tn(): lax.dot_general(a, b, (((0,), (0,)), ((), ())), preferred_element_type=jn...  23.1 us
    all_to_all x2, waiting for transfers between devices, deal(): here = lax.all_to_all(sent, 'dp', split_axis=1, concat_axis=0, tiled=True)  19.1 us
    all_gather x2, waiting for transfers between devices, gather_dp(): return lax.all_gather(block, 'dp', axis=0, tiled=True)  18.8 us
    convert_element_type x2, other arithmetic, attend_back(): grad_scores = (weights * (grad_weights - inner_sum)).astype(jnp.bfloat16)  12.4 us
  transfers between devices with their start and end apart: 31, of which 19 were waited for; matrix products, arithmetic and copies ran while one was open for 36% of the time, Pallas kernels for 0%

profile of v10, /device:TPU:12, one launch (start us, length us, event | category | flops | bytes accessed | tf_op | source)
XLA Modules:
  0.0 425.8 jit_solution(3300412043417482520)
XLA Ops:
  10.6 6.4 %all-to-all-start = ((bf16[32,16,768]{2,0,1:T(8,128)(2,1)}), bf16[32,16,768]{2,0,1:T(8,128)(2,1)S(1)}, u32[]{:S(2)}, u32[]{:S(2)}) async-start(bf16[32,16,768]{2,0,1:T(8,128)(2,1)} %copy.99), calls=%async_computation | async-start | bytes 1572864 | tf_op jit(solution)/shard_map/all_to_all | solution.py:130
  17.9 19.1 %all-to-all-done = bf16[32,16,768]{2,0,1:T(8,128)(2,1)S(1)} async-done(((bf16[32,16,768]{2,0,1:T(8,128)(2,1)}), bf16[32,16,768]{2,0,1:T(8,128)(2,1)S(1)}, u32[]{:S(2)}, u32[]{:S(2)}) %all-to-all-start) | async-done | bytes 786464 | tf_op jit(solution)/shard_map/all_to_all | solution.py:130
  38.7 9.2 %collective-permute-done = bf16[256,768]{1,0:T(8,128)(2,1)S(1)} collective-permute-done((bf16[256,768]{1,0:T(8,128)(2,1)S(1)}, bf16[256,768]{1,0:T(8,128)(2,1)S(1)}, u32[]{:S(2)}, u32[]{:S(2)}) %collective-permute-start) | collective-permute-done | bytes 393248 | tf_op jit(solution)/shard_map/ppermute | solution.py:86
  50.3 11.4 %all-gather.3.cloned.1.call-done = bf16[768,768]{1,0:T(8,128)(2,1)} async-done(((bf16[96,768]{1,0:T(8,128)(2,1)}), bf16[768,768]{1,0:T(8,128)(2,1)}) %all-gather.3.cloned.1.call-update) | async-done | bytes 1179664 | tf_op jit(solution)/shard_map/all_gather | solution.py:92
  70.1 2.9 copy-done.2
  73.0 2.8 fusion.57
  77.8 11.0 %collective-permute-done.2 = bf16[768,768]{1,0:T(8,128)(2,1)S(1)} collective-permute-done((bf16[768,768]{1,0:T(8,128)(2,1)}, bf16[768,768]{1,0:T(8,128)(2,1)S(1)}, u32[]{:S(2)}, u32[]{:S(2)}) %collective-permute-start.2) | collective-permute-done | bytes 1179680 | tf_op jit(solution)/shard_map/ppermute | solution.py:86
  88.8 2.7 add_convert_fusion.2
  95.8 2.9 copy-done.3
  108.4 7.4 %all-gather.5.cloned.1.call-done = bf16[768,1536]{1,0:T(8,128)(2,1)} async-done(((bf16[96,1536]{1,0:T(8,128)(2,1)}), bf16[768,1536]{1,0:T(8,128)(2,1)}) %all-gather.5.cloned.1.call-update) | async-done | bytes 2359312 | tf_op jit(solution)/shard_map/all_gather | solution.py:92
  116.9 4.9 %all-to-all-start.1 = ((bf16[32,16,768]{2,0,1:T(8,128)(2,1)}), bf16[32,16,768]{2,0,1:T(8,128)(2,1)S(1)}, u32[]{:S(2)}, u32[]{:S(2)}) async-start(bf16[32,16,768]{2,0,1:T(8,128)(2,1)} %copy.104), calls=%async_computation.1 | async-start | bytes 1572864 | tf_op jit(solution)/shard_map/all_to_all | solution.py:130
  123.3 11.5 %multiply_convert_fusion.3 = (bf16[1024,768]{1,0:T(8,128)(2,1)S(1)}, f32[1024,768]{1,0:T(8,128)}, f32[1024,768]{1,0:T(8,128)}) fusion(f32[768]{0:T(1024)S(1)} %copy-done.79, bf16[768,1536]{1,0:T(8,128)(2,1)} %all-gather.5.cloned.1.call-done, bf16[512,768]{1,0:T(8,128)(2,1)} %collective-permute-done.4, bf16[512,768]{1,0:T(8,128)(2,1)} %fusion.42), kind=kOutput, calls=%fused_computation.43 | convolution fusion | flops 1263009792 | bytes 10619904 | tf_op jit(solution)/shard_map/dot_general | solution.py:39
  136.2 37.3 %collective-permute-done.5 = bf16[768,1536]{1,0:T(8,128)(2,1)S(1)} collective-permute-done((bf16[768,1536]{1,0:T(8,128)(2,1)}, bf16[768,1536]{1,0:T(8,128)(2,1)S(1)}, u32[]{:S(2)}, u32[]{:S(2)}) %collective-permute-start.5) | collective-permute-done | bytes 2359328 | tf_op jit(solution)/shard_map/ppermute | solution.py:86
  173.5 11.6 %multiply_convert_fusion.2 = (bf16[1024,768]{1,0:T(8,128)(2,1)S(1)}, f32[1024,768]{1,0:T(8,128)}, f32[1024,768]{1,0:T(8,128)}) fusion(f32[768]{0:T(1024)S(1)} %copy-done.77, bf16[768,1536]{1,0:T(8,128)(2,1)S(1)} %collective-permute-done.5, bf16[512,768]{1,0:T(8,128)(2,1)} %collective-permute-done.4, bf16[512,768]{1,0:T(8,128)(2,1)} %fusion.42), kind=kOutput, calls=%fused_computation.30 | convolution fusion | flops 1263009792 | bytes 10620928 | tf_op jit(solution)/shard_map/dot_general | solution.py:39
  193.5 7.5 %collective-permute-done.8 = bf16[256,768]{1,0:T(8,128)(2,1)S(1)} collective-permute-done((bf16[256,768]{1,0:T(8,128)(2,1)S(1)}, bf16[256,768]{1,0:T(8,128)(2,1)S(1)}, u32[]{:S(2)}, u32[]{:S(2)}) %collective-permute-start.8) | collective-permute-done | bytes 393248 | tf_op jit(solution)/shard_map/ppermute | solution.py:86
  205.4 3.8 convert_reduce_fusion.1
  213.3 3.8 convert_reduce_fusion
  226.3 4.5 %fusion.41 = bf16[768,3466]{0,1:T(8,128)(2,1)} fusion(bf16[1024,768]{1,0:T(8,128)(2,1)} %copy-done.94, bf16[512,768]{1,0:T(8,128)(2,1)} %collective-permute-done.4, bf16[512,768]{1,0:T(8,128)(2,1)} %fusion.42), kind=kOutput, calls=%fused_computation.110 | convolution fusion | flops 1211695104 | bytes 4325376 | tf_op jit(solution)/shard_map/dot_general | solution.py:35
  240.9 4.0 fusion.39
  250.4 8.0 %copy.133 = bf16[768,3466]{1,0:T(8,128)(2,1)} copy(bf16[768,3466]{0,1:T(8,128)(2,1)} %fusion.94) | data formatting | bytes 10647552
  258.4 6.1 %multiply_reduce_fusion.1 = (f32[3,1024]{1,0:T(4,128)S(1)}, f32[3,1024,1024]{1,2,0:T(8,128)S(1)}) fusion(f32[3,1024,1024]{1,2,0:T(8,128)} %copy-done.2, f32[3,1024]{1,0:T(4,128)S(1)} %log_add_fusion.1, bf16[1024,3,64]{0,2,1:T(8,128)(2,1)S(1)} %bitcast.193, bf16[1024,3,64]{0,2,1:T(8,128)(2,1)S(1)} %bitcast.196), kind=kOutput, calls=%fused_computation.4 | convolution fusion | flops 412087296 | bytes 25976832 | tf_op jit(solution)/shard_map/qhe,khe->hqk/dot_general | solution.py:212
  266.7 5.4 %multiply_convert_fusion.1 = bf16[3,1024,1024]{1,2,0:T(8,128)(2,1)} fusion(f32[3,1024,1024]{1,2,0:T(8,128)S(1)} %get-tuple-element.163, f32[3,1024,1024]{1,2,0:T(8,128)S(1)} %bitcast.163, f32[3,1024]{1,0:T(4,128)S(1)} %get-tuple-element.162, f32[3,1024]{1,0:T(4,128)S(1)} %log_add_fusion.1), kind=kLoop, calls=%fused_computation.3 | loop fusion | flops 12582912 | bytes 31481856 | tf_op jit(solution)/shard_map/convert_element_type | solution.py:216
  272.1 4.2 fusion.46
  284.3 6.1 %multiply_reduce_fusion = (f32[3,1024]{1,0:T(4,128)S(1)}, f32[3,1024,1024]{1,2,0:T(8,128)}) fusion(f32[3,1024,1024]{1,2,0:T(8,128)S(1)} %bitcast.165, f32[3,1024]{1,0:T(4,128)S(1)} %log_add_fusion, bf16[1024,3,64]{0,2,1:T(8,128)(2,1)S(1)} %bitcast.191, bf16[1024,3,64]{0,2,1:T(8,128)(2,1)S(1)} %bitcast.198), kind=kOutput, calls=%fused_computation.1 | convolution fusion | flops 412087296 | bytes 25976832 | tf_op jit(solution)/shard_map/qhe,khe->hqk/dot_general | solution.py:212
  290.4 7.0 %multiply_convert_fusion = bf16[3,1024,1024]{1,2,0:T(8,128)(2,1)S(1)} fusion(f32[3,1024,1024]{1,2,0:T(8,128)} %get-tuple-element.165, f32[3,1024,1024]{1,2,0:T(8,128)S(1)} %bitcast.165, f32[3,1024]{1,0:T(4,128)S(1)} %get-tuple-element.164, f32[3,1024]{1,0:T(4,128)S(1)} %log_add_fusion), kind=kLoop, calls=%fused_computation | loop fusion | flops 12582912 | bytes 31481856 | tf_op jit(solution)/shard_map/convert_element_type | solution.py:216
  310.3 2.6 convolution_convert_fusion.4
  320.4 7.2 %collective-permute-done.14 = bf16[256,768]{1,0:T(8,128)(2,1)} collective-permute-done((bf16[256,768]{1,0:T(8,128)(2,1)}, bf16[256,768]{1,0:T(8,128)(2,1)}, u32[]{:S(2)}, u32[]{:S(2)}) %collective-permute-start.14) | collective-permute-done | bytes 393248 | tf_op jit(solution)/shard_map/ppermute | solution.py:86
  330.3 6.0 %all-to-all-start.2 = ((bf16[256,2,768]{2,1,0:T(2,128)(2,1)}), bf16[256,2,768]{2,1,0:T(2,128)(2,1)S(1)}, u32[]{:S(2)}, u32[]{:S(2)}) async-start(bf16[256,2,768]{2,1,0:T(2,128)(2,1)} %copy.113), calls=%async_computation.2 | async-start | bytes 1572864 | tf_op jit(solution)/shard_map/all_to_all | solution.py:387
  338.6 8.1 %collective-permute-done.16 = bf16[768,578]{0,1:T(8,128)(2,1)} collective-permute-done((bf16[768,578]{0,1:T(8,128)(2,1)}, bf16[768,578]{0,1:T(8,128)(2,1)}, u32[]{:S(2)}, u32[]{:S(2)}) %collective-permute-start.16) | collective-permute-done | bytes 887840 | tf_op jit(solution)/shard_map/ppermute | solution.py:86
  360.8 26.6 %collective-permute-done.17 = bf16[96,578]{1,0:T(8,128)(2,1)S(1)} collective-permute-done((bf16[96,578]{1,0:T(8,128)(2,1)S(1)}, bf16[96,578]{1,0:T(8,128)(2,1)S(1)}, u32[]{:S(2)}, u32[]{:S(2)}) %collective-permute-start.17) | collective-permute-done | bytes 111008 | tf_op jit(solution)/shard_map/ppermute | solution.py:108
  387.4 2.9 collective-permute-done.18
  405.5 5.6 %collective-permute-done.24 = bf16[96,1738]{0,1:T(8,128)(2,1)} collective-permute-done((bf16[96,1738]{0,1:T(8,128)(2,1)S(1)}, bf16[96,1738]{0,1:T(8,128)(2,1)}, u32[]{:S(2)}, u32[]{:S(2)}) %collective-permute-start.24) | collective-permute-done | bytes 333728 | tf_op jit(solution)/shard_map/ppermute | solution.py:86
  (398 shorter events, 149.4 us)
Async XLA Ops:
  10.6 26.4 %all-to-all-start = ((bf16[32,16,768]{2,0,1:T(8,128)(2,1)}), bf16[32,16,768]{2,0,1:T(8,128)(2,1)S(1)}, u32[]{:S(2)}, u32[]{:S(2)}) async-start(bf16[32,16,768]{2,0,1:T(8,128)(2,1)} %copy.99), calls=%async_computation | async-start | bytes 1572864 | tf_op jit(solution)/shard_map/all_to_all | solution.py:130
  17.0 44.8 %all-gather.3.cloned.1.call-start = ((), (), s32[]{:S(2)}) async-start(), calls=%async_computation.4 | async-start | bytes 1327104 | tf_op jit(solution)/shard_map/all_gather | solution.py:92
  17.8 98.0 %all-gather.5.cloned.1.call-start = ((), (), s32[]{:S(2)}) async-start(), calls=%async_computation.5 | async-start | bytes 2654208 | tf_op jit(solution)/shard_map/all_gather | solution.py:92
  37.1 10.8 %collective-permute-start = (bf16[256,768]{1,0:T(8,128)(2,1)S(1)}, bf16[256,768]{1,0:T(8,128)(2,1)S(1)}, u32[]{:S(2)}, u32[]{:S(2)}) collective-permute-start(bf16[256,768]{1,0:T(8,128)(2,1)S(1)} %get-tuple-element.131), channel_id=1, source_target_pairs={{0,2},{1,3},{2,0},{3,1},{4,6},{5,7},{6,4},{7,5},{8,10},{9,11},{10,... | collective-permute-start | bytes 1179656 | tf_op jit(solution)/shard_map/ppermute | solution.py:86
  47.9 15.3 %collective-permute-start.1 = (bf16[512,768]{1,0:T(8,128)(2,1)S(1)}, bf16[512,768]{1,0:T(8,128)(2,1)}, u32[]{:S(2)}, u32[]{:S(2)}) collective-permute-start(bf16[512,768]{1,0:T(8,128)(2,1)S(1)} %pad_maximum_fusion.7), channel_id=1, source_target_pairs={{0,1},{1,0},{2,3},{3,2},{4,5},{5,4},{6,7},{7,6},{8,9},{9,8},{10,11... | collective-permute-start | bytes 2359304 | tf_op jit(solution)/shard_map/ppermute | solution.py:89
  61.8 27.1 %collective-permute-start.2 = (bf16[768,768]{1,0:T(8,128)(2,1)}, bf16[768,768]{1,0:T(8,128)(2,1)S(1)}, u32[]{:S(2)}, u32[]{:S(2)}) collective-permute-start(bf16[768,768]{1,0:T(8,128)(2,1)} %all-gather.3.cloned.1.call-done), channel_id=1, source_target_pairs={{0,2},{1,3},{2,0},{3,1},{4,6},{5,7},{6,4},{7,5},{8,10},{9,11},{10,... | collective-permute-start | bytes 3538952 | tf_op jit(solution)/shard_map/ppermute | solution.py:86
  102.1 2.4 collective-permute-start.3
  106.4 16.8 %collective-permute-start.4 = (bf16[512,768]{1,0:T(8,128)(2,1)}, bf16[512,768]{1,0:T(8,128)(2,1)}, u32[]{:S(2)}, u32[]{:S(2)}) collective-permute-start(bf16[512,768]{1,0:T(8,128)(2,1)} %fusion.42), channel_id=1, source_target_pairs={{0,1},{1,0},{2,3},{3,2},{4,5},{5,4},{6,7},{7,6},{8,9},{9,8},{10,11... | collective-permute-start | bytes 2359304 | tf_op jit(solution)/shard_map/ppermute | solution.py:89
  116.9 72.4 %all-to-all-start.1 = ((bf16[32,16,768]{2,0,1:T(8,128)(2,1)}), bf16[32,16,768]{2,0,1:T(8,128)(2,1)S(1)}, u32[]{:S(2)}, u32[]{:S(2)}) async-start(bf16[32,16,768]{2,0,1:T(8,128)(2,1)} %copy.104), calls=%async_computation.1 | async-start | bytes 1572864 | tf_op jit(solution)/shard_map/all_to_all | solution.py:130
  121.8 276.7 %reduce-scatter.4.cloned.1.call-start = ((), (), s32[]{:S(2)}) async-start(), calls=%async_computation.6 | async-start | bytes 6193152
  121.8 51.7 %collective-permute-start.5 = (bf16[768,1536]{1,0:T(8,128)(2,1)}, bf16[768,1536]{1,0:T(8,128)(2,1)S(1)}, u32[]{:S(2)}, u32[]{:S(2)}) collective-permute-start(bf16[768,1536]{1,0:T(8,128)(2,1)} %all-gather.5.cloned.1.call-done), channel_id=1, source_target_pairs={{0,2},{1,3},{2,0},{3,1},{4,6},{5,7},{6,4},{7,5},{8,10},{9,11},{10,... | collective-permute-start | bytes 7077896 | tf_op jit(solution)/shard_map/ppermute | solution.py:86
  189.3 2.5 collective-permute-start.6
  189.4 11.6 %collective-permute-start.8 = (bf16[256,768]{1,0:T(8,128)(2,1)S(1)}, bf16[256,768]{1,0:T(8,128)(2,1)S(1)}, u32[]{:S(2)}, u32[]{:S(2)}) collective-permute-start(bf16[256,768]{1,0:T(8,128)(2,1)S(1)} %get-tuple-element.129), channel_id=1, source_target_pairs={{0,2},{1,3},{2,0},{3,1},{4,6},{5,7},{6,4},{7,5},{8,10},{9,11},{10,... | collective-permute-start | bytes 1179656 | tf_op jit(solution)/shard_map/ppermute | solution.py:86
  202.6 115.7 %copy-start.21 = (bf16[512,768]{1,0:T(8,128)(2,1)}, bf16[512,768]{1,0:T(8,128)(2,1)S(1)}, u32[]{:S(2)}) copy-start(bf16[512,768]{1,0:T(8,128)(2,1)S(1)} %get-tuple-element.108) | copy-start | bytes 2359300
  202.7 2.4 collective-permute-start.9
  218.7 2.4 collective-permute-start.10
  224.9 9.2 %collective-permute-start.11 = (bf16[512,768]{1,0:T(8,128)(2,1)S(1)}, bf16[512,768]{1,0:T(8,128)(2,1)}, u32[]{:S(2)}, u32[]{:S(2)}) collective-permute-start(bf16[512,768]{1,0:T(8,128)(2,1)S(1)} %convert_element_type.192), channel_id=1, source_target_pairs={{0,1},{1,0},{2,3},{3,2},{4,5},{5,4},{6,7},{7,6},{8,9},{9,8},{10,11... | collective-permute-start | bytes 2359304 | tf_op jit(solution)/shard_map/ppermute | solution.py:89
  233.6 16.1 %collective-permute-start.12 = (f32[768,10]{0,1:T(8,128)S(1)}, f32[768,10]{0,1:T(8,128)S(1)}, u32[]{:S(2)}, u32[]{:S(2)}) collective-permute-start(f32[768,10]{0,1:T(8,128)S(1)} %concatenate.63), channel_id=1, source_target_pairs={{0,1},{1,0},{2,3},{3,2},{4,5},{5,4},{6,7},{7,6},{8,9},{9,8},{10,11... | collective-permute-start | bytes 92168 | tf_op jit(solution)/shard_map/ppermute | solution.py:89
  306.9 6.0 %collective-permute-start.13 = (bf16[512,768]{1,0:T(8,128)(2,1)}, bf16[512,768]{1,0:T(8,128)(2,1)}, u32[]{:S(2)}, u32[]{:S(2)}) collective-permute-start(bf16[512,768]{1,0:T(8,128)(2,1)} %slice.318), channel_id=1, source_target_pairs={{0,1},{1,0},{2,3},{3,2},{4,5},{5,4},{6,7},{7,6},{8,9},{9,8},{10,11... | collective-permute-start | bytes 2359304 | tf_op jit(solution)/shard_map/ppermute | solution.py:89
  309.7 6.9 %collective-permute-start.15 = (f32[768,2]{0,1:T(2,128)S(1)}, f32[768,2]{0,1:T(2,128)S(1)}, u32[]{:S(2)}, u32[]{:S(2)}) collective-permute-start(f32[768,2]{0,1:T(2,128)S(1)} %pad_maximum_fusion.13), channel_id=1, source_target_pairs={{0,1},{1,0},{2,3},{3,2},{4,5},{5,4},{6,7},{7,6},{8,9},{9,8},{10,11... | collective-permute-start | bytes 18440 | tf_op jit(solution)/shard_map/ppermute | solution.py:89
  315.2 12.3 %collective-permute-start.14 = (bf16[256,768]{1,0:T(8,128)(2,1)}, bf16[256,768]{1,0:T(8,128)(2,1)}, u32[]{:S(2)}, u32[]{:S(2)}) collective-permute-start(bf16[256,768]{1,0:T(8,128)(2,1)} %slice.233), channel_id=1, source_target_pairs={{0,2},{1,3},{2,0},{3,1},{4,6},{5,7},{6,4},{7,5},{8,10},{9,11},{10,... | collective-permute-start | bytes 1179656 | tf_op jit(solution)/shard_map/ppermute | solution.py:86
  317.5 29.2 %collective-permute-start.16 = (bf16[768,578]{0,1:T(8,128)(2,1)}, bf16[768,578]{0,1:T(8,128)(2,1)}, u32[]{:S(2)}, u32[]{:S(2)}) collective-permute-start(bf16[768,578]{0,1:T(8,128)(2,1)} %pad_maximum_fusion.6), channel_id=1, source_target_pairs={{0,2},{1,3},{2,0},{3,1},{4,6},{5,7},{6,4},{7,5},{8,10},{9,11},{10,... | collective-permute-start | bytes 2663432 | tf_op jit(solution)/shard_map/ppermute | solution.py:86
  319.0 35.7 %collective-permute-start.7 = (bf16[256,768]{1,0:T(8,128)(2,1)}, bf16[256,768]{1,0:T(8,128)(2,1)}, u32[]{:S(2)}, u32[]{:S(2)}) collective-permute-start(bf16[256,768]{1,0:T(8,128)(2,1)} %slice.227), channel_id=1, source_target_pairs={{0,2},{1,3},{2,0},{3,1},{4,6},{5,7},{6,4},{7,5},{8,10},{9,11},{10,... | collective-permute-start | bytes 1179656 | tf_op jit(solution)/shard_map/ppermute | solution.py:86
  330.3 72.9 %all-to-all-start.2 = ((bf16[256,2,768]{2,1,0:T(2,128)(2,1)}), bf16[256,2,768]{2,1,0:T(2,128)(2,1)S(1)}, u32[]{:S(2)}, u32[]{:S(2)}) async-start(bf16[256,2,768]{2,1,0:T(2,128)(2,1)} %copy.113), calls=%async_computation.2 | async-start | bytes 1572864 | tf_op jit(solution)/shard_map/all_to_all | solution.py:387
  351.6 35.8 %collective-permute-start.17 = (bf16[96,578]{1,0:T(8,128)(2,1)S(1)}, bf16[96,578]{1,0:T(8,128)(2,1)S(1)}, u32[]{:S(2)}, u32[]{:S(2)}) collective-permute-start(bf16[96,578]{1,0:T(8,128)(2,1)S(1)} %get-tuple-element.119), channel_id=1, source_target_pairs={{0,4},{4,8},{8,12},{12,16},{16,20},{20,24},{24,28},{28,0},{1,5},{5... | collective-permute-start | bytes 332936 | tf_op jit(solution)/shard_map/ppermute | solution.py:108
  353.1 37.3 %collective-permute-start.18 = (bf16[96,578]{1,0:T(8,128)(2,1)S(1)}, bf16[96,578]{1,0:T(8,128)(2,1)S(1)}, u32[]{:S(2)}, u32[]{:S(2)}) collective-permute-start(bf16[96,578]{1,0:T(8,128)(2,1)S(1)} %get-tuple-element.125), channel_id=1, source_target_pairs={{0,8},{4,12},{8,16},{12,20},{16,24},{20,28},{24,0},{28,4},{1,9},{5... | collective-permute-start | bytes 332936 | tf_op jit(solution)/shard_map/ppermute | solution.py:108
  355.8 38.3 %collective-permute-start.19 = (bf16[96,578]{1,0:T(8,128)(2,1)}, bf16[96,578]{1,0:T(8,128)(2,1)S(1)}, u32[]{:S(2)}, u32[]{:S(2)}) collective-permute-start(bf16[96,578]{1,0:T(8,128)(2,1)} %get-tuple-element.124), channel_id=1, source_target_pairs={{0,12},{4,16},{8,20},{12,24},{16,28},{20,0},{24,4},{28,8},{1,13},{... | collective-permute-start | bytes 332936 | tf_op jit(solution)/shard_map/ppermute | solution.py:108
  357.8 37.0 %collective-permute-start.20 = (bf16[96,578]{1,0:T(8,128)(2,1)}, bf16[96,578]{1,0:T(8,128)(2,1)S(1)}, u32[]{:S(2)}, u32[]{:S(2)}) collective-permute-start(bf16[96,578]{1,0:T(8,128)(2,1)} %get-tuple-element.123), channel_id=1, source_target_pairs={{0,16},{4,20},{8,24},{12,28},{16,0},{20,4},{24,8},{28,12},{1,17},{... | collective-permute-start | bytes 332936 | tf_op jit(solution)/shard_map/ppermute | solution.py:108
  358.7 36.1 %collective-permute-start.21 = (bf16[96,578]{1,0:T(8,128)(2,1)}, bf16[96,578]{1,0:T(8,128)(2,1)S(1)}, u32[]{:S(2)}, u32[]{:S(2)}) collective-permute-start(bf16[96,578]{1,0:T(8,128)(2,1)} %get-tuple-element.122), channel_id=1, source_target_pairs={{0,20},{4,24},{8,28},{12,0},{16,4},{20,8},{24,12},{28,16},{1,21},{... | collective-permute-start | bytes 332936 | tf_op jit(solution)/shard_map/ppermute | solution.py:108
  387.4 9.1 %collective-permute-start.22 = (bf16[96,578]{1,0:T(8,128)(2,1)}, bf16[96,578]{1,0:T(8,128)(2,1)S(1)}, u32[]{:S(2)}, u32[]{:S(2)}) collective-permute-start(bf16[96,578]{1,0:T(8,128)(2,1)} %get-tuple-element.121), channel_id=1, source_target_pairs={{0,24},{4,28},{8,0},{12,4},{16,8},{20,12},{24,16},{28,20},{1,25},{... | collective-permute-start | bytes 332936 | tf_op jit(solution)/shard_map/ppermute | solution.py:108
  390.3 6.3 %collective-permute-start.23 = (bf16[96,578]{1,0:T(8,128)(2,1)}, bf16[96,578]{1,0:T(8,128)(2,1)S(1)}, u32[]{:S(2)}, u32[]{:S(2)}) collective-permute-start(bf16[96,578]{1,0:T(8,128)(2,1)} %get-tuple-element.120), channel_id=1, source_target_pairs={{0,28},{4,0},{8,4},{12,8},{16,12},{20,16},{24,20},{28,24},{1,29},{... | collective-permute-start | bytes 332936 | tf_op jit(solution)/shard_map/ppermute | solution.py:108
  400.5 10.7 %collective-permute-start.24 = (bf16[96,1738]{0,1:T(8,128)(2,1)S(1)}, bf16[96,1738]{0,1:T(8,128)(2,1)}, u32[]{:S(2)}, u32[]{:S(2)}) collective-permute-start(bf16[96,1738]{0,1:T(8,128)(2,1)S(1)} %slice.238), channel_id=1, source_target_pairs={{0,2},{1,3},{2,0},{3,1},{4,6},{5,7},{6,4},{7,5},{8,10},{9,11},{10,... | collective-permute-start | bytes 1001096 | tf_op jit(solution)/shard_map/ppermute | solution.py:86
  (104 other events, 942.6 us)
Sparse Core Ops, SparseCore 0:
  20.5 41.1 all-gather.2
  64.5 51.1 all-gather.4
  258.5 130.7 reduce-scatter.3
